TPU v7x, 128 devices: a whole 4x4x4 slice. The times are simulated.
128 devices in a mesh: client: 32 (over z, x, core), head: 4 (over y).
Axes of the slice: x: 4, y: 4, z: 4, core: 2. Of those that a mesh axis runs over, the one named last changes fastest.
Arguments:
- pre: bfloat16 [40960, 4096], P('client'), may hold values from -40 to 40
- delta: float32 [40960, 4096], P('client', 'head'), may hold values from -300 to 300
- head_weight: bfloat16 [4096, 4096], P(None, 'head'), may hold values from -0.09375 to 0.09375
- client_ids: int32 [512], P('client'), may hold values from 0 to 511, as said below
Outputs:
- head_grad: float32 [4096, 4096], P('client', 'head')
- bias_grad: float32 [4096], P('head')
- embed_grad: float32 [512, 4096], P('client', 'head')
- span_grad: float32 [80, 4096], P(None, 'head')
Inputs may be any that keep to these rules, and one draw needn't show every extreme that they name: `client_ids`: each of the 512 clients appears exactly once.
All inputs are finite; a program needn't handle non-finite values.
Results may differ from a plain program's by a relative error of at most 0.024.
Values may be sent and summed in bfloat16 or wider, within the bound.
No kernel may reach another device: no remote copies, remote signals or barrier semaphores. Data moves between devices by JAX's collectives and lax.ppermute only.
A program may use at most 128 MiB of HBM per device.

v0:
```python
import jax
import jax.numpy as jnp
from jax import lax
from jax.sharding import Mesh
from jax.sharding import PartitionSpec as P

CLIENT = ("client_0", "client_1", "client_2")


EPSILON = 1e-06


def cut_along(x, dim, peers):
    before, after = (x.shape[:dim], x.shape[dim + 1 :])
    return jnp.moveaxis(x.reshape(*before, peers, -1, *after), dim, 0)


def sum_at_owner(x, axis, dim):
    tiles = cut_along(x, dim, lax.axis_size(axis))
    arrived = lax.all_to_all(tiles, axis, split_axis=0, concat_axis=0, tiled=True)
    return arrived.astype(jnp.float32).sum(axis=0)


def side_by_side(arrays, axis, dim, along):
    ends, at = ([], 0)
    for a in arrays[:-1]:
        at += a.shape[along]
        ends.append(at)
    both = jnp.concatenate(arrays, axis=along)
    return tuple(jnp.split(sum_at_owner(both, axis, dim), ends, axis=along))


def padded_to(lines, peers):
    spare = -len(lines) % peers
    return jnp.pad(lines, [(0, spare)] + [(0, 0)] * (lines.ndim - 1))


def joined_along(tiles, dim):
    shape = list(tiles.shape[1:])
    shape[dim] *= tiles.shape[0]
    return jnp.moveaxis(tiles, 0, dim).reshape(shape)


def sent_to_all(x, axis):
    peers = lax.axis_size(axis)
    return lax.all_to_all(jnp.broadcast_to(x[None], (peers, *x.shape)), axis, 0, 0, tiled=True)


def collect(x, axis, dim):
    return joined_along(sent_to_all(x, axis), dim)


def sum_by_parts(x, axes):
    lines = x.reshape(-1)
    padded = padded_to(lines, lax.axis_size(axes))
    whole = collect(sum_at_owner(padded, axes, 0).astype(jnp.bfloat16), axes, 0)
    return lax.slice_in_dim(whole, 0, len(lines)).reshape(x.shape).astype(jnp.float32)


def of_everyone(x, axis):
    return sent_to_all(x, axis).sum(axis=0)


def by_axis(x, axes):
    far, near = axes
    return of_everyone(of_everyone(x, near), far)


def in_one(arrays, axis):
    ends = [0]
    for a in arrays:
        ends.append(ends[-1] + a.size)
    subtotal = by_axis(jnp.concatenate([a.ravel() for a in arrays]), axis)
    return tuple((subtotal[b:e].reshape(a.shape) for a, b, e in zip(arrays, ends, ends[1:])))


def silu_slope(values):
    sigma = jax.nn.sigmoid(values)
    return sigma * (1.0 + values * (1.0 - sigma))


def clip_factor(total, number):
    return jnp.minimum(1.0, 1.0 / jnp.sqrt(total / number + EPSILON))


def per_device(pre, delta, head_weight, client_ids):
    rows_here, hidden_width = pre.shape
    emit_here = delta.shape[1]
    clients_here = client_ids.shape[0]
    span_count = rows_here // clients_here
    head_devices = lax.axis_size("head")
    client_devices = lax.axis_size(CLIENT)
    hidden = jax.nn.silu(pre.astype(jnp.float32)).astype(jnp.bfloat16)
    delta_low = delta.astype(jnp.bfloat16)
    head_raw = lax.psum_scatter(
        lax.dot_general(
            hidden, delta_low, (((0,), (0,)), ((), ())), preferred_element_type=jnp.float32
        ).astype(jnp.bfloat16),
        CLIENT,
        scatter_dimension=0,
        tiled=True,
    ).astype(jnp.float32)
    head_square = jnp.sum(head_raw * head_raw)
    bias_local = jnp.sum(delta, axis=0)
    partial_sum = lax.dot_general(
        delta_low, head_weight, (((1,), (1,)), ((), ())), preferred_element_type=jnp.float32
    )
    rounded = lax.optimization_barrier(partial_sum.astype(jnp.bfloat16))
    block_grad = rounded.astype(jnp.float32) * silu_slope(pre.astype(jnp.float32))
    grouped = block_grad.reshape(clients_here, span_count, hidden_width)
    client_whole = jnp.sum(grouped, axis=1)
    span_whole = jnp.sum(grouped, axis=0)
    client_part, span_part = side_by_side(
        (client_whole.astype(jnp.bfloat16), span_whole.astype(jnp.bfloat16)), "head", 1, 0
    )
    span_raw, bias_raw = (
        sum_by_parts(span_part.astype(jnp.bfloat16), CLIENT),
        sum_by_parts(bias_local.astype(jnp.bfloat16), CLIENT),
    )
    targets = lax.iota(jnp.int32, clients_here * lax.axis_size(CLIENT))
    selector = (targets[:, None] == client_ids[None, :]).astype(jnp.float32)
    embed_raw = sum_at_owner(
        jnp.dot(
            selector,
            client_part,
            precision=lax.Precision.HIGHEST,
            preferred_element_type=jnp.float32,
        ).astype(jnp.bfloat16),
        CLIENT,
        0,
    )
    leading = (lax.axis_index(CLIENT) == 0).astype(jnp.float32)
    small_square = leading * (jnp.sum(span_raw * span_raw) + jnp.sum(bias_raw * bias_raw))
    embed_square = jnp.sum(embed_raw * embed_raw)
    head_total, embed_total, small_total = in_one(
        (head_square, embed_square, small_square), (("client_0", "client_1"), ("client_2", "head"))
    )
    emit_total = emit_here * head_devices
    clients_total = clients_here * client_devices
    head_factor = clip_factor(head_total, hidden_width * emit_total)
    embed_factor = clip_factor(embed_total, clients_total * hidden_width)
    rest_factor = clip_factor(small_total, span_count * hidden_width + emit_total)
    return (
        head_factor * head_raw,
        rest_factor * bias_raw,
        embed_factor * embed_raw,
        rest_factor * span_raw,
    )


def solution(mesh):
    torus = Mesh(
        mesh.devices.reshape(4, 4, 2, mesh.shape["head"]),
        ("client_0", "client_1", "client_2", "head"),
    )
    return jax.shard_map(
        per_device,
        mesh=torus,
        in_specs=(P(CLIENT, None), P(CLIENT, "head"), P(None, "head"), P(CLIENT)),
        out_specs=(P(CLIENT, "head"), P("head"), P(CLIENT, "head"), P(None, "head")),
        check_vma=False,
    )
```

profile of v0, /device:TPU:0, one launch (start us, length us, event | category | flops | bytes accessed | tf_op | source)
XLA Modules:
  0.0 185.5 jit_solution(11156022891619115548)
XLA Ops:
  7.2 0.0 reduce-scatter.2.cloned.1.call-start
  7.2 18.3 %fusion.9 = bf16[4096,1024]{1,0:T(8,128)(2,1)} fusion(bf16[1280,4096]{1,0:T(8,128)(2,1)} %param.4, f32[1280,1024]{1,0:T(8,128)} %param.5), kind=kOutput, calls=%fused_computation.12 | convolution fusion | flops 10774380544 | bytes 24117248 | tf_op jit(solution)/shard_map/dot_general | solution.py:96
  25.5 0.0 slice-start
  25.5 0.0 reduce-scatter.2.cloned.1.call-update
  25.5 0.0 slice-start.1
  25.5 0.0 slice-start.2
  25.5 17.6 %convolution_convert_fusion = bf16[1280,4096]{1,0:T(8,128)(2,1)} fusion(bf16[4096,1024]{1,0:T(8,128)(2,1)} %param.6, f32[1280,1024]{1,0:T(8,128)} %param.5), kind=kOutput, calls=%fused_computation.10 | convolution fusion | flops 10743971840 | bytes 24117248 | tf_op jit(solution)/shard_map/dot_general | solution.py:105
  43.1 0.0 slice-done
  43.1 0.0 slice-done.1
  43.1 0.0 slice-done.2
  43.1 10.1 %fusion.6 = f32[1280,4096]{1,0:T(8,128)S(1)} fusion(bf16[1280,4096]{1,0:T(8,128)(2,1)S(1)} %bitcast.15, bf16[1280,4096]{1,0:T(8,128)(2,1)} %convolution_convert_fusion), kind=kLoop, calls=%fused_computation.9 | loop fusion | flops 52428800 | bytes 41943040 | tf_op jit(solution)/shard_map/mul | solution.py:109
  53.2 4.3 %fusion.19 = (bf16[16,4096]{1,0:T(8,128)(2,1)S(1)}, bf16[80,4096]{1,0:T(8,128)(2,1)S(1)}) fusion(f32[16,80,4096]{2,1,0:T(8,128)S(1)} %bitcast.13), kind=kLoop, calls=%fused_computation.35 | loop fusion | flops 10092544 | bytes 21757952 | tf_op jit(solution)/shard_map/reduce_sum | solution.py:111
  57.5 0.0 copy-start
  57.5 0.5 convert_element_type.88
  58.0 0.1 convert_element_type.86
  58.1 0.5 maximum_bitcast_fusion
  58.6 1.1 copy.27
  59.7 4.6 %all-to-all-start = ((bf16[4,96,1024]{2,1,0:T(8,128)(2,1)}), bf16[4,96,1024]{2,1,0:T(8,128)(2,1)S(1)}, u32[]{:S(2)}, u32[]{:S(2)}) async-start(bf16[4,96,1024]{2,1,0:T(8,128)(2,1)} %copy.27), calls=%async_computation.1 | async-start | bytes 1572864 | tf_op jit(solution)/shard_map/all_to_all | solution.py:20
  64.3 3.0 %reduce_sum.131 = bf16[1024]{0:T(1024)(128)(2,1)S(1)} reduce(f32[1280,1024]{1,0:T(8,128)} %param.5, f32[]{:T(128)} %constant.38.clone.1), dimensions={0}, to_apply=%region_9.10 | reduce | flops 1309696 | bytes 5244932 | tf_op jit(solution)/shard_map/reduce_sum | solution.py:104
  67.3 0.7 convert_element_type.96
  68.0 8.6 %all-to-all-done = bf16[4,96,1024]{2,1,0:T(8,128)(2,1)S(1)} async-done(((bf16[4,96,1024]{2,1,0:T(8,128)(2,1)}), bf16[4,96,1024]{2,1,0:T(8,128)(2,1)S(1)}, u32[]{:S(2)}, u32[]{:S(2)}) %all-to-all-start) | async-done | bytes 786464 | tf_op jit(solution)/shard_map/all_to_all | solution.py:20
  76.6 8.2 %all-to-all-start.4 = ((bf16[32,1,32]{2,1,0:T(2,128)(2,1)}), bf16[32,1,32]{2,1,0:T(2,128)(2,1)S(1)}, u32[]{:S(2)}, u32[]{:S(2)}) async-start(bf16[32,1,32]{2,1,0:T(2,128)(2,1)} %convert_element_type.96), calls=%async_computation.5 | async-start | bytes 32768 | tf_op jit(solution)/shard_map/all_to_all | solution.py:20
  84.8 0.1 convert_reduce_fusion.1
  84.9 0.1 all_to_all.41
  85.1 0.5 broadcast.22
  85.6 1.6 reduce.12
  87.2 0.7 reshape.119
  87.9 4.4 %all-to-all-done.4 = bf16[32,1,32]{2,1,0:T(2,128)(2,1)S(1)} async-done(((bf16[32,1,32]{2,1,0:T(2,128)(2,1)}), bf16[32,1,32]{2,1,0:T(2,128)(2,1)S(1)}, u32[]{:S(2)}, u32[]{:S(2)}) %all-to-all-start.4) | async-done | bytes 2080 | tf_op jit(solution)/shard_map/all_to_all | solution.py:20
  92.3 3.9 %all-to-all-start.2 = ((bf16[32,2,1280]{2,1,0:T(2,128)(2,1)}), bf16[32,2,1280]{2,1,0:T(2,128)(2,1)S(1)}, u32[]{:S(2)}, u32[]{:S(2)}) async-start(bf16[32,2,1280]{2,1,0:T(2,128)(2,1)} %reshape.119), calls=%async_computation.3 | async-start | bytes 327680 | tf_op jit(solution)/shard_map/all_to_all | solution.py:20
  96.1 0.1 reduce_sum.132
  96.2 8.0 %all-to-all-done.2 = bf16[32,2,1280]{2,1,0:T(2,128)(2,1)S(1)} async-done(((bf16[32,2,1280]{2,1,0:T(2,128)(2,1)}), bf16[32,2,1280]{2,1,0:T(2,128)(2,1)S(1)}, u32[]{:S(2)}, u32[]{:S(2)}) %all-to-all-start.2) | async-done | bytes 163872 | tf_op jit(solution)/shard_map/all_to_all | solution.py:20
  104.2 0.6 broadcast_in_dim.9
  104.8 3.8 %all-to-all-start.5 = ((bf16[32,1,32]{2,1,0:T(2,128)(2,1)}), bf16[32,1,32]{2,1,0:T(2,128)(2,1)S(1)}, u32[]{:S(2)}, u32[]{:S(2)}) async-start(bf16[32,1,32]{2,1,0:T(2,128)(2,1)} %broadcast_in_dim.9), calls=%async_computation.6 | async-start | bytes 32768 | tf_op jit(solution)/shard_map/all_to_all | solution.py:46
  108.6 0.1 reshape.120
  108.7 0.3 reduce_sum.129
  109.0 0.2 broadcast_in_dim.8
  109.2 1.6 reduce.13
  110.8 0.7 reshape.121
  111.5 4.4 %all-to-all-done.5 = bf16[32,1,32]{2,1,0:T(2,128)(2,1)S(1)} async-done(((bf16[32,1,32]{2,1,0:T(2,128)(2,1)}), bf16[32,1,32]{2,1,0:T(2,128)(2,1)S(1)}, u32[]{:S(2)}, u32[]{:S(2)}) %all-to-all-start.5) | async-done | bytes 2080 | tf_op jit(solution)/shard_map/all_to_all | solution.py:46
  115.9 3.9 %all-to-all-start.3 = ((bf16[32,2,1280]{2,1,0:T(2,128)(2,1)}), bf16[32,2,1280]{2,1,0:T(2,128)(2,1)S(1)}, u32[]{:S(2)}, u32[]{:S(2)}) async-start(bf16[32,2,1280]{2,1,0:T(2,128)(2,1)} %reshape.121), calls=%async_computation.4 | async-start | bytes 327680 | tf_op jit(solution)/shard_map/all_to_all | solution.py:46
  119.8 0.0 copy-done
  119.8 2.0 %convolution_convert_fusion.1 = bf16[512,1024]{1,0:T(8,128)(2,1)} fusion(s32[16]{0:T(128)S(1)} %copy-done, f32[96,1024]{1,0:T(8,128)S(1)} %convert_reduce_fusion.1), kind=kOutput, calls=%fused_computation.15 | convolution fusion | flops 101195776 | bytes 1114624 | tf_op jit(solution)/shard_map/dot_general | solution.py:123
  121.7 6.0 %all-to-all-done.3 = bf16[32,2,1280]{2,1,0:T(2,128)(2,1)S(1)} async-done(((bf16[32,2,1280]{2,1,0:T(2,128)(2,1)}), bf16[32,2,1280]{2,1,0:T(2,128)(2,1)S(1)}, u32[]{:S(2)}, u32[]{:S(2)}) %all-to-all-start.3) | async-done | bytes 163872 | tf_op jit(solution)/shard_map/all_to_all | solution.py:46
  127.8 3.9 %all-to-all-start.1 = ((bf16[32,16,1024]{2,1,0:T(8,128)(2,1)}), bf16[32,16,1024]{2,1,0:T(8,128)(2,1)S(1)}, u32[]{:S(2)}, u32[]{:S(2)}) async-start(bf16[32,16,1024]{2,1,0:T(8,128)(2,1)} %bitcast.3), calls=%async_computation.2 | async-start | bytes 2097152 | tf_op jit(solution)/shard_map/all_to_all | solution.py:20
  131.7 0.6 fusion.17
  132.3 0.1 reshape.122
  132.5 1.3 multiply_reduce_fusion.1
  135.1 13.9 %all-to-all-done.1 = bf16[32,16,1024]{2,1,0:T(8,128)(2,1)S(1)} async-done(((bf16[32,16,1024]{2,1,0:T(8,128)(2,1)}), bf16[32,16,1024]{2,1,0:T(8,128)(2,1)S(1)}, u32[]{:S(2)}, u32[]{:S(2)}) %all-to-all-start.1) | async-done | bytes 1048608 | tf_op jit(solution)/shard_map/all_to_all | solution.py:20
  148.9 0.2 convert_reduce_fusion
  149.1 0.6 multiply_reduce_fusion.2
  149.7 0.0 reduce-scatter.2.cloned.1.call-done
  149.7 1.7 fusion.14
  151.4 1.4 pad_maximum_fusion
  152.8 7.6 %all_to_all.50 = f32[8,1,3]{2,1,0:T(1,128)S(1)} all-to-all(f32[8,1,3]{2,1,0:T(1,128)S(1)} %broadcast_in_dim.10), channel_id=1, replica_groups=mesh['client_0'=4,'client_1'=4,'client_2'=2,'head'=4] {'client_2','head'}, dimensions={0} | all-to-all | bytes 192 | tf_op jit(solution)/shard_map/all_to_all | solution.py:46
  160.4 10.7 %all_to_all.51 = f32[16,1,3]{2,1,0:T(1,128)S(1)} all-to-all(f32[16,1,3]{2,1,0:T(1,128)S(1)} %broadcast_in_dim.11), channel_id=1, replica_groups=mesh['client_0'=4,'client_1'=4,'client_2'=2,'head'=4] {'client_0','clien..., dimensions={0} | all-to-all | bytes 384 | tf_op jit(solution)/shard_map/all_to_all | solution.py:46
  171.2 0.6 fusion.20
  172.4 0.9 multiply_reduce_fusion
  173.4 0.8 mul.88
  174.9 0.6 broadcast_multiply_fusion
  175.5 0.7 mul.83
  176.9 1.8 convert_multiply_fusion.2
  (7 shorter events, 0.1 us)
Async XLA Ops:
  7.2 142.6 %reduce-scatter.2.cloned.1.call-start = ((), (), s32[]{:S(2)}) async-start(), calls=%async_computation.9 | async-start | bytes 8650752 | tf_op jit(solution)/shard_map/reduce_scatter | solution.py:95
  25.5 17.6 %slice-start = ((s8[10485760]{0:T(1024)(128)(4,1)}), s8[2097152]{0:T(1024)(128)(4,1)S(1)}, s32[]{:S(2)}) async-start(s8[10485760]{0:T(1024)(128)(4,1)} %bitcast.14), calls=%async_computation.10 | async-start | bytes 4194304
  25.5 17.6 %slice-start.1 = ((s8[10485760]{0:T(1024)(128)(4,1)}), s8[4194304]{0:T(1024)(128)(4,1)S(1)}, s32[]{:S(2)}) async-start(s8[10485760]{0:T(1024)(128)(4,1)} %bitcast.14), calls=%async_computation.11 | async-start | bytes 8388608
  25.5 17.6 %slice-start.2 = ((s8[10485760]{0:T(1024)(128)(4,1)}), s8[4194304]{0:T(1024)(128)(4,1)S(1)}, s32[]{:S(2)}) async-start(s8[10485760]{0:T(1024)(128)(4,1)} %bitcast.14), calls=%async_computation.12 | async-start | bytes 8388608
  57.5 62.3 %copy-start = (s32[16]{0:T(128)S(1)}, s32[16]{0:T(128)}, u32[]{:S(2)}) copy-start(s32[16]{0:T(128)} %param.7) | copy-start | bytes 196
  59.7 16.9 %all-to-all-start = ((bf16[4,96,1024]{2,1,0:T(8,128)(2,1)}), bf16[4,96,1024]{2,1,0:T(8,128)(2,1)S(1)}, u32[]{:S(2)}, u32[]{:S(2)}) async-start(bf16[4,96,1024]{2,1,0:T(8,128)(2,1)} %copy.27), calls=%async_computation.1 | async-start | bytes 1572864 | tf_op jit(solution)/shard_map/all_to_all | solution.py:20
  76.6 15.7 %all-to-all-start.4 = ((bf16[32,1,32]{2,1,0:T(2,128)(2,1)}), bf16[32,1,32]{2,1,0:T(2,128)(2,1)S(1)}, u32[]{:S(2)}, u32[]{:S(2)}) async-start(bf16[32,1,32]{2,1,0:T(2,128)(2,1)} %convert_element_type.96), calls=%async_computation.5 | async-start | bytes 32768 | tf_op jit(solution)/shard_map/all_to_all | solution.py:20
  92.3 11.9 %all-to-all-start.2 = ((bf16[32,2,1280]{2,1,0:T(2,128)(2,1)}), bf16[32,2,1280]{2,1,0:T(2,128)(2,1)S(1)}, u32[]{:S(2)}, u32[]{:S(2)}) async-start(bf16[32,2,1280]{2,1,0:T(2,128)(2,1)} %reshape.119), calls=%async_computation.3 | async-start | bytes 327680 | tf_op jit(solution)/shard_map/all_to_all | solution.py:20
  104.8 11.1 %all-to-all-start.5 = ((bf16[32,1,32]{2,1,0:T(2,128)(2,1)}), bf16[32,1,32]{2,1,0:T(2,128)(2,1)S(1)}, u32[]{:S(2)}, u32[]{:S(2)}) async-start(bf16[32,1,32]{2,1,0:T(2,128)(2,1)} %broadcast_in_dim.9), calls=%async_computation.6 | async-start | bytes 32768 | tf_op jit(solution)/shard_map/all_to_all | solution.py:46
  115.9 11.9 %all-to-all-start.3 = ((bf16[32,2,1280]{2,1,0:T(2,128)(2,1)}), bf16[32,2,1280]{2,1,0:T(2,128)(2,1)S(1)}, u32[]{:S(2)}, u32[]{:S(2)}) async-start(bf16[32,2,1280]{2,1,0:T(2,128)(2,1)} %reshape.121), calls=%async_computation.4 | async-start | bytes 327680 | tf_op jit(solution)/shard_map/all_to_all | solution.py:46
  127.8 21.1 %all-to-all-start.1 = ((bf16[32,16,1024]{2,1,0:T(8,128)(2,1)}), bf16[32,16,1024]{2,1,0:T(8,128)(2,1)S(1)}, u32[]{:S(2)}, u32[]{:S(2)}) async-start(bf16[32,16,1024]{2,1,0:T(8,128)(2,1)} %bitcast.3), calls=%async_computation.2 | async-start | bytes 2097152 | tf_op jit(solution)/shard_map/all_to_all | solution.py:20
Sparse Core Ops, SparseCore 0:
  25.6 96.4 reduce-scatter.1
where the time goes:
time: 186 us
  waiting for transfers between devices  45.3 us (24%)
  matrix products  37.8 us (20%)
  other arithmetic  30.7 us (17%)
  starting transfers between devices  28.3 us (15%)
  blocking collectives  18.3 us (10%)
  between operations  17.6 us (9%)
  local copies, waits for them, and re-layouts  7.57 us (4%)
    all_to_all x4, waiting for transfers between devices, sum_at_owner(): lax.all_to_all(tiles, axis, split_axis=0, concat_axis=0, tiled=True)  34.8 us
    all_to_all x4, starting transfers between devices, sum_at_owner(): lax.all_to_all(tiles, axis, split_axis=0, concat_axis=0, tiled=True)  20.6 us
    all_to_all x2, blocking collectives, sent_to_all(): lax.all_to_all(jnp.broadcast_to(x[None], (peers, *x.shape)), axis, 0, 0,...  18.3 us
    dot_general x1, matrix products, per_device(): lax.dot_general(hidden, delta_low, (((0,), (0,)), ((), ())), preferred_el...  18.3 us
    dot_general x1, matrix products, per_device(): lax.dot_general(delta_low, head_weight, (((1,), (1,)), ((), ())), preferr...  17.6 us
    all_to_all x2, waiting for transfers between devices, sent_to_all(): lax.all_to_all(jnp.broadcast_to(x[None], (peers, *x.shape)), axis, 0, 0,...  10.4 us
    mul x1, other arithmetic, per_device(): rounded.astype(jnp.float32) * silu_slope(pre.astype(jnp.float32))  10.1 us
    all_to_all x2, starting transfers between devices, sent_to_all(): lax.all_to_all(jnp.broadcast_to(x[None], (peers, *x.shape)), axis, 0, 0,...  7.7 us
  transfers between devices with their start and end apart: 7, of which 6 were waited for; matrix products, arithmetic and copies ran while one was open for 26% of the time, Pallas kernels for 0%

commit v1 on v0

v1 whole, which is shorter than its diff:
```python
import jax
import jax.numpy as jnp
from jax import lax
from jax.experimental import pallas as pl
from jax.experimental.pallas import tpu as pltpu
from jax.sharding import Mesh
from jax.sharding import PartitionSpec as P

CLIENT = ("client_0", "client_1", "client_2")
EPSILON = 1e-06
LIMIT = 16 * 2**20
LANES = 128

FIRST = ((2, 0), (2, 1), (1, 0), (1, 1), (2, 2), (2, 3), (3, 2), (3, 3))
ALL = tuple((u, v) for u in range(4) for v in range(4))
KEPT = ((3, 0), (3, 1), (0, 0), (0, 1), (1, 2), (1, 3), (0, 2), (0, 3))


def sigmoid(v):
    return 0.5 * jnp.tanh(0.5 * v) + 0.5


def params(limit=LIMIT):
    return pltpu.CompilerParams(dimension_semantics=("arbitrary",), vmem_limit_bytes=limit)


def whole():
    return pl.BlockSpec(memory_space=pltpu.VMEM)


PARTS = 5


def prepare_body(delta, pre, low, turned, sums, units, buffer, arrived, loaded):
    rows = delta.shape[0] // PARTS
    copies = [
        pltpu.make_async_copy(delta.at[pl.ds(k * rows, rows)], buffer.at[k], arrived.at[k]) for k in range(PARTS)
    ]
    for copy in copies:
        copy.start()
    load = pltpu.make_async_copy(pre, units, loaded)
    load.start()
    total = None
    for k in range(PARTS):
        copies[k].wait()
        value = buffer[k]
        narrow = value.astype(jnp.bfloat16)
        low[k * rows : (k + 1) * rows, :] = narrow
        turned[:, k * rows : (k + 1) * rows] = narrow.T
        part = jnp.sum(value.reshape(rows // 8, 8, value.shape[1]), axis=0)
        total = part if total is None else total + part
    sums[...] = total
    load.wait()


def prepare(delta, pre):
    rows, width = delta.shape
    return pl.pallas_call(
        prepare_body,
        in_specs=[pl.BlockSpec(memory_space=pltpu.HBM)] * 2,
        out_specs=[whole()] * 4,
        out_shape=[
            jax.ShapeDtypeStruct((rows, width), jnp.bfloat16),
            jax.ShapeDtypeStruct((width, rows), jnp.bfloat16),
            jax.ShapeDtypeStruct((8, width), jnp.float32),
            jax.ShapeDtypeStruct(pre.shape, pre.dtype),
        ],
        scratch_shapes=[
            pltpu.VMEM((PARTS, rows // PARTS, width), jnp.float32),
            pltpu.SemaphoreType.DMA((PARTS,)),
            pltpu.SemaphoreType.DMA(()),
        ],
        compiler_params=pltpu.CompilerParams(vmem_limit_bytes=44 * 2**20),
        name="prepare",
    )(delta, pre)


STEP = 4
TILE = 512
CHUNK = 320
SPANS = 80


def product(i, owner, pre, turned):
    units = []
    for j in range(STEP):
        at = pl.multiple_of(owner[STEP * i + j] * LANES, LANES)
        v = pre[:, pl.ds(at, LANES)].astype(jnp.float32)
        units.append((v * sigmoid(v)).astype(jnp.bfloat16))
    return jnp.dot(turned[...], jnp.concatenate(units, axis=1), preferred_element_type=jnp.float32)


def head_call(body, owners, operands, outs, out_shape):
    grid = pltpu.PrefetchScalarGridSpec(
        num_scalar_prefetch=1,
        grid=(len(FIRST) // STEP,),
        in_specs=[whole()] * len(operands),
        out_specs=[whole()] * outs if outs > 1 else whole(),
    )
    return pl.pallas_call(
        body, grid_spec=grid, out_shape=out_shape, compiler_params=params()
    )(owners, *operands)


def plain_body(owner, pre, turned, out):
    i = pl.program_id(0)
    acc = product(i, owner, pre, turned)
    for j in range(STEP):
        out[STEP * i + j] = acc[:, j * LANES : (j + 1) * LANES].astype(out.dtype)


def partner_product(owners, pre, turned):
    shape = jax.ShapeDtypeStruct((len(FIRST), turned.shape[0], LANES), jnp.bfloat16)
    return head_call(plain_body, owners, (pre, turned), 1, shape)


def loading_body(owner, pre, turned, source, out, loaded, arrived):
    i = pl.program_id(0)
    copy = pltpu.make_async_copy(source, loaded, arrived)

    @pl.when(i == 0)
    def _():
        copy.start()

    plain_body(owner, pre, turned, out)

    @pl.when(i == pl.num_programs(0) - 1)
    def _():
        copy.wait()


def loading_product(owners, pre, turned, source):
    grid = pltpu.PrefetchScalarGridSpec(
        num_scalar_prefetch=1,
        grid=(len(FIRST) // STEP,),
        in_specs=[whole(), whole(), pl.BlockSpec(memory_space=pltpu.HBM)],
        out_specs=[whole()] * 2,
        scratch_shapes=[pltpu.SemaphoreType.DMA(())],
    )
    return pl.pallas_call(
        loading_body,
        grid_spec=grid,
        out_shape=[
            jax.ShapeDtypeStruct((len(FIRST), turned.shape[0], LANES), jnp.bfloat16),
            jax.ShapeDtypeStruct(source.shape, source.dtype),
        ],
        compiler_params=params(32 * 2**20),
    )(owners, pre, turned, source)


def first_body(owner, pre, turned, arrived, near, far):
    i = pl.program_id(0)
    acc = product(i, owner, pre, turned)

    def store(out, base):
        for j in range(STEP):
            piece = acc[:, j * LANES : (j + 1) * LANES]
            out[j] = (piece + arrived[base + j].astype(jnp.float32)).astype(out.dtype)

    @pl.when(i == 0)
    def _():
        store(near, 0)

    @pl.when(i == 1)
    def _():
        store(far, STEP)


def first_product(owners, pre, turned, arrived):
    shape = jax.ShapeDtypeStruct((STEP, turned.shape[0], LANES), jnp.bfloat16)
    return head_call(first_body, owners, (pre, turned, arrived), 2, [shape, shape])


def kept_body(owner, pre, turned, arrived, near, far, send_a, send_b, keep):
    i = pl.program_id(0)
    acc = product(i, owner, pre, turned)

    def store(side, base, send, at):
        for j in range(STEP):
            piece = acc[:, j * LANES : (j + 1) * LANES]
            total = piece + arrived[base + j].astype(jnp.float32) + side[j].astype(jnp.float32)
            if j < STEP // 2:
                send[j] = total.astype(send.dtype)
            else:
                keep[at + j - STEP // 2] = total.astype(keep.dtype)

    @pl.when(i == 0)
    def _():
        store(near, 0, send_a, 0)

    @pl.when(i == 1)
    def _():
        store(far, STEP, send_b, STEP // 2)


def kept_product(owners, pre, turned, arrived, near, far):
    width = turned.shape[0]
    half = jax.ShapeDtypeStruct((STEP // 2, width, LANES), jnp.bfloat16)
    full = jax.ShapeDtypeStruct((STEP, width, LANES), jnp.float32)
    return head_call(kept_body, owners, (pre, turned, arrived, near, far), 3, [half, half, full])


def slope_body(tile, pre, low, weight, out):
    i = pl.program_id(0)
    rows, width = low.shape
    per = width // TILE
    clients = rows // SPANS
    at = pl.multiple_of(tile[i] * TILE, TILE)
    turned = weight[pl.ds(at, TILE), :].T
    put = pl.ds(pl.multiple_of((i % per) * TILE, TILE), TILE)
    spans = None
    for row in range(0, rows, CHUNK):
        part = jnp.dot(low[row : row + CHUNK, :], turned, preferred_element_type=jnp.float32)
        half = 0.5 * pre[row : row + CHUNK, pl.ds(at, TILE)].astype(jnp.float32)
        t = jnp.tanh(half)
        grad = part * ((1.0 + t) * (1.0 + half * (1.0 - t)))
        grad = grad.reshape(CHUNK // SPANS, SPANS, TILE)
        first = row // SPANS
        out[i // per, first : first + CHUNK // SPANS, put] = (0.5 * jnp.sum(grad, axis=1)).astype(out.dtype)
        some = jnp.sum(grad, axis=0)
        spans = some if spans is None else spans + some
    out[i // per, clients:, put] = (0.5 * spans).astype(out.dtype)


def slope_sums(tiles, pre, low, weight, dtype):
    rows, width = low.shape
    lines = rows // SPANS + SPANS
    grid = pltpu.PrefetchScalarGridSpec(
        num_scalar_prefetch=1,
        grid=(2 * width // TILE,),
        in_specs=[whole()] * 3,
        out_specs=whole(),
    )
    return pl.pallas_call(
        slope_body,
        grid_spec=grid,
        out_shape=jax.ShapeDtypeStruct((2, lines, width), dtype),
        compiler_params=params(),
    )(tiles, pre, low, weight)


def small_body(owner, kept, got, got_two, selector, bias, send, keep, square, lines):
    f32 = jnp.float32
    sums = kept[1] + got[1].astype(f32) + got_two[...].astype(f32)
    width = sums.shape[1]
    across = width // LANES
    clients = selector.shape[1]
    mine = sums[:clients]
    square[...] = jnp.full(square.shape, jnp.sum(mine * mine))
    placed = jnp.dot(selector[...], mine.astype(jnp.bfloat16), preferred_element_type=f32)
    spans = sums[clients:]
    lines[...] = jnp.zeros(lines.shape, f32)
    for r in range(SPANS // 8):
        for c in range(across):
            lines[r * across + c] = spans[8 * r : 8 * r + 8, c * LANES : (c + 1) * LANES]
    bias_row = jnp.sum(bias[...], axis=0, keepdims=True)
    for c in range(across):
        lines[SPANS // 8 * across, c : c + 1, :] = bias_row[:, c * LANES : (c + 1) * LANES]
    groups = clients // 8
    share = send.shape[1] - groups * across
    for k in range(2 * send.shape[0]):
        out = send if k < send.shape[0] else keep
        at = k % send.shape[0]
        for g in range(groups):
            for c in range(across):
                top = k * clients + 8 * g
                block = placed[top : top + 8, c * LANES : (c + 1) * LANES]
                out[at, g * across + c] = block.astype(out.dtype)
        out[at, groups * across :] = lines[pl.ds(share * owner[k], share)].astype(out.dtype)


def small_sends(owners, kept, got, got_two, selector, bias, share):
    width = kept.shape[2]
    across = width // LANES
    count = owners.shape[0] // 2
    tiles = selector.shape[1] // 8 * across + share
    shape = (count, tiles, 8, LANES)
    grid = pltpu.PrefetchScalarGridSpec(
        num_scalar_prefetch=1,
        grid=(1,),
        in_specs=[whole()] * 5,
        out_specs=[whole()] * 3,
        scratch_shapes=[pltpu.VMEM((share * owners.shape[0], 8, LANES), jnp.float32)],
    )
    return pl.pallas_call(
        small_body,
        grid_spec=grid,
        out_shape=[
            jax.ShapeDtypeStruct(shape, jnp.bfloat16),
            jax.ShapeDtypeStruct(shape, jnp.float32),
            jax.ShapeDtypeStruct((8, LANES), jnp.float32),
        ],
        compiler_params=params(),
        name="small_sends",
    )(owners, kept, got, got_two, selector, bias)


def simple_call(body, operands, shapes):
    return pl.pallas_call(
        body,
        in_specs=[whole()] * len(operands),
        out_specs=[whole()] * len(shapes),
        out_shape=shapes,
        compiler_params=pltpu.CompilerParams(vmem_limit_bytes=LIMIT),
    )(*operands)


def core_sum_body(keep, arrived, own, one, two, three):
    total = keep[...] + arrived[...].astype(jnp.float32)
    own[...] = total[0:4]
    for k, out in ((1, one), (2, two), (3, three)):
        out[...] = total[4 * k : 4 * k + 4].astype(out.dtype)


def core_sum(keep, arrived):
    shape = (keep.shape[0] // 4, *keep.shape[1:])
    low = jax.ShapeDtypeStruct(shape, jnp.bfloat16)
    return simple_call(
        core_sum_body, (keep, arrived), [jax.ShapeDtypeStruct(shape, jnp.float32), low, low, low]
    )


def join_body(keep, got_a, got_b, own, in_one, in_two, in_three, head, small, one, two, three):
    f32 = jnp.float32
    lines = own.shape[1]
    for k in range(4):
        side = got_a if k < 2 else got_b
        total = keep[k] + side[k % 2].astype(f32)
        tiles = own[k] + in_one[k].astype(f32) + in_two[k].astype(f32) + in_three[k].astype(f32)
        if k == 0:
            head[...] = total
            small[...] = tiles
        else:
            out = (one, two, three)[k - 1]
            width = total.shape[0]
            out[:width] = total.astype(out.dtype)
            for t in range(lines):
                out[width + 8 * t : width + 8 * t + 8, :] = tiles[t].astype(out.dtype)


def join(keep, got_a, got_b, own, arrived):
    width = keep.shape[1]
    lines = own.shape[1]
    low = jax.ShapeDtypeStruct((width + 8 * lines, LANES), jnp.bfloat16)
    return simple_call(
        join_body,
        (keep, got_a, got_b, own, *arrived),
        [
            jax.ShapeDtypeStruct((width, LANES), jnp.float32),
            jax.ShapeDtypeStruct((lines, 8, LANES), jnp.float32),
            low,
            low,
            low,
        ],
    )


def close_body(head, small, square, one, two, three, out, embed, message):
    f32 = jnp.float32
    width = head.shape[0]
    lines = small.shape[0]
    across = width // LANES
    total = head[...]
    for side in (one, two, three):
        total = total + side[:width].astype(f32)
    out[...] = total.T
    share = message.shape[1] - 1
    rows = lines - share
    part = jnp.zeros((8, LANES), f32)
    for t in range(lines):
        at = slice(width + 8 * t, width + 8 * t + 8)
        tile = small[t] + one[at].astype(f32) + two[at].astype(f32) + three[at].astype(f32)
        if t < rows:
            r, c = divmod(t, across)
            embed[8 * r : 8 * r + 8, c * LANES : (c + 1) * LANES] = tile
        else:
            low = tile.astype(message.dtype)
            wide_again = low.astype(f32)
            part = part + wide_again * wide_again
            for p in range(message.shape[0]):
                message[p, t - rows] = low
    head_square = jnp.sum(total * total)
    small_square = jnp.sum(part)
    column = lax.broadcasted_iota(jnp.int32, (8, LANES), 1)
    values = jnp.where(column == 0, head_square, jnp.where(column == 1, square[...], small_square))
    coarse = values.astype(message.dtype)
    fine = (values - coarse.astype(f32)).astype(message.dtype)
    line = lax.broadcasted_iota(jnp.int32, (8, LANES), 0)
    mixed = jnp.where(line == 0, coarse.astype(f32), fine.astype(f32)).astype(message.dtype)
    for p in range(message.shape[0]):
        message[p, share] = mixed


def close(head, small, square, arrived, peers, share):
    width = head.shape[0]
    rows = 8 * (small.shape[0] - share) * LANES // width
    return simple_call(
        close_body,
        (head, small, square, *arrived),
        [
            jax.ShapeDtypeStruct((LANES, width), jnp.float32),
            jax.ShapeDtypeStruct((rows, width), jnp.float32),
            jax.ShapeDtypeStruct((peers, share + 1, 8, LANES), jnp.bfloat16),
        ],
    )


def flipped(first, second):
    pairs = []
    for z in range(4):
        for x in range(4):
            pairs.append(((z * 4 + x) * 2, ((z ^ first[0]) * 4 + (x ^ first[1])) * 2))
            pairs.append(((z * 4 + x) * 2 + 1, ((z ^ second[0]) * 4 + (x ^ second[1])) * 2 + 1))
    return pairs


def along_u(x, k):
    return lax.ppermute(x, CLIENT, flipped((0, k), (k, 0)))


def along_v(x, k):
    return lax.ppermute(x, CLIENT, flipped((k, 0), (0, k)))


def to_core(x):
    return lax.ppermute(x, "client_2", [(0, 1), (1, 0)])


def along_head(x, low, high):
    axes = ("client_2", "head")
    pairs = [(h, h ^ low) for h in range(4)] + [(4 + h, 4 + (h ^ high)) for h in range(4)]
    return lax.ppermute(x, axes, pairs)


def wide(x):
    return x.astype(jnp.float32)


def narrow(x):
    return x.astype(jnp.bfloat16)


def clip_factor(total, number):
    return jnp.minimum(1.0, 1.0 / jnp.sqrt(total / number + EPSILON))


def exchange(x, axes):
    return lax.all_to_all(x, axes, 0, 0, tiled=True)


def per_device(pre, delta, head_weight, client_ids):
    _, hidden_width = pre.shape
    emit_here = delta.shape[1]
    clients_here = client_ids.shape[0]
    head_devices = lax.axis_size("head")
    peers = lax.axis_size(CLIENT)
    z, x, core, head = (lax.axis_index(a) for a in (*CLIENT, "head"))

    def owners(side, places):
        u = jnp.array([p[0] for p in places], jnp.int32)
        v = jnp.array([p[1] for p in places], jnp.int32)
        at_z = jnp.where(side == 0, z ^ v, z ^ u)
        at_x = jnp.where(side == 0, x ^ u, x ^ v)
        return ((at_z * 4 + at_x) * 2 + side).astype(jnp.int32)

    def tiles(places):
        per = emit_here // TILE
        return (jnp.stack(places)[:, None] * per + jnp.arange(per)[None, :]).reshape(-1).astype(jnp.int32)

    other = 1 - core
    listed = jnp.concatenate([owners(other, ALL), owners(core, ALL)])
    rows = (listed[:, None] * clients_here + jnp.arange(clients_here)[None, :]).reshape(-1)
    selector = narrow(rows[:, None] == client_ids[None, :])
    share = -(-(SPANS // 8 * (emit_here // LANES) + 1) // peers)

    step_one = jnp.where(core == 0, 1, 3)
    step_two = jnp.where(core == 0, 3, 1)
    places = (
        owners(other, FIRST),
        owners(other, KEPT),
        owners(core, FIRST),
        owners(core, KEPT),
        tiles((head ^ 2, head ^ step_one)),
        tiles((head ^ step_two, head)),
        listed,
        selector,
    )
    delta, *places = lax.optimization_barrier((delta, *places))
    partner_first, partner_kept, own_first, own_kept, tiles_sent, tiles_kept, listed, selector = places

    low, turned, bias_part, pre = prepare(delta, pre)
    part, head_weight = loading_product(partner_first, pre, turned, head_weight)
    arrived_first = to_core(part)
    part = partner_product(partner_kept, pre, turned)
    arrived_kept = to_core(part)
    near, far = first_product(own_first, pre, turned, arrived_first)
    near = along_u(near, 1)
    far = along_u(far, 3)
    sent = slope_sums(tiles_sent, pre, low, head_weight, jnp.bfloat16)
    got = along_head(sent, 1, 3)
    kept = slope_sums(tiles_kept, pre, low, head_weight, jnp.float32)
    message = narrow(kept[0] + wide(got[0]))
    got_two = along_head(message, 3, 1)
    send_a, send_b, keep = kept_product(own_kept, pre, turned, arrived_kept, near, far)
    got_a = along_u(send_a, 3)
    got_b = along_u(send_b, 1)
    small_send, small_keep, embed_square = small_sends(
        listed, kept, got, got_two, selector, bias_part, share
    )
    small_got = to_core(small_send)
    own, one, two, three = core_sum(small_keep, small_got)
    arrived = along_u(two, 2), along_u(one, 1), along_u(three, 3)
    final, small, one, two, three = join(keep, got_a, got_b, own, arrived)
    arrived = along_v(two, 2), along_v(one, 1), along_v(three, 3)
    head_raw, embed_raw, message = close(final, small, embed_square, arrived, peers, share)

    everyone = exchange(message, CLIENT)
    count = SPANS * emit_here // (8 * LANES)
    lines = everyone[:, :share].reshape(-1, 8, LANES)
    spans = lines[:count].reshape(SPANS // 8, emit_here // LANES, 8, LANES)
    span_raw = wide(spans.transpose(0, 2, 1, 3).reshape(SPANS, emit_here))
    bias_raw = wide(lines[count].reshape(emit_here))
    squares = wide(everyone[:, share, :2, :3]).sum(axis=(0, 1))
    squares = exchange(jnp.broadcast_to(squares[None], (head_devices, 3)), "head").sum(axis=0)

    emit_total = emit_here * head_devices
    clients_total = clients_here * peers
    head_factor = clip_factor(squares[0], hidden_width * emit_total)
    embed_factor = clip_factor(squares[1], clients_total * hidden_width)
    rest_factor = clip_factor(squares[2], SPANS * hidden_width + emit_total)
    return (
        head_factor * head_raw,
        rest_factor * bias_raw,
        embed_factor * embed_raw,
        rest_factor * span_raw,
    )


def solution(mesh):
    torus = Mesh(
        mesh.devices.reshape(4, 4, 2, mesh.shape["head"]),
        ("client_0", "client_1", "client_2", "head"),
    )
    return jax.shard_map(
        per_device,
        mesh=torus,
        in_specs=(P(CLIENT, None), P(CLIENT, "head"), P(None, "head"), P(CLIENT)),
        out_specs=(P(CLIENT, "head"), P("head"), P(CLIENT, "head"), P(None, "head")),
        check_vma=False,
    )
```

time: 186 us -> 133 us (0.72)
  Pallas kernels: 0 us -> 50.6 us
  matrix products: 37.8 us -> 0 us
  other arithmetic: 30.7 us -> 5.58 us
  waiting for transfers between devices: 45.3 us -> 26.7 us
  between operations: 17.6 us -> 2.94 us
  starting transfers between devices: 28.3 us -> 23.3 us
  blocking collectives: 18.3 us -> 13.5 us
  local copies, waits for them, and re-layouts: 7.57 us -> 9.94 us
    pallas_call x0 -> x11, Pallas kernels: none -> 50.6 us  [the longest x2 18 us: slope_sums(): pl.pallas_call(slope_body, grid_spec=grid, out_shape=jax.ShapeDtypeStruct...]
    all_to_all x6 -> x1, waiting for transfers between devices: 45.2 us -> 5.19 us  [exchange(): return lax.all_to_all(x, axes, 0, 0, tiled=True)]
    dot_general x3 -> x0, matrix products: 37.8 us -> none  [the longest x1 18.3 us: per_device(): lax.dot_general(hidden, delta_low, (((0,), (0,)), ((), ())), preferred_el...]
    all_to_all x6 -> x1, starting transfers between devices: 28.2 us -> 3.44 us  [exchange(): return lax.all_to_all(x, axes, 0, 0, tiled=True)]
    ppermute x0 -> x15, waiting for transfers between devices: none -> 21.6 us  [the longest x7 8.8 us: along_u(): return lax.ppermute(x, CLIENT, flipped((0, k), (k, 0)))]
    ppermute x0 -> x15, starting transfers between devices: none -> 19.9 us  [the longest x7 10 us: along_u(): return lax.ppermute(x, CLIENT, flipped((0, k), (k, 0)))]
    reduce_sum x12 -> x2, other arithmetic: 12.2 us -> 0.07 us  [the longest x1 0.05 us: per_device(): squares = wide(everyone[:, share, :2, :3]).sum(axis=(0, 1))]
    mul x1 -> x3, other arithmetic: 10.1 us -> 0.23 us  [the longest x2 0.15 us: tiles(): jnp.stack(places)[:, None] * per + jnp.arange(per)[None, :]]
  transfers between devices with their start and end apart: 7 -> 16, of which waited for: 6 -> 6; matrix products, arithmetic and copies ran while one was open for 26% -> 0% of each run, Pallas kernels for 0% -> 24%
where the time goes in v1:
time: 133 us
  Pallas kernels  50.6 us (38%)
  waiting for transfers between devices  26.7 us (20%)
  starting transfers between devices  23.3 us (18%)
  blocking collectives  13.5 us (10%)
  local copies, waits for them, and re-layouts  9.94 us (7%)
  other arithmetic  5.58 us (4%)
  between operations  2.94 us (2%)
    pallas_call x2, Pallas kernels, slope_sums(): pl.pallas_call(slope_body, grid_spec=grid, out_shape=jax.ShapeDtypeStruct...  18 us
    all_to_all x1, blocking collectives, exchange(): return lax.all_to_all(x, axes, 0, 0, tiled=True)  13.5 us
    pallas_call x3, Pallas kernels, head_call(): pl.pallas_call(body, grid_spec=grid, out_shape=out_shape, compiler_params...  12.7 us
    ppermute x7, starting transfers between devices, along_u(): return lax.ppermute(x, CLIENT, flipped((0, k), (k, 0)))  10 us
    pallas_call x1, Pallas kernels, prepare(): pl.pallas_call(prepare_body, in_specs=[pl.BlockSpec(memory_space=pltpu.HB...  9.64 us
    ppermute x7, waiting for transfers between devices, along_u(): return lax.ppermute(x, CLIENT, flipped((0, k), (k, 0)))  8.8 us
    pallas_call x1, Pallas kernels, loading_product(): pl.pallas_call(loading_body, grid_spec=grid, out_shape=[jax.ShapeDtypeStr...  8.66 us
    unnamed x18, local copies, waits for them, and re-layouts  8.5 us
  transfers between devices with their start and end apart: 16, of which 6 were waited for; matrix products, arithmetic and copies ran while one was open for 0% of the time, Pallas kernels for 24%

profile of v1, /device:TPU:0, one launch (start us, length us, event | category | flops | bytes accessed | tf_op | source)
XLA Modules:
  0.0 132.7 jit_solution(15866908400896887233)
XLA Ops:
  0.7 0.7 fusion.22
  1.3 0.1 broadcast_multiply_fusion.2
  1.4 0.1 iota_add_fusion
  1.5 0.1 add.147
  1.6 0.1 add_multiply_fusion
  1.7 0.1 iota_add_fusion.2
  1.7 0.1 add.133.tile
  1.8 0.1 add_multiply_fusion.1
  1.9 0.1 iota_add_fusion.1
  2.0 0.1 add.137.tile
  2.0 0.8 compare_convert_fusion.selector
  2.8 0.7 fusion.19
  3.5 9.6 %prepare.1 = (bf16[1280,1024]{1,0:T(8,128)(2,1)S(1)}, bf16[1024,1280]{1,0:T(8,128)(2,1)S(1)}, f32[8,1024]{1,0:T(8,128)S(1)}, bf16[1280,4096]{1,0:T(8,128)(2,1)}) custom-call(f32[1280,1024]{1,0:T(8,128)} %delta, bf16[1280,4096]{1,0:T(8,128)(2,1)} %pre.1), custom_call_target="tpu_custom_call" | custom-call | tf_op jit(solution)/shard_map/prepare/pallas_call | solution.py:58
  13.2 1.6 %copy-done = bf16[1024,1280]{1,0:T(8,128)(2,1)} copy-done((bf16[1024,1280]{1,0:T(8,128)(2,1)}, bf16[1024,1280]{1,0:T(8,128)(2,1)S(1)}, u32[]{:S(2)}) %copy-start) | copy-done | bytes 2621464
  14.8 1.5 %copy-done.3 = bf16[1280,1024]{1,0:T(8,128)(2,1)} copy-done((bf16[1280,1024]{1,0:T(8,128)(2,1)}, bf16[1280,1024]{1,0:T(8,128)(2,1)S(1)}, u32[]{:S(2)}) %copy-start.3) | copy-done | bytes 2621464
  16.3 1.9 %copy-done.1 = bf16[1024,1280]{1,0:T(8,128)(2,1)S(1)} copy-done((bf16[1024,1280]{1,0:T(8,128)(2,1)S(1)}, bf16[1024,1280]{1,0:T(8,128)(2,1)}, u32[]{:S(2)}) %copy-start.1) | copy-done | bytes 2621464
  18.1 3.5 %copy-done.5 = bf16[4096,1024]{1,0:T(8,128)(2,1)S(1)} copy-done((bf16[4096,1024]{1,0:T(8,128)(2,1)S(1)}, bf16[4096,1024]{1,0:T(8,128)(2,1)}, u32[]{:S(2)}) %copy-start.5) | copy-done | bytes 8388632
  21.7 8.7 %shard_map.184 = (bf16[8,1024,128]{2,1,0:T(8,128)(2,1)S(1)}, bf16[4096,1024]{1,0:T(8,128)(2,1)S(1)}) custom-call(s32[8]{0:T(128)S(1)} %get-tuple-element.45.owner, bf16[1280,4096]{1,0:T(8,128)(2,1)} %get-tuple-element.41.pre, bf16[1024,1280]{1,0:T(8,128)(2,1)S(1)} %copy-done.1, bf16[4096,1024]{1,0:T(8,128)(2,1)S(1)} %copy-done.5), custom_call_target="tpu_custom_call" | custom-call | tf_op jit(solution)/shard_map/pallas_call | solution.py:140
  30.4 0.1 collective-permute-start.1
  30.5 3.8 %shard_map.183 = bf16[8,1024,128]{2,1,0:T(8,128)(2,1)S(1)} custom-call(s32[8]{0:T(128)S(1)} %get-tuple-element.43.owner, bf16[1280,4096]{1,0:T(8,128)(2,1)S(1)} %bitcast.18, bf16[1024,1280]{1,0:T(8,128)(2,1)S(1)} %copy-done.1), custom_call_target="tpu_custom_call" | custom-call | tf_op jit(solution)/shard_map/pallas_call | solution.py:100
  34.4 0.5 collective-permute-start
  34.9 9.0 %shard_map.188 = bf16[2,96,1024]{2,1,0:T(8,128)(2,1)S(1)} custom-call(s32[4]{0:T(128)S(1)} %add.133.tile, bf16[1280,4096]{1,0:T(8,128)(2,1)S(1)} %bitcast.18, bf16[1280,1024]{1,0:T(8,128)(2,1)S(1)} %copy-done.4, bf16[4096,1024]{1,0:T(8,128)(2,1)S(1)} %get-tuple-element.55.weight), custom_call_target="tpu_custom_call" | custom-call | tf_op jit(solution)/shard_map/pallas_call | solution.py:234
  43.9 1.8 %collective-permute-start.6 = (bf16[2,96,1024]{2,1,0:T(8,128)(2,1)S(1)}, bf16[2,96,1024]{2,1,0:T(8,128)(2,1)S(1)}, u32[]{:S(2)}, u32[]{:S(2)}) collective-permute-start(bf16[2,96,1024]{2,1,0:T(8,128)(2,1)S(1)} %shard_map.188), channel_id=1, source_target_pairs={{0,1},{1,0},{2,3},{3,2},{4,7},{5,6},{6,5},{7,4},{8,9},{9,8},{10,11... | collective-permute-start | bytes 1179656 | tf_op jit(solution)/shard_map/ppermute | solution.py:432
  45.7 0.0 collective-permute-done.1.arrived
  45.7 4.3 %shard_map.185 = (bf16[4,1024,128]{2,1,0:T(8,128)(2,1)S(1)}, bf16[4,1024,128]{2,1,0:T(8,128)(2,1)S(1)}) custom-call(s32[8]{0:T(128)S(1)} %get-tuple-element.44.owner, bf16[1280,4096]{1,0:T(8,128)(2,1)S(1)} %bitcast.18, bf16[1024,1280]{1,0:T(8,128)(2,1)S(1)} %copy-done.2, bf16[8,1024,128]{2,1,0:T(8,128)(2,1)S(1)} %collective-permute-done.1.arrived), custom_call_target="tpu_custom_call" | custom-call | tf_op jit(solution)/shard_map/pallas_call | solution.py:100
  50.0 1.6 %collective-permute-start.2 = (bf16[4,1024,128]{2,1,0:T(8,128)(2,1)S(1)}, bf16[4,1024,128]{2,1,0:T(8,128)(2,1)S(1)}, u32[]{:S(2)}, u32[]{:S(2)}) collective-permute-start(bf16[4,1024,128]{2,1,0:T(8,128)(2,1)S(1)} %get-tuple-element.47), channel_id=1, source_target_pairs={{0,8},{4,36},{8,0},{12,44},{16,24},{20,52},{24,16},{28,60},{32,40}... | collective-permute-start | bytes 3145736 | tf_op jit(solution)/shard_map/ppermute | solution.py:418
  51.6 2.1 %collective-permute-start.3 = (bf16[4,1024,128]{2,1,0:T(8,128)(2,1)S(1)}, bf16[4,1024,128]{2,1,0:T(8,128)(2,1)S(1)}, u32[]{:S(2)}, u32[]{:S(2)}) collective-permute-start(bf16[4,1024,128]{2,1,0:T(8,128)(2,1)S(1)} %get-tuple-element.48), channel_id=1, source_target_pairs={{0,24},{4,100},{8,16},{12,108},{16,8},{20,116},{24,0},{28,124},{32... | collective-permute-start | bytes 3145736 | tf_op jit(solution)/shard_map/ppermute | solution.py:418
  53.7 8.9 %shard_map.187.kept = f32[2,96,1024]{2,1,0:T(8,128)S(1)} custom-call(s32[4]{0:T(128)S(1)} %add.137.tile, bf16[1280,4096]{1,0:T(8,128)(2,1)S(1)} %bitcast.18, bf16[1280,1024]{1,0:T(8,128)(2,1)S(1)} %copy-done.4, bf16[4096,1024]{1,0:T(8,128)(2,1)S(1)} %get-tuple-element.55.weight), custom_call_target="tpu_custom_call" | custom-call | tf_op jit(solution)/shard_map/pallas_call | solution.py:234
  62.6 0.0 collective-permute-done.6.got
  62.7 2.4 %collective-permute-start.7 = (bf16[96,1024]{1,0:T(8,128)(2,1)S(1)}, bf16[96,1024]{1,0:T(8,128)(2,1)S(1)}, u32[]{:S(2)}, u32[]{:S(2)}) collective-permute-start(bf16[96,1024]{1,0:T(8,128)(2,1)S(1)} %fusion.1), channel_id=1, source_target_pairs={{0,3},{1,2},{2,1},{3,0},{4,5},{5,4},{6,7},{7,6},{8,11},{9,10},{10,... | collective-permute-start | bytes 589832 | tf_op jit(solution)/shard_map/ppermute | solution.py:432
  65.1 4.7 %collective-permute-done.7.got_two = bf16[96,1024]{1,0:T(8,128)(2,1)S(1)} collective-permute-done((bf16[96,1024]{1,0:T(8,128)(2,1)S(1)}, bf16[96,1024]{1,0:T(8,128)(2,1)S(1)}, u32[]{:S(2)}, u32[]{:S(2)}) %collective-permute-start.7) | collective-permute-done | bytes 196640 | tf_op jit(solution)/shard_map/ppermute | solution.py:432
  69.8 1.0 small_sends.1
  70.8 0.1 collective-permute-start.8
  70.9 0.0 collective-permute-done.arrived
  70.9 0.0 collective-permute-done.3.far
  70.9 4.5 %shard_map.186 = (bf16[2,1024,128]{2,1,0:T(8,128)(2,1)S(1)}, bf16[2,1024,128]{2,1,0:T(8,128)(2,1)S(1)}, f32[4,1024,128]{2,1,0:T(8,128)S(1)}) custom-call(s32[8]{0:T(128)S(1)} %get-tuple-element.39.owner, bf16[1280,4096]{1,0:T(8,128)(2,1)S(1)} %bitcast.18, bf16[1024,1280]{1,0:T(8,128)(2,1)S(1)} %copy-done.2, ...), custom_call_target="tpu_custom_call" | custom-call | tf_op jit(solution)/shard_map/pallas_call | solution.py:100
  75.5 2.0 %collective-permute-start.4 = (bf16[2,1024,128]{2,1,0:T(8,128)(2,1)S(1)}, bf16[2,1024,128]{2,1,0:T(8,128)(2,1)S(1)}, u32[]{:S(2)}, u32[]{:S(2)}) collective-permute-start(bf16[2,1024,128]{2,1,0:T(8,128)(2,1)S(1)} %get-tuple-element.50), channel_id=1, source_target_pairs={{0,24},{4,100},{8,16},{12,108},{16,8},{20,116},{24,0},{28,124},{32... | collective-permute-start | bytes 1572872 | tf_op jit(solution)/shard_map/ppermute | solution.py:418
  77.4 0.2 collective-permute-start.5
  77.7 0.0 collective-permute-done.8.arrived
  77.7 0.1 shard_map.189
  77.8 1.9 %collective-permute-start.10 = (bf16[4,19,8,128]{3,2,1,0:T(8,128)(2,1)S(1)}, bf16[4,19,8,128]{3,2,1,0:T(8,128)(2,1)S(1)}, u32[]{:S(2)}, u32[]{:S(2)}) collective-permute-start(bf16[4,19,8,128]{3,2,1,0:T(8,128)(2,1)S(1)} %get-tuple-element.63), channel_id=1, source_target_pairs={{0,8},{4,36},{8,0},{12,44},{16,24},{20,52},{24,16},{28,60},{32,40}... | collective-permute-start | bytes 466952 | tf_op jit(solution)/shard_map/ppermute | solution.py:418
  79.7 1.3 %collective-permute-start.11 = (bf16[4,19,8,128]{3,2,1,0:T(8,128)(2,1)S(1)}, bf16[4,19,8,128]{3,2,1,0:T(8,128)(2,1)S(1)}, u32[]{:S(2)}, u32[]{:S(2)}) collective-permute-start(bf16[4,19,8,128]{3,2,1,0:T(8,128)(2,1)S(1)} %get-tuple-element.64), channel_id=1, source_target_pairs={{0,24},{4,100},{8,16},{12,108},{16,8},{20,116},{24,0},{28,124},{32... | collective-permute-start | bytes 466952 | tf_op jit(solution)/shard_map/ppermute | solution.py:418
  81.0 0.9 collective-permute-start.9
  81.9 6.4 %collective-permute-done.10.in_two = bf16[4,19,8,128]{3,2,1,0:T(8,128)(2,1)S(1)} collective-permute-done((bf16[4,19,8,128]{3,2,1,0:T(8,128)(2,1)S(1)}, bf16[4,19,8,128]{3,2,1,0:T(8,128)(2,1)S(1)}, u32[]{:S(2)}, u32[]{:S(2)}) %collective-permute-start.10) | collective-permute-done | bytes 155680 | tf_op jit(solution)/shard_map/ppermute | solution.py:418
  88.3 0.0 collective-permute-done.11.in_three
  88.3 2.4 %collective-permute-done.9.in_one = bf16[4,19,8,128]{3,2,1,0:T(8,128)(2,1)S(1)} collective-permute-done((bf16[4,19,8,128]{3,2,1,0:T(8,128)(2,1)S(1)}, bf16[4,19,8,128]{3,2,1,0:T(8,128)(2,1)S(1)}, u32[]{:S(2)}, u32[]{:S(2)}) %collective-permute-start.9) | collective-permute-done | bytes 155680 | tf_op jit(solution)/shard_map/ppermute | solution.py:418
  90.7 0.3 shard_map.190
  91.0 4.0 %collective-permute-start.12 = (bf16[1176,128]{1,0:T(8,128)(2,1)S(1)}, bf16[1176,128]{1,0:T(8,128)(2,1)S(1)}, u32[]{:S(2)}, u32[]{:S(2)}) collective-permute-start(bf16[1176,128]{1,0:T(8,128)(2,1)S(1)} %get-tuple-element.68), channel_id=1, source_target_pairs={{0,64},{4,20},{8,72},{12,28},{16,80},{20,4},{24,88},{28,12},{32,96... | collective-permute-start | bytes 903176 | tf_op jit(solution)/shard_map/ppermute | solution.py:422
  95.0 1.0 collective-permute-start.13
  96.0 0.0 collective-permute-start.14
  96.0 3.8 %collective-permute-done.12.one = bf16[1176,128]{1,0:T(8,128)(2,1)S(1)} collective-permute-done((bf16[1176,128]{1,0:T(8,128)(2,1)S(1)}, bf16[1176,128]{1,0:T(8,128)(2,1)S(1)}, u32[]{:S(2)}, u32[]{:S(2)}) %collective-permute-start.12) | collective-permute-done | bytes 301088 | tf_op jit(solution)/shard_map/ppermute | solution.py:422
  99.8 4.3 %collective-permute-done.13.two = bf16[1176,128]{1,0:T(8,128)(2,1)S(1)} collective-permute-done((bf16[1176,128]{1,0:T(8,128)(2,1)S(1)}, bf16[1176,128]{1,0:T(8,128)(2,1)S(1)}, u32[]{:S(2)}, u32[]{:S(2)}) %collective-permute-start.13) | collective-permute-done | bytes 301088 | tf_op jit(solution)/shard_map/ppermute | solution.py:422
  104.0 0.0 collective-permute-done.14.three
  104.0 0.3 shard_map.191
  104.4 13.5 %all_to_all.11 = bf16[32,4,8,128]{3,2,1,0:T(8,128)(2,1)S(1)} all-to-all(bf16[32,4,8,128]{3,2,1,0:T(8,128)(2,1)S(1)} %get-tuple-element.71), channel_id=1, replica_groups=mesh['client_0'=4,'client_1'=4,'client_2'=2,'head'=4] {'client_0','clien..., dimensions={0} | all-to-all | bytes 524288 | tf_op jit(solution)/shard_map/all_to_all | solution.py:448
  117.9 0.1 convert_reduce_fusion
  117.9 0.6 broadcast_in_dim.2
  118.5 3.4 %all-to-all-start.1 = ((f32[4,1,3]{2,1,0:T(1,128)}), f32[4,1,3]{2,1,0:T(1,128)S(1)}, u32[]{:S(2)}, u32[]{:S(2)}) async-start(f32[4,1,3]{2,1,0:T(1,128)} %broadcast_in_dim.2), calls=%async_computation.1 | async-start | bytes 4096 | tf_op jit(solution)/shard_map/all_to_all | solution.py:448
  122.0 5.2 %all-to-all-done.1 = f32[4,1,3]{2,1,0:T(1,128)S(1)} async-done(((f32[4,1,3]{2,1,0:T(1,128)}), f32[4,1,3]{2,1,0:T(1,128)S(1)}, u32[]{:S(2)}, u32[]{:S(2)}) %all-to-all-start.1) | async-done | bytes 80 | tf_op jit(solution)/shard_map/all_to_all | solution.py:448
  127.2 0.6 fusion.26
  128.4 0.7 convert_multiply_fusion
  129.2 0.6 multiply_bitcast_fusion
  131.2 0.6 broadcast_multiply_fusion.1
  131.8 0.8 broadcast_multiply_fusion
  (21 shorter events, 0.1 us)
Async XLA Ops:
  13.2 1.6 %copy-start = (bf16[1024,1280]{1,0:T(8,128)(2,1)}, bf16[1024,1280]{1,0:T(8,128)(2,1)S(1)}, u32[]{:S(2)}) copy-start(bf16[1024,1280]{1,0:T(8,128)(2,1)S(1)} %get-tuple-element.42.turned) | copy-start | bytes 7864324
  14.8 1.5 %copy-start.3 = (bf16[1280,1024]{1,0:T(8,128)(2,1)}, bf16[1280,1024]{1,0:T(8,128)(2,1)S(1)}, u32[]{:S(2)}) copy-start(bf16[1280,1024]{1,0:T(8,128)(2,1)S(1)} %get-tuple-element.54.low) | copy-start | bytes 7864324
  16.3 14.2 %slice-start = ((s8[10485760]{0:T(1024)(128)(4,1)}), s8[4194304]{0:T(1024)(128)(4,1)S(1)}, s32[]{:S(2)}) async-start(s8[10485760]{0:T(1024)(128)(4,1)} %bitcast.17), calls=%async_computation.2 | async-start | bytes 8388608
  16.3 1.9 %copy-start.1 = (bf16[1024,1280]{1,0:T(8,128)(2,1)S(1)}, bf16[1024,1280]{1,0:T(8,128)(2,1)}, u32[]{:S(2)}) copy-start(bf16[1024,1280]{1,0:T(8,128)(2,1)} %copy-done) | copy-start | bytes 7864324
  18.1 3.5 %copy-start.5 = (bf16[4096,1024]{1,0:T(8,128)(2,1)S(1)}, bf16[4096,1024]{1,0:T(8,128)(2,1)}, u32[]{:S(2)}) copy-start(bf16[4096,1024]{1,0:T(8,128)(2,1)} %source.1) | copy-start | bytes 25165828
  21.7 8.8 %slice-start.1 = ((s8[10485760]{0:T(1024)(128)(4,1)}), s8[4194304]{0:T(1024)(128)(4,1)S(1)}, s32[]{:S(2)}) async-start(s8[10485760]{0:T(1024)(128)(4,1)} %bitcast.17), calls=%async_computation.3 | async-start | bytes 8388608
  21.7 8.8 %slice-start.2 = ((s8[10485760]{0:T(1024)(128)(4,1)}), s8[2097152]{0:T(1024)(128)(4,1)S(1)}, s32[]{:S(2)}) async-start(s8[10485760]{0:T(1024)(128)(4,1)} %bitcast.17), calls=%async_computation.4 | async-start | bytes 4194304
  30.4 4.5 %copy-start.4 = (bf16[1280,1024]{1,0:T(8,128)(2,1)S(1)}, bf16[1280,1024]{1,0:T(8,128)(2,1)}, u32[]{:S(2)}) copy-start(bf16[1280,1024]{1,0:T(8,128)(2,1)} %copy-done.3) | copy-start | bytes 7864324
  30.4 15.3 %collective-permute-start.1 = (bf16[8,1024,128]{2,1,0:T(8,128)(2,1)S(1)}, bf16[8,1024,128]{2,1,0:T(8,128)(2,1)S(1)}, u32[]{:S(2)}, u32[]{:S(2)}) collective-permute-start(bf16[8,1024,128]{2,1,0:T(8,128)(2,1)S(1)} %get-tuple-element.46), channel_id=1, source_target_pairs={{0,4},{4,0},{1,5},{5,1},{2,6},{6,2},{3,7},{7,3},{8,12},{12,8},{9,1... | collective-permute-start | bytes 6291464 | tf_op jit(solution)/shard_map/ppermute | solution.py:426
  34.4 36.6 %collective-permute-start = (bf16[8,1024,128]{2,1,0:T(8,128)(2,1)S(1)}, bf16[8,1024,128]{2,1,0:T(8,128)(2,1)S(1)}, u32[]{:S(2)}, u32[]{:S(2)}) collective-permute-start(bf16[8,1024,128]{2,1,0:T(8,128)(2,1)S(1)} %shard_map.183), channel_id=1, source_target_pairs={{0,4},{4,0},{1,5},{5,1},{2,6},{6,2},{3,7},{7,3},{8,12},{12,8},{9,1... | collective-permute-start | bytes 6291464 | tf_op jit(solution)/shard_map/ppermute | solution.py:426
  34.9 10.8 %copy-start.2 = (bf16[1024,1280]{1,0:T(8,128)(2,1)S(1)}, bf16[1024,1280]{1,0:T(8,128)(2,1)}, u32[]{:S(2)}) copy-start(bf16[1024,1280]{1,0:T(8,128)(2,1)} %copy-done) | copy-start | bytes 7864324
  43.9 18.7 %collective-permute-start.6 = (bf16[2,96,1024]{2,1,0:T(8,128)(2,1)S(1)}, bf16[2,96,1024]{2,1,0:T(8,128)(2,1)S(1)}, u32[]{:S(2)}, u32[]{:S(2)}) collective-permute-start(bf16[2,96,1024]{2,1,0:T(8,128)(2,1)S(1)} %shard_map.188), channel_id=1, source_target_pairs={{0,1},{1,0},{2,3},{3,2},{4,7},{5,6},{6,5},{7,4},{8,9},{9,8},{10,11... | collective-permute-start | bytes 1179656 | tf_op jit(solution)/shard_map/ppermute | solution.py:432
  50.0 20.9 %collective-permute-start.2 = (bf16[4,1024,128]{2,1,0:T(8,128)(2,1)S(1)}, bf16[4,1024,128]{2,1,0:T(8,128)(2,1)S(1)}, u32[]{:S(2)}, u32[]{:S(2)}) collective-permute-start(bf16[4,1024,128]{2,1,0:T(8,128)(2,1)S(1)} %get-tuple-element.47), channel_id=1, source_target_pairs={{0,8},{4,36},{8,0},{12,44},{16,24},{20,52},{24,16},{28,60},{32,40}... | collective-permute-start | bytes 3145736 | tf_op jit(solution)/shard_map/ppermute | solution.py:418
  51.6 19.4 %collective-permute-start.3 = (bf16[4,1024,128]{2,1,0:T(8,128)(2,1)S(1)}, bf16[4,1024,128]{2,1,0:T(8,128)(2,1)S(1)}, u32[]{:S(2)}, u32[]{:S(2)}) collective-permute-start(bf16[4,1024,128]{2,1,0:T(8,128)(2,1)S(1)} %get-tuple-element.48), channel_id=1, source_target_pairs={{0,24},{4,100},{8,16},{12,108},{16,8},{20,116},{24,0},{28,124},{32... | collective-permute-start | bytes 3145736 | tf_op jit(solution)/shard_map/ppermute | solution.py:418
  62.7 7.1 %collective-permute-start.7 = (bf16[96,1024]{1,0:T(8,128)(2,1)S(1)}, bf16[96,1024]{1,0:T(8,128)(2,1)S(1)}, u32[]{:S(2)}, u32[]{:S(2)}) collective-permute-start(bf16[96,1024]{1,0:T(8,128)(2,1)S(1)} %fusion.1), channel_id=1, source_target_pairs={{0,3},{1,2},{2,1},{3,0},{4,5},{5,4},{6,7},{7,6},{8,11},{9,10},{10,... | collective-permute-start | bytes 589832 | tf_op jit(solution)/shard_map/ppermute | solution.py:432
  70.8 6.9 %collective-permute-start.8 = (bf16[16,19,8,128]{3,2,1,0:T(8,128)(2,1)S(1)}, bf16[16,19,8,128]{3,2,1,0:T(8,128)(2,1)S(1)}, u32[]{:S(2)}, u32[]{:S(2)}) collective-permute-start(bf16[16,19,8,128]{3,2,1,0:T(8,128)(2,1)S(1)} %get-tuple-element.60), channel_id=1, source_target_pairs={{0,4},{4,0},{1,5},{5,1},{2,6},{6,2},{3,7},{7,3},{8,12},{12,8},{9,1... | collective-permute-start | bytes 1867784 | tf_op jit(solution)/shard_map/ppermute | solution.py:426
  75.5 15.3 %collective-permute-start.4 = (bf16[2,1024,128]{2,1,0:T(8,128)(2,1)S(1)}, bf16[2,1024,128]{2,1,0:T(8,128)(2,1)S(1)}, u32[]{:S(2)}, u32[]{:S(2)}) collective-permute-start(bf16[2,1024,128]{2,1,0:T(8,128)(2,1)S(1)} %get-tuple-element.50), channel_id=1, source_target_pairs={{0,24},{4,100},{8,16},{12,108},{16,8},{20,116},{24,0},{28,124},{32... | collective-permute-start | bytes 1572872 | tf_op jit(solution)/shard_map/ppermute | solution.py:418
  77.4 13.3 %collective-permute-start.5 = (bf16[2,1024,128]{2,1,0:T(8,128)(2,1)S(1)}, bf16[2,1024,128]{2,1,0:T(8,128)(2,1)S(1)}, u32[]{:S(2)}, u32[]{:S(2)}) collective-permute-start(bf16[2,1024,128]{2,1,0:T(8,128)(2,1)S(1)} %get-tuple-element.51), channel_id=1, source_target_pairs={{0,8},{4,36},{8,0},{12,44},{16,24},{20,52},{24,16},{28,60},{32,40}... | collective-permute-start | bytes 1572872 | tf_op jit(solution)/shard_map/ppermute | solution.py:418
  77.8 10.5 %collective-permute-start.10 = (bf16[4,19,8,128]{3,2,1,0:T(8,128)(2,1)S(1)}, bf16[4,19,8,128]{3,2,1,0:T(8,128)(2,1)S(1)}, u32[]{:S(2)}, u32[]{:S(2)}) collective-permute-start(bf16[4,19,8,128]{3,2,1,0:T(8,128)(2,1)S(1)} %get-tuple-element.63), channel_id=1, source_target_pairs={{0,8},{4,36},{8,0},{12,44},{16,24},{20,52},{24,16},{28,60},{32,40}... | collective-permute-start | bytes 466952 | tf_op jit(solution)/shard_map/ppermute | solution.py:418
  79.7 8.6 %collective-permute-start.11 = (bf16[4,19,8,128]{3,2,1,0:T(8,128)(2,1)S(1)}, bf16[4,19,8,128]{3,2,1,0:T(8,128)(2,1)S(1)}, u32[]{:S(2)}, u32[]{:S(2)}) collective-permute-start(bf16[4,19,8,128]{3,2,1,0:T(8,128)(2,1)S(1)} %get-tuple-element.64), channel_id=1, source_target_pairs={{0,24},{4,100},{8,16},{12,108},{16,8},{20,116},{24,0},{28,124},{32... | collective-permute-start | bytes 466952 | tf_op jit(solution)/shard_map/ppermute | solution.py:418
  81.0 9.7 %collective-permute-start.9 = (bf16[4,19,8,128]{3,2,1,0:T(8,128)(2,1)S(1)}, bf16[4,19,8,128]{3,2,1,0:T(8,128)(2,1)S(1)}, u32[]{:S(2)}, u32[]{:S(2)}) collective-permute-start(bf16[4,19,8,128]{3,2,1,0:T(8,128)(2,1)S(1)} %get-tuple-element.62), channel_id=1, source_target_pairs={{0,16},{4,68},{8,24},{12,76},{16,0},{20,84},{24,8},{28,92},{32,48}... | collective-permute-start | bytes 466952 | tf_op jit(solution)/shard_map/ppermute | solution.py:418
  91.0 8.7 %collective-permute-start.12 = (bf16[1176,128]{1,0:T(8,128)(2,1)S(1)}, bf16[1176,128]{1,0:T(8,128)(2,1)S(1)}, u32[]{:S(2)}, u32[]{:S(2)}) collective-permute-start(bf16[1176,128]{1,0:T(8,128)(2,1)S(1)} %get-tuple-element.68), channel_id=1, source_target_pairs={{0,64},{4,20},{8,72},{12,28},{16,80},{20,4},{24,88},{28,12},{32,96... | collective-permute-start | bytes 903176 | tf_op jit(solution)/shard_map/ppermute | solution.py:422
  95.0 9.0 %collective-permute-start.13 = (bf16[1176,128]{1,0:T(8,128)(2,1)S(1)}, bf16[1176,128]{1,0:T(8,128)(2,1)S(1)}, u32[]{:S(2)}, u32[]{:S(2)}) collective-permute-start(bf16[1176,128]{1,0:T(8,128)(2,1)S(1)} %get-tuple-element.69), channel_id=1, source_target_pairs={{0,32},{4,12},{8,40},{12,4},{16,48},{20,28},{24,56},{28,20},{32,0}... | collective-permute-start | bytes 903176 | tf_op jit(solution)/shard_map/ppermute | solution.py:422
  96.0 8.0 %collective-permute-start.14 = (bf16[1176,128]{1,0:T(8,128)(2,1)S(1)}, bf16[1176,128]{1,0:T(8,128)(2,1)S(1)}, u32[]{:S(2)}, u32[]{:S(2)}) collective-permute-start(bf16[1176,128]{1,0:T(8,128)(2,1)S(1)} %get-tuple-element.70), channel_id=1, source_target_pairs={{0,96},{4,28},{8,104},{12,20},{16,112},{20,12},{24,120},{28,4},{32... | collective-permute-start | bytes 903176 | tf_op jit(solution)/shard_map/ppermute | solution.py:422
  118.5 8.7 %all-to-all-start.1 = ((f32[4,1,3]{2,1,0:T(1,128)}), f32[4,1,3]{2,1,0:T(1,128)S(1)}, u32[]{:S(2)}, u32[]{:S(2)}) async-start(f32[4,1,3]{2,1,0:T(1,128)} %broadcast_in_dim.2), calls=%async_computation.1 | async-start | bytes 4096 | tf_op jit(solution)/shard_map/all_to_all | solution.py:448

commit v2 on v1

v2 whole, which is shorter than its diff:
```python
import jax
import jax.numpy as jnp
from jax import lax
from jax.experimental import pallas as pl
from jax.experimental.pallas import tpu as pltpu
from jax.sharding import Mesh
from jax.sharding import PartitionSpec as P

CLIENT = ("client_0", "client_1", "client_2")
EPSILON = 1e-06
LIMIT = 16 * 2**20
PREPARE_LIMIT = 44 * 2**20
LANES = 128

FIRST = ((2, 0), (2, 1), (1, 0), (1, 1), (2, 2), (2, 3), (3, 2), (3, 3))
ALL = tuple((u, v) for u in range(4) for v in range(4))
KEPT = ((3, 0), (3, 1), (0, 0), (0, 1), (1, 2), (1, 3), (0, 2), (0, 3))


def sigmoid(v):
    return 0.5 * jnp.tanh(0.5 * v) + 0.5


def params(limit=LIMIT):
    return pltpu.CompilerParams(dimension_semantics=("arbitrary",), vmem_limit_bytes=limit)


def whole():
    return pl.BlockSpec(memory_space=pltpu.VMEM)


PARTS = 5
STEP = 4
TILE = 512
CHUNK = 320
SPANS = 80


def position():
    return tuple(lax.axis_index(a) for a in (*CLIENT, "head"))


def owner_at(side, u, v):
    z, x, _, _ = position()
    at_z = jnp.where(side == 0, z ^ v, z ^ u)
    at_x = jnp.where(side == 0, x ^ u, x ^ v)
    return (at_z * 4 + at_x) * 2 + side


def listed(i, places, j):
    early, late = places[j], places[STEP + j]
    return tuple(jnp.where(i == 0, e, l) for e, l in zip(early, late))


def product(owners, pre, turned):
    units = []
    for owner in owners:
        v = pre[:, pl.ds(pl.multiple_of(owner * LANES, LANES), LANES)].astype(jnp.float32)
        units.append((v * sigmoid(v)).astype(jnp.bfloat16))
    return jnp.dot(turned[...], jnp.concatenate(units, axis=1), preferred_element_type=jnp.float32)


def pieces(acc):
    return [acc[:, j * LANES : (j + 1) * LANES] for j in range(STEP)]


def prepare_body(delta, low, turned, sums, buffer, arrived):
    rows = delta.shape[0] // PARTS
    copies = [
        pltpu.make_async_copy(delta.at[pl.ds(k * rows, rows)], buffer.at[k], arrived.at[k]) for k in range(PARTS)
    ]
    for copy in copies:
        copy.start()
    total = None
    for k in range(PARTS):
        copies[k].wait()
        value = buffer[k]
        narrow = value.astype(jnp.bfloat16)
        low[k * rows : (k + 1) * rows, :] = narrow
        turned[:, k * rows : (k + 1) * rows] = narrow.T
        part = jnp.sum(value.reshape(rows // 8, 8, value.shape[1]), axis=0)
        total = part if total is None else total + part
    sums[...] = total


def prepare(delta):
    rows, width = delta.shape
    return pl.pallas_call(
        prepare_body,
        in_specs=[pl.BlockSpec(memory_space=pltpu.HBM)],
        out_specs=[whole()] * 3,
        out_shape=[
            jax.ShapeDtypeStruct((rows, width), jnp.bfloat16),
            jax.ShapeDtypeStruct((width, rows), jnp.bfloat16),
            jax.ShapeDtypeStruct((8, width), jnp.float32),
        ],
        scratch_shapes=[
            pltpu.VMEM((PARTS, rows // PARTS, width), jnp.float32),
            pltpu.SemaphoreType.DMA((PARTS,)),
        ],
        compiler_params=pltpu.CompilerParams(vmem_limit_bytes=PREPARE_LIMIT),
        cost_estimate=pl.CostEstimate(flops=8 * 10**9, bytes_accessed=2 * 10**7, transcendentals=0),
        name="prepare",
    )(delta)


def head_call(body, operands, out_shape):
    return pl.pallas_call(
        body,
        grid=(len(FIRST) // STEP,),
        in_specs=[whole()] * len(operands),
        out_specs=[whole()] * len(out_shape),
        out_shape=out_shape,
        compiler_params=params(),
    )(*operands)


def partner_body(places, pre, turned, out):
    i = pl.program_id(0)
    other = 1 - lax.axis_index("client_2")
    acc = product([owner_at(other, *listed(i, places, j)) for j in range(STEP)], pre, turned)
    for j, piece in enumerate(pieces(acc)):
        out[STEP * i + j] = piece.astype(out.dtype)


def partner_call(places, pre, turned):
    shape = jax.ShapeDtypeStruct((len(FIRST), turned.shape[0], LANES), jnp.bfloat16)
    return head_call(lambda *refs: partner_body(places, *refs), (pre, turned), [shape])[0]


def first_body(pre, turned, arrived, near, far):
    i = pl.program_id(0)
    core = lax.axis_index("client_2")
    acc = product([owner_at(core, *listed(i, FIRST, j)) for j in range(STEP)], pre, turned)

    def store(out, base):
        for j, piece in enumerate(pieces(acc)):
            out[j] = (piece + arrived[base + j].astype(jnp.float32)).astype(out.dtype)

    @pl.when(i == 0)
    def _():
        store(near, 0)

    @pl.when(i == 1)
    def _():
        store(far, STEP)


def first_call(pre, turned, arrived):
    shape = jax.ShapeDtypeStruct((STEP, turned.shape[0], LANES), jnp.bfloat16)
    return head_call(first_body, (pre, turned, arrived), [shape, shape])


def kept_body(pre, turned, arrived, near, far, send_a, send_b, keep):
    i = pl.program_id(0)
    core = lax.axis_index("client_2")
    acc = product([owner_at(core, *listed(i, KEPT, j)) for j in range(STEP)], pre, turned)

    def store(side, base, send, at):
        for j, piece in enumerate(pieces(acc)):
            total = piece + arrived[base + j].astype(jnp.float32) + side[j].astype(jnp.float32)
            if j < STEP // 2:
                send[j] = total.astype(send.dtype)
            else:
                keep[at + j - STEP // 2] = total.astype(keep.dtype)

    @pl.when(i == 0)
    def _():
        store(near, 0, send_a, 0)

    @pl.when(i == 1)
    def _():
        store(far, STEP, send_b, STEP // 2)


def kept_call(pre, turned, arrived, near, far):
    width = turned.shape[0]
    half = jax.ShapeDtypeStruct((STEP // 2, width, LANES), jnp.bfloat16)
    full = jax.ShapeDtypeStruct((STEP, width, LANES), jnp.float32)
    return head_call(kept_body, (pre, turned, arrived, near, far), [half, half, full])


def slope_body(kept, pre, low, weight, out):
    i = pl.program_id(0)
    _, _, core, head = position()
    rows, width = low.shape
    per = width // TILE
    clients = rows // SPANS
    if kept:
        first, second = jnp.where(core == 0, head ^ 3, head ^ 1), head
    else:
        first, second = head ^ 2, jnp.where(core == 0, head ^ 1, head ^ 3)
    at = pl.multiple_of((jnp.where(i < per, first, second) * per + i % per) * TILE, TILE)
    turned = weight[pl.ds(at, TILE), :].T
    put = pl.ds(pl.multiple_of((i % per) * TILE, TILE), TILE)
    spans = None
    for row in range(0, rows, CHUNK):
        part = jnp.dot(low[row : row + CHUNK, :], turned, preferred_element_type=jnp.float32)
        half = 0.5 * pre[row : row + CHUNK, pl.ds(at, TILE)].astype(jnp.float32)
        t = jnp.tanh(half)
        grad = part * ((1.0 + t) * (1.0 + half * (1.0 - t)))
        grad = grad.reshape(CHUNK // SPANS, SPANS, TILE)
        top = row // SPANS
        out[i // per, top : top + CHUNK // SPANS, put] = (0.5 * jnp.sum(grad, axis=1)).astype(out.dtype)
        some = jnp.sum(grad, axis=0)
        spans = some if spans is None else spans + some
    out[i // per, clients:, put] = (0.5 * spans).astype(out.dtype)


def slope_call(kept, pre, low, weight):
    rows, width = low.shape
    return pl.pallas_call(
        lambda *refs: slope_body(kept, *refs),
        grid=(2 * width // TILE,),
        in_specs=[whole()] * 3,
        out_specs=whole(),
        out_shape=jax.ShapeDtypeStruct((2, rows // SPANS + SPANS, width), jnp.float32 if kept else jnp.bfloat16),
        compiler_params=params(),
        name="slope_kept" if kept else "slope_sent",
    )(pre, low, weight)


def small_body(kept, got, got_two, ids, bias, send, keep, square, lines):
    f32 = jnp.float32
    core = lax.axis_index("client_2")
    sums = kept[1] + got[1].astype(f32) + got_two[...].astype(f32)
    width = sums.shape[1]
    across = width // LANES
    clients = ids.shape[1]
    count = 2 * send.shape[0]
    mine = sums[:clients]
    square[...] = jnp.full(square.shape, jnp.sum(mine * mine))
    line = lax.broadcasted_iota(jnp.int32, (count * clients, clients), 0)
    which = line // clients
    side = jnp.where(which < len(ALL), 1 - core, core)
    target = owner_at(side, (which >> 2) & 3, which & 3) * clients + line % clients
    selector = jnp.where(target == ids[...], 1.0, 0.0).astype(jnp.bfloat16)
    placed = jnp.dot(selector, mine.astype(jnp.bfloat16), preferred_element_type=f32)
    spans = sums[clients:]
    lines[...] = jnp.zeros(lines.shape, f32)
    for r in range(SPANS // 8):
        for c in range(across):
            lines[r * across + c] = spans[8 * r : 8 * r + 8, c * LANES : (c + 1) * LANES]
    bias_row = jnp.sum(bias[...], axis=0, keepdims=True)
    for c in range(across):
        lines[SPANS // 8 * across, c : c + 1, :] = bias_row[:, c * LANES : (c + 1) * LANES]
    groups = clients // 8
    share = send.shape[1] - groups * across
    for k in range(count):
        out = send if k < len(ALL) else keep
        at = k % len(ALL)
        for g in range(groups):
            for c in range(across):
                top = k * clients + 8 * g
                block = placed[top : top + 8, c * LANES : (c + 1) * LANES]
                out[at, g * across + c] = block.astype(out.dtype)
        owner = owner_at(1 - core if k < len(ALL) else core, *ALL[at])
        out[at, groups * across :] = lines[pl.ds(share * owner, share)].astype(out.dtype)


def small_sends(kept, got, got_two, ids, bias, share):
    width = kept.shape[2]
    tiles = ids.shape[1] // 8 * (width // LANES) + share
    shape = (len(ALL), tiles, 8, LANES)
    return pl.pallas_call(
        small_body,
        in_specs=[whole()] * 5,
        out_specs=[whole()] * 3,
        out_shape=[
            jax.ShapeDtypeStruct(shape, jnp.bfloat16),
            jax.ShapeDtypeStruct(shape, jnp.float32),
            jax.ShapeDtypeStruct((8, LANES), jnp.float32),
        ],
        scratch_shapes=[pltpu.VMEM((2 * len(ALL) * share, 8, LANES), jnp.float32)],
        compiler_params=pltpu.CompilerParams(vmem_limit_bytes=LIMIT),
        name="small_sends",
    )(kept, got, got_two, ids, bias)


def simple_call(body, operands, shapes):
    return pl.pallas_call(
        body,
        in_specs=[whole()] * len(operands),
        out_specs=[whole()] * len(shapes),
        out_shape=shapes,
        compiler_params=pltpu.CompilerParams(vmem_limit_bytes=LIMIT),
    )(*operands)


def core_sum_body(keep, arrived, own, one, two, three):
    total = keep[...] + arrived[...].astype(jnp.float32)
    own[...] = total[0:4]
    for k, out in ((1, one), (2, two), (3, three)):
        out[...] = total[4 * k : 4 * k + 4].astype(out.dtype)


def core_sum(keep, arrived):
    shape = (keep.shape[0] // 4, *keep.shape[1:])
    low = jax.ShapeDtypeStruct(shape, jnp.bfloat16)
    return simple_call(
        core_sum_body, (keep, arrived), [jax.ShapeDtypeStruct(shape, jnp.float32), low, low, low]
    )


def join_body(keep, got_a, got_b, own, in_one, in_two, in_three, head, small, one, two, three):
    f32 = jnp.float32
    lines = own.shape[1]
    for k in range(4):
        side = got_a if k < 2 else got_b
        total = keep[k] + side[k % 2].astype(f32)
        tiles = own[k] + in_one[k].astype(f32) + in_two[k].astype(f32) + in_three[k].astype(f32)
        if k == 0:
            head[...] = total
            small[...] = tiles
        else:
            out = (one, two, three)[k - 1]
            width = total.shape[0]
            out[:width] = total.astype(out.dtype)
            for t in range(lines):
                out[width + 8 * t : width + 8 * t + 8, :] = tiles[t].astype(out.dtype)


def join(keep, got_a, got_b, own, arrived):
    width = keep.shape[1]
    lines = own.shape[1]
    low = jax.ShapeDtypeStruct((width + 8 * lines, LANES), jnp.bfloat16)
    return simple_call(
        join_body,
        (keep, got_a, got_b, own, *arrived),
        [
            jax.ShapeDtypeStruct((width, LANES), jnp.float32),
            jax.ShapeDtypeStruct((lines, 8, LANES), jnp.float32),
            low,
            low,
            low,
        ],
    )


def close_body(head, small, square, one, two, three, out, embed, shares, scalars):
    f32 = jnp.float32
    width = head.shape[0]
    lines = small.shape[0]
    across = width // LANES
    total = head[...]
    for side in (one, two, three):
        total = total + side[:width].astype(f32)
    out[...] = total.T
    rows = lines - shares.shape[1]
    part = jnp.zeros((8, LANES), f32)
    for t in range(lines):
        at = slice(width + 8 * t, width + 8 * t + 8)
        tile = small[t] + one[at].astype(f32) + two[at].astype(f32) + three[at].astype(f32)
        if t < rows:
            r, c = divmod(t, across)
            embed[8 * r : 8 * r + 8, c * LANES : (c + 1) * LANES] = tile
        else:
            low = tile.astype(shares.dtype)
            part = part + low.astype(f32) * low.astype(f32)
            for p in range(shares.shape[0]):
                shares[p, t - rows] = low
    column = lax.broadcasted_iota(jnp.int32, scalars.shape, 2)
    values = jnp.where(column == 1, square[0:1, :][None], jnp.sum(part))
    scalars[...] = jnp.where(column == 0, jnp.sum(total * total), values)


def close(head, small, square, arrived, peers, share):
    width = head.shape[0]
    rows = 8 * (small.shape[0] - share) * LANES // width
    return simple_call(
        close_body,
        (head, small, square, *arrived),
        [
            jax.ShapeDtypeStruct((LANES, width), jnp.float32),
            jax.ShapeDtypeStruct((rows, width), jnp.float32),
            jax.ShapeDtypeStruct((peers, share, 8, LANES), jnp.bfloat16),
            jax.ShapeDtypeStruct((peers, 1, LANES), jnp.float32),
        ],
    )


def subtotal_body(arrived, out):
    out[...] = jnp.sum(arrived[...], axis=0)


def subtotal(arrived):
    return simple_call(subtotal_body, (arrived,), [jax.ShapeDtypeStruct(arrived.shape[1:], jnp.float32)])[0]


def scale_body(counts, mine, two, one, three, head, embed, shares, head_grad, bias_grad, embed_grad, span_grad):
    f32 = jnp.float32
    totals = (mine[...] + two[...]) + (one[...] + three[...])

    def factor(k):
        mean = totals[:, k : k + 1] / counts[k] + EPSILON
        return jnp.minimum(1.0, 1.0 / jnp.sqrt(mean))

    head_grad[...] = factor(0) * head[...]
    embed_grad[...] = factor(1) * embed[...]
    rest = factor(2)
    across = span_grad.shape[1] // LANES
    share = shares.shape[1]
    for t in range(SPANS // 8 * across):
        r, c = divmod(t, across)
        tile = shares[t // share, t % share].astype(f32)
        span_grad[8 * r : 8 * r + 8, c * LANES : (c + 1) * LANES] = rest * tile
    t = SPANS // 8 * across
    bias_grad[...] = rest * shares[t // share, t % share].astype(f32)


def scale(counts, squares, head, embed, shares):
    width = head.shape[1]
    return simple_call(
        lambda *refs: scale_body(counts, *refs),
        (*squares, head, embed, shares),
        [
            jax.ShapeDtypeStruct(head.shape, jnp.float32),
            jax.ShapeDtypeStruct((width // LANES, LANES), jnp.float32),
            jax.ShapeDtypeStruct(embed.shape, jnp.float32),
            jax.ShapeDtypeStruct((SPANS, width), jnp.float32),
        ],
    )


def flipped(first, second):
    pairs = []
    for z in range(4):
        for x in range(4):
            pairs.append(((z * 4 + x) * 2, ((z ^ first[0]) * 4 + (x ^ first[1])) * 2))
            pairs.append(((z * 4 + x) * 2 + 1, ((z ^ second[0]) * 4 + (x ^ second[1])) * 2 + 1))
    return pairs


def along_u(x, k):
    return lax.ppermute(x, CLIENT, flipped((0, k), (k, 0)))


def along_v(x, k):
    return lax.ppermute(x, CLIENT, flipped((k, 0), (0, k)))


def to_core(x):
    return lax.ppermute(x, "client_2", [(0, 1), (1, 0)])


def along_head(x, low, high):
    axes = ("client_2", "head")
    pairs = [(h, h ^ low) for h in range(4)] + [(4 + h, 4 + (h ^ high)) for h in range(4)]
    return lax.ppermute(x, axes, pairs)


def wide(x):
    return x.astype(jnp.float32)


def narrow(x):
    return x.astype(jnp.bfloat16)


def to_head(x, k):
    return lax.ppermute(x, "head", [(h, h ^ k) for h in range(4)])


def exchange(x, axes):
    return lax.all_to_all(x, axes, 0, 0, tiled=True)


def per_device(pre, delta, head_weight, client_ids):
    hidden_width = pre.shape[1]
    emit_here = delta.shape[1]
    clients_here = client_ids.shape[0]
    head_devices = lax.axis_size("head")
    peers = lax.axis_size(CLIENT)
    share = -(-(SPANS // 8 * (emit_here // LANES) + 1) // peers)

    low, turned, bias_part = prepare(delta)
    part = partner_call(FIRST, pre, turned)
    arrived_first = to_core(part)
    part = partner_call(KEPT, pre, turned)
    arrived_kept = to_core(part)
    near, far = first_call(pre, turned, arrived_first)
    near = along_u(near, 1)
    far = along_u(far, 3)
    sent = slope_call(False, pre, low, head_weight)
    got = along_head(sent, 1, 3)
    kept = slope_call(True, pre, low, head_weight)
    message = narrow(kept[0] + wide(got[0]))
    got_two = along_head(message, 3, 1)
    send_a, send_b, keep = kept_call(pre, turned, arrived_kept, near, far)
    got_a = along_u(send_a, 3)
    got_b = along_u(send_b, 1)
    small_send, small_keep, embed_square = small_sends(
        kept, got, got_two, client_ids[None, :], bias_part, share
    )
    small_got = to_core(small_send)
    own, one, two, three = core_sum(small_keep, small_got)
    arrived = along_u(two, 2), along_u(one, 1), along_u(three, 3)
    final, small, one, two, three = join(keep, got_a, got_b, own, arrived)
    arrived = along_v(two, 2), along_v(one, 1), along_v(three, 3)
    head_raw, embed_raw, shares, scalars = close(final, small, embed_square, arrived, peers, share)
    scalars = exchange(scalars, CLIENT)
    shares = exchange(shares, CLIENT)
    squares = subtotal(scalars)
    squares = (squares, *(to_head(squares, k) for k in (2, 1, 3)))
    emit_total = emit_here * head_devices
    counts = (
        float(hidden_width * emit_total),
        float(clients_here * peers * hidden_width),
        float(SPANS * hidden_width + emit_total),
    )
    head_grad, bias_grad, embed_grad, span_grad = scale(counts, squares, head_raw, embed_raw, shares)
    return head_grad, bias_grad.reshape(emit_here), embed_grad, span_grad


def solution(mesh):
    torus = Mesh(
        mesh.devices.reshape(4, 4, 2, mesh.shape["head"]),
        ("client_0", "client_1", "client_2", "head"),
    )
    return jax.shard_map(
        per_device,
        mesh=torus,
        in_specs=(P(CLIENT, None), P(CLIENT, "head"), P(None, "head"), P(CLIENT)),
        out_specs=(P(CLIENT, "head"), P("head"), P(CLIENT, "head"), P(None, "head")),
        check_vma=False,
    )
```

time: 133 us -> 107 us (0.80); the launches traced: 133 us -> 105 us
  Pallas kernels: 50.6 us -> 36.8 us
  local copies, waits for them, and re-layouts: 9.94 us -> 2.65 us
  other arithmetic: 5.58 us -> 0.04 us
  starting transfers between devices: 23.3 us -> 28.2 us
  waiting for transfers between devices: 26.7 us -> 23.7 us
  between operations: 2.94 us -> 0.8 us
    pallas_call x7, Pallas kernels: 40.3 us -> 31.5 us  [the longest x2 16.5 us: slope_call(): pl.pallas_call(lambda *refs: slope_body(kept, *refs), grid=(2 * width //...]
    pallas_call x1, Pallas kernels: 9.64 us -> 2.9 us  [prepare(): pl.pallas_call(prepare_body, in_specs=[pl.BlockSpec(memory_space=pltpu.HB...]
    unnamed x18 -> x8, local copies, waits for them, and re-layouts: 8.5 us -> 2.65 us
    ppermute x0 -> x3, starting transfers between devices: none -> 4.77 us  [to_head(): return lax.ppermute(x, 'head', [(h, h ^ k) for h in range(4)])]
    all_to_all x1, waiting for transfers between devices: 5.19 us -> 0.8 us  [exchange(): return lax.all_to_all(x, axes, 0, 0, tiled=True)]
    mul x7 -> x0, other arithmetic: 3.05 us -> none  [the longest x1 0.84 us: per_device(): head_factor * head_raw]
    ppermute x0 -> x3, waiting for transfers between devices: none -> 2.55 us  [to_head(): return lax.ppermute(x, 'head', [(h, h ^ k) for h in range(4)])]
    pallas_call x3 -> x5, Pallas kernels: 0.71 us -> 2.41 us  [simple_call(): pl.pallas_call(body, in_specs=[whole()] * len(operands), out_specs=[whole...]
  transfers between devices with their start and end apart: 16 -> 19, of which waited for: 6 -> 9; matrix products, arithmetic and copies ran while one was open for 0% -> 0% of each run, Pallas kernels for 24% -> 27%
where the time goes in v2:
time: 107 us; the launch traced here: 105 us
  Pallas kernels  36.8 us (34%)
  starting transfers between devices  28.2 us (26%)
  waiting for transfers between devices  23.7 us (22%)
  blocking collectives  13 us (12%)
  local copies, waits for them, and re-layouts  2.65 us (2%)
    pallas_call x2, Pallas kernels, slope_call(): pl.pallas_call(lambda *refs: slope_body(kept, *refs), grid=(2 * width //...  16.5 us
    pallas_call x4, Pallas kernels, head_call(): pl.pallas_call(body, grid=(len(FIRST) // STEP,), in_specs=[whole()] * len...  14.3 us
    all_to_all x1, blocking collectives, exchange(): return lax.all_to_all(x, axes, 0, 0, tiled=True)  13 us
    ppermute x7, starting transfers between devices, along_u(): return lax.ppermute(x, CLIENT, flipped((0, k), (k, 0)))  10.4 us
    ppermute x3, waiting for transfers between devices, along_v(): return lax.ppermute(x, CLIENT, flipped((k, 0), (0, k)))  8.03 us
    ppermute x7, waiting for transfers between devices, along_u(): return lax.ppermute(x, CLIENT, flipped((0, k), (k, 0)))  7.63 us
    ppermute x3, starting transfers between devices, to_head(): return lax.ppermute(x, 'head', [(h, h ^ k) for h in range(4)])  4.77 us
    ppermute x2, waiting for transfers between devices, along_head(): return lax.ppermute(x, axes, pairs)  4.7 us
  transfers between devices with their start and end apart: 19, of which 9 were waited for; matrix products, arithmetic and copies ran while one was open for 0% of the time, Pallas kernels for 27%

profile of v2, /device:TPU:0, one launch (start us, length us, event | category | flops | bytes accessed | tf_op | source)
XLA Modules:
  0.0 105.2 jit_solution(5314131555712363401)
XLA Ops:
  0.6 0.0 copy-start
  0.6 2.9 %prepare.1 = (bf16[1280,1024]{1,0:T(8,128)(2,1)S(1)}, bf16[1024,1280]{1,0:T(8,128)(2,1)S(1)}, f32[8,1024]{1,0:T(8,128)S(1)}) custom-call(f32[1280,1024]{1,0:T(8,128)} %delta.1), custom_call_target="tpu_custom_call" | custom-call | flops 8000000000 | bytes 20000000 | tf_op jit(solution)/shard_map/prepare/pallas_call | solution.py:88
  3.5 2.6 %copy-done = bf16[1280,4096]{1,0:T(8,128)(2,1)S(1)} copy-done((bf16[1280,4096]{1,0:T(8,128)(2,1)S(1)}, bf16[1280,4096]{1,0:T(8,128)(2,1)}, u32[]{:S(2)}) %copy-start) | copy-done | bytes 10485784
  6.2 0.0 slice-start
  6.2 3.3 %shard_map.76 = bf16[8,1024,128]{2,1,0:T(8,128)(2,1)S(1)} custom-call(bf16[1280,4096]{1,0:T(8,128)(2,1)S(1)} %copy-done, bf16[1024,1280]{1,0:T(8,128)(2,1)S(1)} %get-tuple-element.32.refs_1_.turned), custom_call_target="tpu_custom_call" | custom-call | tf_op jit(solution)/shard_map/pallas_call | solution.py:108
  9.5 0.0 slice-start.1
  9.5 0.1 collective-permute-start.1
  9.6 3.4 %shard_map.75 = bf16[8,1024,128]{2,1,0:T(8,128)(2,1)S(1)} custom-call(bf16[1280,4096]{1,0:T(8,128)(2,1)S(1)} %copy-done, bf16[1024,1280]{1,0:T(8,128)(2,1)S(1)} %get-tuple-element.32.refs_1_.turned), custom_call_target="tpu_custom_call" | custom-call | tf_op jit(solution)/shard_map/pallas_call | solution.py:108
  13.0 0.5 collective-permute-start
  13.5 0.0 slice-done
  13.5 0.0 slice-done.1
  13.5 8.3 %slope_sent.1 = bf16[2,96,1024]{2,1,0:T(8,128)(2,1)S(1)} custom-call(bf16[1280,4096]{1,0:T(8,128)(2,1)S(1)} %copy-done, bf16[1280,1024]{1,0:T(8,128)(2,1)S(1)} %get-tuple-element.38.refs_1_, bf16[4096,1024]{1,0:T(8,128)(2,1)S(1)} %bitcast.5), custom_call_target="tpu_custom_call" | custom-call | tf_op jit(solution)/shard_map/slope_sent/pallas_call | solution.py:212
  21.8 1.8 %collective-permute-start.6 = (bf16[2,96,1024]{2,1,0:T(8,128)(2,1)S(1)}, bf16[2,96,1024]{2,1,0:T(8,128)(2,1)S(1)}, u32[]{:S(2)}, u32[]{:S(2)}) collective-permute-start(bf16[2,96,1024]{2,1,0:T(8,128)(2,1)S(1)} %slope_sent.1), channel_id=1, source_target_pairs={{0,1},{1,0},{2,3},{3,2},{4,7},{5,6},{6,5},{7,4},{8,9},{9,8},{10,11... | collective-permute-start | bytes 1179656 | tf_op jit(solution)/shard_map/ppermute | solution.py:449
  23.6 0.0 collective-permute-done.1.arrived
  23.6 3.6 %shard_map.77 = (bf16[4,1024,128]{2,1,0:T(8,128)(2,1)S(1)}, bf16[4,1024,128]{2,1,0:T(8,128)(2,1)S(1)}) custom-call(bf16[1280,4096]{1,0:T(8,128)(2,1)S(1)} %copy-done, bf16[1024,1280]{1,0:T(8,128)(2,1)S(1)} %get-tuple-element.32.refs_1_.turned, bf16[8,1024,128]{2,1,0:T(8,128)(2,1)S(1)} %collective-permute-done.1.arrived), custom_call_target="tpu_custom_call" | custom-call | tf_op jit(solution)/shard_map/pallas_call | solution.py:108
  27.2 1.6 %collective-permute-start.2 = (bf16[4,1024,128]{2,1,0:T(8,128)(2,1)S(1)}, bf16[4,1024,128]{2,1,0:T(8,128)(2,1)S(1)}, u32[]{:S(2)}, u32[]{:S(2)}) collective-permute-start(bf16[4,1024,128]{2,1,0:T(8,128)(2,1)S(1)} %get-tuple-element.33), channel_id=1, source_target_pairs={{0,8},{4,36},{8,0},{12,44},{16,24},{20,52},{24,16},{28,60},{32,40}... | collective-permute-start | bytes 3145736 | tf_op jit(solution)/shard_map/ppermute | solution.py:435
  28.8 0.0 copy-start.1
  28.8 2.1 %collective-permute-start.3 = (bf16[4,1024,128]{2,1,0:T(8,128)(2,1)S(1)}, bf16[4,1024,128]{2,1,0:T(8,128)(2,1)S(1)}, u32[]{:S(2)}, u32[]{:S(2)}) collective-permute-start(bf16[4,1024,128]{2,1,0:T(8,128)(2,1)S(1)} %get-tuple-element.34), channel_id=1, source_target_pairs={{0,24},{4,100},{8,16},{12,108},{16,8},{20,116},{24,0},{28,124},{32... | collective-permute-start | bytes 3145736 | tf_op jit(solution)/shard_map/ppermute | solution.py:435
  30.9 8.2 %slope_kept.1.kept = f32[2,96,1024]{2,1,0:T(8,128)S(1)} custom-call(bf16[1280,4096]{1,0:T(8,128)(2,1)S(1)} %copy-done, bf16[1280,1024]{1,0:T(8,128)(2,1)S(1)} %get-tuple-element.38.refs_1_, bf16[4096,1024]{1,0:T(8,128)(2,1)S(1)} %bitcast.5), custom_call_target="tpu_custom_call" | custom-call | tf_op jit(solution)/shard_map/slope_kept/pallas_call | solution.py:212
  39.1 0.0 collective-permute-done.6.got
  39.2 2.3 %collective-permute-start.7 = (bf16[96,1024]{1,0:T(8,128)(2,1)S(1)}, bf16[96,1024]{1,0:T(8,128)(2,1)S(1)}, u32[]{:S(2)}, u32[]{:S(2)}) collective-permute-start(bf16[96,1024]{1,0:T(8,128)(2,1)S(1)} %fusion.1), channel_id=1, source_target_pairs={{0,3},{1,2},{2,1},{3,0},{4,5},{5,4},{6,7},{7,6},{8,11},{9,10},{10,... | collective-permute-start | bytes 589832 | tf_op jit(solution)/shard_map/ppermute | solution.py:449
  41.5 4.7 %collective-permute-done.7.got_two = bf16[96,1024]{1,0:T(8,128)(2,1)S(1)} collective-permute-done((bf16[96,1024]{1,0:T(8,128)(2,1)S(1)}, bf16[96,1024]{1,0:T(8,128)(2,1)S(1)}, u32[]{:S(2)}, u32[]{:S(2)}) %collective-permute-start.7) | collective-permute-done | bytes 196640 | tf_op jit(solution)/shard_map/ppermute | solution.py:449
  46.2 0.0 copy-done.1
  46.2 0.6 small_sends.1
  46.8 0.3 collective-permute-start.8
  47.1 0.0 collective-permute-done.arrived
  47.1 0.0 collective-permute-done.2.near
  47.1 0.0 collective-permute-done.3.far
  47.1 4.0 %shard_map.78 = (bf16[2,1024,128]{2,1,0:T(8,128)(2,1)S(1)}, bf16[2,1024,128]{2,1,0:T(8,128)(2,1)S(1)}, f32[4,1024,128]{2,1,0:T(8,128)S(1)}) custom-call(bf16[1280,4096]{1,0:T(8,128)(2,1)S(1)} %copy-done, bf16[1024,1280]{1,0:T(8,128)(2,1)S(1)} %get-tuple-element.32.refs_1_.turned, bf16[8,1024,128]{2,1,0:T(8,128)(2,1)S(1)} %collective-permute-done.arrived, ...), custom_call_target="tpu_custom_call" | custom-call | tf_op jit(solution)/shard_map/pallas_call | solution.py:108
  51.1 2.0 %collective-permute-start.4 = (bf16[2,1024,128]{2,1,0:T(8,128)(2,1)S(1)}, bf16[2,1024,128]{2,1,0:T(8,128)(2,1)S(1)}, u32[]{:S(2)}, u32[]{:S(2)}) collective-permute-start(bf16[2,1024,128]{2,1,0:T(8,128)(2,1)S(1)} %get-tuple-element.36), channel_id=1, source_target_pairs={{0,24},{4,100},{8,16},{12,108},{16,8},{20,116},{24,0},{28,124},{32... | collective-permute-start | bytes 1572872 | tf_op jit(solution)/shard_map/ppermute | solution.py:435
  53.1 0.3 collective-permute-start.5
  53.4 0.0 collective-permute-done.8.arrived
  53.4 0.2 shard_map.79
  53.5 2.6 %collective-permute-start.9 = (bf16[4,19,8,128]{3,2,1,0:T(8,128)(2,1)S(1)}, bf16[4,19,8,128]{3,2,1,0:T(8,128)(2,1)S(1)}, u32[]{:S(2)}, u32[]{:S(2)}) collective-permute-start(bf16[4,19,8,128]{3,2,1,0:T(8,128)(2,1)S(1)} %get-tuple-element.43), channel_id=1, source_target_pairs={{0,16},{4,68},{8,24},{12,76},{16,0},{20,84},{24,8},{28,92},{32,48}... | collective-permute-start | bytes 466952 | tf_op jit(solution)/shard_map/ppermute | solution.py:435
  56.1 0.0 collective-permute-start.10
  56.2 1.9 %collective-permute-start.11 = (bf16[4,19,8,128]{3,2,1,0:T(8,128)(2,1)S(1)}, bf16[4,19,8,128]{3,2,1,0:T(8,128)(2,1)S(1)}, u32[]{:S(2)}, u32[]{:S(2)}) collective-permute-start(bf16[4,19,8,128]{3,2,1,0:T(8,128)(2,1)S(1)} %get-tuple-element.45), channel_id=1, source_target_pairs={{0,24},{4,100},{8,16},{12,108},{16,8},{20,116},{24,0},{28,124},{32... | collective-permute-start | bytes 466952 | tf_op jit(solution)/shard_map/ppermute | solution.py:435
  58.0 6.8 %collective-permute-done.9.in_one = bf16[4,19,8,128]{3,2,1,0:T(8,128)(2,1)S(1)} collective-permute-done((bf16[4,19,8,128]{3,2,1,0:T(8,128)(2,1)S(1)}, bf16[4,19,8,128]{3,2,1,0:T(8,128)(2,1)S(1)}, u32[]{:S(2)}, u32[]{:S(2)}) %collective-permute-start.9) | collective-permute-done | bytes 155680 | tf_op jit(solution)/shard_map/ppermute | solution.py:435
  64.8 0.8 collective-permute-done.10.in_two
  65.7 0.0 collective-permute-done.11.in_three
  65.7 0.0 collective-permute-done.4.got_a
  65.7 0.0 collective-permute-done.5.got_b
  65.7 0.3 shard_map.80
  66.0 3.2 %collective-permute-start.12 = (bf16[1176,128]{1,0:T(8,128)(2,1)S(1)}, bf16[1176,128]{1,0:T(8,128)(2,1)S(1)}, u32[]{:S(2)}, u32[]{:S(2)}) collective-permute-start(bf16[1176,128]{1,0:T(8,128)(2,1)S(1)} %get-tuple-element.49), channel_id=1, source_target_pairs={{0,64},{4,20},{8,72},{12,28},{16,80},{20,4},{24,88},{28,12},{32,96... | collective-permute-start | bytes 903176 | tf_op jit(solution)/shard_map/ppermute | solution.py:439
  69.2 1.0 collective-permute-start.13
  70.2 0.0 collective-permute-start.14
  70.2 4.1 %collective-permute-done.12.one = bf16[1176,128]{1,0:T(8,128)(2,1)S(1)} collective-permute-done((bf16[1176,128]{1,0:T(8,128)(2,1)S(1)}, bf16[1176,128]{1,0:T(8,128)(2,1)S(1)}, u32[]{:S(2)}, u32[]{:S(2)}) %collective-permute-start.12) | collective-permute-done | bytes 301088 | tf_op jit(solution)/shard_map/ppermute | solution.py:439
  74.4 3.9 %collective-permute-done.13.two = bf16[1176,128]{1,0:T(8,128)(2,1)S(1)} collective-permute-done((bf16[1176,128]{1,0:T(8,128)(2,1)S(1)}, bf16[1176,128]{1,0:T(8,128)(2,1)S(1)}, u32[]{:S(2)}, u32[]{:S(2)}) %collective-permute-start.13) | collective-permute-done | bytes 301088 | tf_op jit(solution)/shard_map/ppermute | solution.py:439
  78.3 0.0 collective-permute-done.14.three
  78.3 0.9 shard_map.81
  79.1 13.0 %all_to_all.10.arrived = f32[32,1,128]{2,1,0:T(1,128)S(1)} all-to-all(f32[32,1,128]{2,1,0:T(1,128)S(1)} %get-tuple-element.52), channel_id=1, replica_groups=mesh['client_0'=4,'client_1'=4,'client_2'=2,'head'=4] {'client_0','clien..., dimensions={0} | all-to-all | bytes 32768 | tf_op jit(solution)/shard_map/all_to_all | solution.py:465
  92.1 3.9 %all-to-all-start.1 = ((bf16[32,3,8,128]{3,2,1,0:T(8,128)(2,1)}), bf16[32,3,8,128]{3,2,1,0:T(8,128)(2,1)S(1)}, u32[]{:S(2)}, u32[]{:S(2)}) async-start(bf16[32,3,8,128]{3,2,1,0:T(8,128)(2,1)} %get-tuple-element.55), calls=%async_computation.1 | async-start | bytes 393216 | tf_op jit(solution)/shard_map/all_to_all | solution.py:465
  96.0 2.2 %collective-permute-start.17 = (f32[1,128]{1,0:T(1,128)S(1)}, f32[1,128]{1,0:T(1,128)S(1)}, u32[]{:S(2)}, u32[]{:S(2)}) collective-permute-start(f32[1,128]{1,0:T(1,128)S(1)} %shard_map.82.refs_0_), channel_id=1, source_target_pairs={{0,3},{1,2},{2,1},{3,0},{4,7},{5,6},{6,5},{7,4},{8,11},{9,10},{10,... | collective-permute-start | bytes 1544 | tf_op jit(solution)/shard_map/ppermute | solution.py:461
  98.3 0.0 collective-permute-start.16
  98.3 2.5 %collective-permute-start.15 = (f32[1,128]{1,0:T(1,128)S(1)}, f32[1,128]{1,0:T(1,128)S(1)}, u32[]{:S(2)}, u32[]{:S(2)}) collective-permute-start(f32[1,128]{1,0:T(1,128)S(1)} %shard_map.82.refs_0_), channel_id=1, source_target_pairs={{0,2},{1,3},{2,0},{3,1},{4,6},{5,7},{6,4},{7,5},{8,10},{9,11},{10,... | collective-permute-start | bytes 1544 | tf_op jit(solution)/shard_map/ppermute | solution.py:461
  100.8 0.1 collective-permute-done.17.refs_3_
  100.9 1.0 collective-permute-done.16.refs_2_
  101.9 1.5 %collective-permute-done.15.refs_1_ = f32[1,128]{1,0:T(1,128)S(1)} collective-permute-done((f32[1,128]{1,0:T(1,128)S(1)}, f32[1,128]{1,0:T(1,128)S(1)}, u32[]{:S(2)}, u32[]{:S(2)}) %collective-permute-start.15) | collective-permute-done | bytes 544 | tf_op jit(solution)/shard_map/ppermute | solution.py:461
  103.4 0.8 all-to-all-done.1.refs_6_
  104.2 1.0 shard_map.83
  (3 shorter events, 0.1 us)
Async XLA Ops:
  0.6 5.6 %copy-start = (bf16[1280,4096]{1,0:T(8,128)(2,1)S(1)}, bf16[1280,4096]{1,0:T(8,128)(2,1)}, u32[]{:S(2)}) copy-start(bf16[1280,4096]{1,0:T(8,128)(2,1)} %refs_0_.7) | copy-start | bytes 31457284
  6.2 7.3 %slice-start = ((s8[8388608]{0:T(1024)(128)(4,1)}), s8[4194304]{0:T(1024)(128)(4,1)S(1)}, s32[]{:S(2)}) async-start(s8[8388608]{0:T(1024)(128)(4,1)} %bitcast.4), calls=%async_computation.2 | async-start | bytes 8388608
  9.5 4.0 %slice-start.1 = ((s8[8388608]{0:T(1024)(128)(4,1)}), s8[4194304]{0:T(1024)(128)(4,1)S(1)}, s32[]{:S(2)}) async-start(s8[8388608]{0:T(1024)(128)(4,1)} %bitcast.4), calls=%async_computation.3 | async-start | bytes 8388608
  9.5 14.1 %collective-permute-start.1 = (bf16[8,1024,128]{2,1,0:T(8,128)(2,1)S(1)}, bf16[8,1024,128]{2,1,0:T(8,128)(2,1)S(1)}, u32[]{:S(2)}, u32[]{:S(2)}) collective-permute-start(bf16[8,1024,128]{2,1,0:T(8,128)(2,1)S(1)} %shard_map.76), channel_id=1, source_target_pairs={{0,4},{4,0},{1,5},{5,1},{2,6},{6,2},{3,7},{7,3},{8,12},{12,8},{9,1... | collective-permute-start | bytes 6291464 | tf_op jit(solution)/shard_map/ppermute | solution.py:443
  13.0 34.1 %collective-permute-start = (bf16[8,1024,128]{2,1,0:T(8,128)(2,1)S(1)}, bf16[8,1024,128]{2,1,0:T(8,128)(2,1)S(1)}, u32[]{:S(2)}, u32[]{:S(2)}) collective-permute-start(bf16[8,1024,128]{2,1,0:T(8,128)(2,1)S(1)} %shard_map.75), channel_id=1, source_target_pairs={{0,4},{4,0},{1,5},{5,1},{2,6},{6,2},{3,7},{7,3},{8,12},{12,8},{9,1... | collective-permute-start | bytes 6291464 | tf_op jit(solution)/shard_map/ppermute | solution.py:443
  21.8 17.3 %collective-permute-start.6 = (bf16[2,96,1024]{2,1,0:T(8,128)(2,1)S(1)}, bf16[2,96,1024]{2,1,0:T(8,128)(2,1)S(1)}, u32[]{:S(2)}, u32[]{:S(2)}) collective-permute-start(bf16[2,96,1024]{2,1,0:T(8,128)(2,1)S(1)} %slope_sent.1), channel_id=1, source_target_pairs={{0,1},{1,0},{2,3},{3,2},{4,7},{5,6},{6,5},{7,4},{8,9},{9,8},{10,11... | collective-permute-start | bytes 1179656 | tf_op jit(solution)/shard_map/ppermute | solution.py:449
  27.2 19.8 %collective-permute-start.2 = (bf16[4,1024,128]{2,1,0:T(8,128)(2,1)S(1)}, bf16[4,1024,128]{2,1,0:T(8,128)(2,1)S(1)}, u32[]{:S(2)}, u32[]{:S(2)}) collective-permute-start(bf16[4,1024,128]{2,1,0:T(8,128)(2,1)S(1)} %get-tuple-element.33), channel_id=1, source_target_pairs={{0,8},{4,36},{8,0},{12,44},{16,24},{20,52},{24,16},{28,60},{32,40}... | collective-permute-start | bytes 3145736 | tf_op jit(solution)/shard_map/ppermute | solution.py:435
  28.8 17.4 %copy-start.1 = (s32[16]{0:T(128)S(1)}, s32[16]{0:T(128)}, u32[]{:S(2)}) copy-start(s32[16]{0:T(128)} %param.7) | copy-start | bytes 196
  28.8 18.3 %collective-permute-start.3 = (bf16[4,1024,128]{2,1,0:T(8,128)(2,1)S(1)}, bf16[4,1024,128]{2,1,0:T(8,128)(2,1)S(1)}, u32[]{:S(2)}, u32[]{:S(2)}) collective-permute-start(bf16[4,1024,128]{2,1,0:T(8,128)(2,1)S(1)} %get-tuple-element.34), channel_id=1, source_target_pairs={{0,24},{4,100},{8,16},{12,108},{16,8},{20,116},{24,0},{28,124},{32... | collective-permute-start | bytes 3145736 | tf_op jit(solution)/shard_map/ppermute | solution.py:435
  39.2 7.0 %collective-permute-start.7 = (bf16[96,1024]{1,0:T(8,128)(2,1)S(1)}, bf16[96,1024]{1,0:T(8,128)(2,1)S(1)}, u32[]{:S(2)}, u32[]{:S(2)}) collective-permute-start(bf16[96,1024]{1,0:T(8,128)(2,1)S(1)} %fusion.1), channel_id=1, source_target_pairs={{0,3},{1,2},{2,1},{3,0},{4,5},{5,4},{6,7},{7,6},{8,11},{9,10},{10,... | collective-permute-start | bytes 589832 | tf_op jit(solution)/shard_map/ppermute | solution.py:449
  46.8 6.6 %collective-permute-start.8 = (bf16[16,19,8,128]{3,2,1,0:T(8,128)(2,1)S(1)}, bf16[16,19,8,128]{3,2,1,0:T(8,128)(2,1)S(1)}, u32[]{:S(2)}, u32[]{:S(2)}) collective-permute-start(bf16[16,19,8,128]{3,2,1,0:T(8,128)(2,1)S(1)} %get-tuple-element.41), channel_id=1, source_target_pairs={{0,4},{4,0},{1,5},{5,1},{2,6},{6,2},{3,7},{7,3},{8,12},{12,8},{9,1... | collective-permute-start | bytes 1867784 | tf_op jit(solution)/shard_map/ppermute | solution.py:443
  51.1 14.5 %collective-permute-start.4 = (bf16[2,1024,128]{2,1,0:T(8,128)(2,1)S(1)}, bf16[2,1024,128]{2,1,0:T(8,128)(2,1)S(1)}, u32[]{:S(2)}, u32[]{:S(2)}) collective-permute-start(bf16[2,1024,128]{2,1,0:T(8,128)(2,1)S(1)} %get-tuple-element.36), channel_id=1, source_target_pairs={{0,24},{4,100},{8,16},{12,108},{16,8},{20,116},{24,0},{28,124},{32... | collective-permute-start | bytes 1572872 | tf_op jit(solution)/shard_map/ppermute | solution.py:435
  53.1 12.6 %collective-permute-start.5 = (bf16[2,1024,128]{2,1,0:T(8,128)(2,1)S(1)}, bf16[2,1024,128]{2,1,0:T(8,128)(2,1)S(1)}, u32[]{:S(2)}, u32[]{:S(2)}) collective-permute-start(bf16[2,1024,128]{2,1,0:T(8,128)(2,1)S(1)} %get-tuple-element.37), channel_id=1, source_target_pairs={{0,8},{4,36},{8,0},{12,44},{16,24},{20,52},{24,16},{28,60},{32,40}... | collective-permute-start | bytes 1572872 | tf_op jit(solution)/shard_map/ppermute | solution.py:435
  53.5 11.3 %collective-permute-start.9 = (bf16[4,19,8,128]{3,2,1,0:T(8,128)(2,1)S(1)}, bf16[4,19,8,128]{3,2,1,0:T(8,128)(2,1)S(1)}, u32[]{:S(2)}, u32[]{:S(2)}) collective-permute-start(bf16[4,19,8,128]{3,2,1,0:T(8,128)(2,1)S(1)} %get-tuple-element.43), channel_id=1, source_target_pairs={{0,16},{4,68},{8,24},{12,76},{16,0},{20,84},{24,8},{28,92},{32,48}... | collective-permute-start | bytes 466952 | tf_op jit(solution)/shard_map/ppermute | solution.py:435
  56.1 9.5 %collective-permute-start.10 = (bf16[4,19,8,128]{3,2,1,0:T(8,128)(2,1)S(1)}, bf16[4,19,8,128]{3,2,1,0:T(8,128)(2,1)S(1)}, u32[]{:S(2)}, u32[]{:S(2)}) collective-permute-start(bf16[4,19,8,128]{3,2,1,0:T(8,128)(2,1)S(1)} %get-tuple-element.44), channel_id=1, source_target_pairs={{0,8},{4,36},{8,0},{12,44},{16,24},{20,52},{24,16},{28,60},{32,40}... | collective-permute-start | bytes 466952 | tf_op jit(solution)/shard_map/ppermute | solution.py:435
  56.2 9.5 %collective-permute-start.11 = (bf16[4,19,8,128]{3,2,1,0:T(8,128)(2,1)S(1)}, bf16[4,19,8,128]{3,2,1,0:T(8,128)(2,1)S(1)}, u32[]{:S(2)}, u32[]{:S(2)}) collective-permute-start(bf16[4,19,8,128]{3,2,1,0:T(8,128)(2,1)S(1)} %get-tuple-element.45), channel_id=1, source_target_pairs={{0,24},{4,100},{8,16},{12,108},{16,8},{20,116},{24,0},{28,124},{32... | collective-permute-start | bytes 466952 | tf_op jit(solution)/shard_map/ppermute | solution.py:435
  66.0 8.4 %collective-permute-start.12 = (bf16[1176,128]{1,0:T(8,128)(2,1)S(1)}, bf16[1176,128]{1,0:T(8,128)(2,1)S(1)}, u32[]{:S(2)}, u32[]{:S(2)}) collective-permute-start(bf16[1176,128]{1,0:T(8,128)(2,1)S(1)} %get-tuple-element.49), channel_id=1, source_target_pairs={{0,64},{4,20},{8,72},{12,28},{16,80},{20,4},{24,88},{28,12},{32,96... | collective-permute-start | bytes 903176 | tf_op jit(solution)/shard_map/ppermute | solution.py:439
  69.2 9.1 %collective-permute-start.13 = (bf16[1176,128]{1,0:T(8,128)(2,1)S(1)}, bf16[1176,128]{1,0:T(8,128)(2,1)S(1)}, u32[]{:S(2)}, u32[]{:S(2)}) collective-permute-start(bf16[1176,128]{1,0:T(8,128)(2,1)S(1)} %get-tuple-element.50), channel_id=1, source_target_pairs={{0,32},{4,12},{8,40},{12,4},{16,48},{20,28},{24,56},{28,20},{32,0}... | collective-permute-start | bytes 903176 | tf_op jit(solution)/shard_map/ppermute | solution.py:439
  70.2 8.0 %collective-permute-start.14 = (bf16[1176,128]{1,0:T(8,128)(2,1)S(1)}, bf16[1176,128]{1,0:T(8,128)(2,1)S(1)}, u32[]{:S(2)}, u32[]{:S(2)}) collective-permute-start(bf16[1176,128]{1,0:T(8,128)(2,1)S(1)} %get-tuple-element.51), channel_id=1, source_target_pairs={{0,96},{4,28},{8,104},{12,20},{16,112},{20,12},{24,120},{28,4},{32... | collective-permute-start | bytes 903176 | tf_op jit(solution)/shard_map/ppermute | solution.py:439
  92.1 12.0 %all-to-all-start.1 = ((bf16[32,3,8,128]{3,2,1,0:T(8,128)(2,1)}), bf16[32,3,8,128]{3,2,1,0:T(8,128)(2,1)S(1)}, u32[]{:S(2)}, u32[]{:S(2)}) async-start(bf16[32,3,8,128]{3,2,1,0:T(8,128)(2,1)} %get-tuple-element.55), calls=%async_computation.1 | async-start | bytes 393216 | tf_op jit(solution)/shard_map/all_to_all | solution.py:465
  96.0 4.9 %collective-permute-start.17 = (f32[1,128]{1,0:T(1,128)S(1)}, f32[1,128]{1,0:T(1,128)S(1)}, u32[]{:S(2)}, u32[]{:S(2)}) collective-permute-start(f32[1,128]{1,0:T(1,128)S(1)} %shard_map.82.refs_0_), channel_id=1, source_target_pairs={{0,3},{1,2},{2,1},{3,0},{4,7},{5,6},{6,5},{7,4},{8,11},{9,10},{10,... | collective-permute-start | bytes 1544 | tf_op jit(solution)/shard_map/ppermute | solution.py:461
  98.3 3.6 %collective-permute-start.16 = (f32[1,128]{1,0:T(1,128)S(1)}, f32[1,128]{1,0:T(1,128)S(1)}, u32[]{:S(2)}, u32[]{:S(2)}) collective-permute-start(f32[1,128]{1,0:T(1,128)S(1)} %shard_map.82.refs_0_), channel_id=1, source_target_pairs={{0,1},{1,0},{2,3},{3,2},{4,5},{5,4},{6,7},{7,6},{8,9},{9,8},{10,11... | collective-permute-start | bytes 1544 | tf_op jit(solution)/shard_map/ppermute | solution.py:461
  98.3 5.1 %collective-permute-start.15 = (f32[1,128]{1,0:T(1,128)S(1)}, f32[1,128]{1,0:T(1,128)S(1)}, u32[]{:S(2)}, u32[]{:S(2)}) collective-permute-start(f32[1,128]{1,0:T(1,128)S(1)} %shard_map.82.refs_0_), channel_id=1, source_target_pairs={{0,2},{1,3},{2,0},{3,1},{4,6},{5,7},{6,4},{7,5},{8,10},{9,11},{10,... | collective-permute-start | bytes 1544 | tf_op jit(solution)/shard_map/ppermute | solution.py:461

commit v3 on v2

--- a/solution.py
+++ b/solution.py
@@ -13,7 +13,7 @@
 LANES = 128
 
 FIRST = ((2, 0), (2, 1), (1, 0), (1, 1), (2, 2), (2, 3), (3, 2), (3, 3))
-ALL = tuple((u, v) for u in range(4) for v in range(4))
+ALL = tuple((u, v) for v in range(4) for u in range(4))
 KEPT = ((3, 0), (3, 1), (0, 0), (0, 1), (1, 2), (1, 3), (0, 2), (0, 3))
 
 
@@ -31,7 +31,7 @@
 
 PARTS = 5
 STEP = 4
-TILE = 512
+TILE = 1024
 CHUNK = 320
 SPANS = 80
 
@@ -45,11 +45,6 @@
     at_z = jnp.where(side == 0, z ^ v, z ^ u)
     at_x = jnp.where(side == 0, x ^ u, x ^ v)
     return (at_z * 4 + at_x) * 2 + side
-
-
-def listed(i, places, j):
-    early, late = places[j], places[STEP + j]
-    return tuple(jnp.where(i == 0, e, l) for e, l in zip(early, late))
 
 
 def product(owners, pre, turned):
@@ -61,7 +56,7 @@
 
 
 def pieces(acc):
-    return [acc[:, j * LANES : (j + 1) * LANES] for j in range(STEP)]
+    return [acc[:, j * LANES : (j + 1) * LANES] for j in range(acc.shape[1] // LANES)]
 
 
 def prepare_body(delta, low, turned, sums, buffer, arrived):
@@ -104,80 +99,60 @@
     )(delta)
 
 
-def head_call(body, operands, out_shape):
+def simple_call(body, operands, shapes):
     return pl.pallas_call(
         body,
-        grid=(len(FIRST) // STEP,),
         in_specs=[whole()] * len(operands),
-        out_specs=[whole()] * len(out_shape),
-        out_shape=out_shape,
-        compiler_params=params(),
+        out_specs=[whole()] * len(shapes),
+        out_shape=shapes,
+        compiler_params=pltpu.CompilerParams(vmem_limit_bytes=LIMIT),
     )(*operands)
 
 
 def partner_body(places, pre, turned, out):
-    i = pl.program_id(0)
     other = 1 - lax.axis_index("client_2")
-    acc = product([owner_at(other, *listed(i, places, j)) for j in range(STEP)], pre, turned)
+    acc = product([owner_at(other, *place) for place in places], pre, turned)
     for j, piece in enumerate(pieces(acc)):
-        out[STEP * i + j] = piece.astype(out.dtype)
+        out[j] = piece.astype(out.dtype)
 
 
 def partner_call(places, pre, turned):
-    shape = jax.ShapeDtypeStruct((len(FIRST), turned.shape[0], LANES), jnp.bfloat16)
-    return head_call(lambda *refs: partner_body(places, *refs), (pre, turned), [shape])[0]
+    shape = jax.ShapeDtypeStruct((len(places), turned.shape[0], LANES), jnp.bfloat16)
+    return simple_call(lambda *refs: partner_body(places, *refs), (pre, turned), [shape])[0]
 
 
 def first_body(pre, turned, arrived, near, far):
-    i = pl.program_id(0)
     core = lax.axis_index("client_2")
-    acc = product([owner_at(core, *listed(i, FIRST, j)) for j in range(STEP)], pre, turned)
-
-    def store(out, base):
-        for j, piece in enumerate(pieces(acc)):
-            out[j] = (piece + arrived[base + j].astype(jnp.float32)).astype(out.dtype)
-
-    @pl.when(i == 0)
-    def _():
-        store(near, 0)
-
-    @pl.when(i == 1)
-    def _():
-        store(far, STEP)
+    acc = product([owner_at(core, *place) for place in FIRST], pre, turned)
+    for j, piece in enumerate(pieces(acc)):
+        out = near if j < STEP else far
+        out[j % STEP] = (piece + arrived[j].astype(jnp.float32)).astype(out.dtype)
 
 
 def first_call(pre, turned, arrived):
     shape = jax.ShapeDtypeStruct((STEP, turned.shape[0], LANES), jnp.bfloat16)
-    return head_call(first_body, (pre, turned, arrived), [shape, shape])
+    return simple_call(first_body, (pre, turned, arrived), [shape, shape])
 
 
 def kept_body(pre, turned, arrived, near, far, send_a, send_b, keep):
-    i = pl.program_id(0)
     core = lax.axis_index("client_2")
-    acc = product([owner_at(core, *listed(i, KEPT, j)) for j in range(STEP)], pre, turned)
-
-    def store(side, base, send, at):
-        for j, piece in enumerate(pieces(acc)):
-            total = piece + arrived[base + j].astype(jnp.float32) + side[j].astype(jnp.float32)
-            if j < STEP // 2:
-                send[j] = total.astype(send.dtype)
-            else:
-                keep[at + j - STEP // 2] = total.astype(keep.dtype)
-
-    @pl.when(i == 0)
-    def _():
-        store(near, 0, send_a, 0)
-
-    @pl.when(i == 1)
-    def _():
-        store(far, STEP, send_b, STEP // 2)
+    acc = product([owner_at(core, *place) for place in KEPT], pre, turned)
+    half = STEP // 2
+    for j, piece in enumerate(pieces(acc)):
+        side, send = (near, send_a) if j < STEP else (far, send_b)
+        k = j % STEP
+        total = piece + arrived[j].astype(jnp.float32) + side[k].astype(jnp.float32)
+        if k < half:
+            send[k] = total.astype(send.dtype)
+        else:
+            keep[j // STEP * half + k - half] = total.astype(keep.dtype)
 
 
 def kept_call(pre, turned, arrived, near, far):
     width = turned.shape[0]
     half = jax.ShapeDtypeStruct((STEP // 2, width, LANES), jnp.bfloat16)
     full = jax.ShapeDtypeStruct((STEP, width, LANES), jnp.float32)
-    return head_call(kept_body, (pre, turned, arrived, near, far), [half, half, full])
+    return simple_call(kept_body, (pre, turned, arrived, near, far), [half, half, full])
 
 
 def slope_body(kept, pre, low, weight, out):
@@ -233,7 +208,7 @@
     line = lax.broadcasted_iota(jnp.int32, (count * clients, clients), 0)
     which = line // clients
     side = jnp.where(which < len(ALL), 1 - core, core)
-    target = owner_at(side, (which >> 2) & 3, which & 3) * clients + line % clients
+    target = owner_at(side, which & 3, (which >> 2) & 3) * clients + line % clients
     selector = jnp.where(target == ids[...], 1.0, 0.0).astype(jnp.bfloat16)
     placed = jnp.dot(selector, mine.astype(jnp.bfloat16), preferred_element_type=f32)
     spans = sums[clients:]
@@ -277,16 +252,6 @@
     )(kept, got, got_two, ids, bias)
 
 
-def simple_call(body, operands, shapes):
-    return pl.pallas_call(
-        body,
-        in_specs=[whole()] * len(operands),
-        out_specs=[whole()] * len(shapes),
-        out_shape=shapes,
-        compiler_params=pltpu.CompilerParams(vmem_limit_bytes=LIMIT),
-    )(*operands)
-
-
 def core_sum_body(keep, arrived, own, one, two, three):
     total = keep[...] + arrived[...].astype(jnp.float32)
     own[...] = total[0:4]
@@ -297,94 +262,101 @@
 def core_sum(keep, arrived):
     shape = (keep.shape[0] // 4, *keep.shape[1:])
     low = jax.ShapeDtypeStruct(shape, jnp.bfloat16)
-    return simple_call(
-        core_sum_body, (keep, arrived), [jax.ShapeDtypeStruct(shape, jnp.float32), low, low, low]
-    )
-
-
-def join_body(keep, got_a, got_b, own, in_one, in_two, in_three, head, small, one, two, three):
+    return simple_call(core_sum_body, (keep, arrived), [jax.ShapeDtypeStruct(shape, jnp.float32), low, low, low])
+
+
+def line_sum_body(own, side_one, side_two, side_three, mine, one, two, three):
     f32 = jnp.float32
-    lines = own.shape[1]
-    for k in range(4):
+    total = own[...] + side_one[...].astype(f32) + side_two[...].astype(f32) + side_three[...].astype(f32)
+    mine[...] = total[0]
+    for k, out in ((1, one), (2, two), (3, three)):
+        out[...] = total[k].astype(out.dtype)
+
+
+def line_sum(own, arrived):
+    shape = own.shape[1:]
+    low = jax.ShapeDtypeStruct(shape, jnp.bfloat16)
+    return simple_call(line_sum_body, (own, *arrived), [jax.ShapeDtypeStruct(shape, jnp.float32), low, low, low])
+
+
+def join_body(keep, got_a, got_b, head, one, two, three):
+    for k, out in enumerate((head, one, two, three)):
         side = got_a if k < 2 else got_b
-        total = keep[k] + side[k % 2].astype(f32)
-        tiles = own[k] + in_one[k].astype(f32) + in_two[k].astype(f32) + in_three[k].astype(f32)
-        if k == 0:
-            head[...] = total
-            small[...] = tiles
-        else:
-            out = (one, two, three)[k - 1]
-            width = total.shape[0]
-            out[:width] = total.astype(out.dtype)
-            for t in range(lines):
-                out[width + 8 * t : width + 8 * t + 8, :] = tiles[t].astype(out.dtype)
-
-
-def join(keep, got_a, got_b, own, arrived):
-    width = keep.shape[1]
-    lines = own.shape[1]
-    low = jax.ShapeDtypeStruct((width + 8 * lines, LANES), jnp.bfloat16)
-    return simple_call(
-        join_body,
-        (keep, got_a, got_b, own, *arrived),
-        [
-            jax.ShapeDtypeStruct((width, LANES), jnp.float32),
-            jax.ShapeDtypeStruct((lines, 8, LANES), jnp.float32),
-            low,
-            low,
-            low,
-        ],
-    )
-
-
-def close_body(head, small, square, one, two, three, out, embed, shares, scalars):
+        out[...] = (keep[k] + side[k % 2].astype(jnp.float32)).astype(out.dtype)
+
+
+def join(keep, got_a, got_b):
+    low = jax.ShapeDtypeStruct(keep.shape[1:], jnp.bfloat16)
+    own = jax.ShapeDtypeStruct(keep.shape[1:], jnp.float32)
+    return simple_call(join_body, (keep, got_a, got_b), [own, low, low, low])
+
+
+def close_body(head, one, two, three, small, s_one, s_two, s_three, square, total, embed, message):
     f32 = jnp.float32
     width = head.shape[0]
     lines = small.shape[0]
     across = width // LANES
-    total = head[...]
-    for side in (one, two, three):
-        total = total + side[:width].astype(f32)
-    out[...] = total.T
-    rows = lines - shares.shape[1]
+    peers, share = message.shape[0], message.shape[1] - 1
+    rows = lines - share
     part = jnp.zeros((8, LANES), f32)
     for t in range(lines):
-        at = slice(width + 8 * t, width + 8 * t + 8)
-        tile = small[t] + one[at].astype(f32) + two[at].astype(f32) + three[at].astype(f32)
+        tile = small[t] + s_one[t].astype(f32) + s_two[t].astype(f32) + s_three[t].astype(f32)
         if t < rows:
             r, c = divmod(t, across)
             embed[8 * r : 8 * r + 8, c * LANES : (c + 1) * LANES] = tile
         else:
-            low = tile.astype(shares.dtype)
+            low = tile.astype(message.dtype)
             part = part + low.astype(f32) * low.astype(f32)
-            for p in range(shares.shape[0]):
-                shares[p, t - rows] = low
-    column = lax.broadcasted_iota(jnp.int32, scalars.shape, 2)
-    values = jnp.where(column == 1, square[0:1, :][None], jnp.sum(part))
-    scalars[...] = jnp.where(column == 0, jnp.sum(total * total), values)
-
-
-def close(head, small, square, arrived, peers, share):
+            for p in range(peers):
+                message[p, t - rows] = low
+    value = head[...]
+    for side in (one, two, three):
+        value = value + side[...].astype(f32)
+    total[...] = value
+    column = lax.broadcasted_iota(jnp.int32, (8, LANES), 1)
+    line = lax.broadcasted_iota(jnp.int32, (8, LANES), 0)
+    sums = jnp.where(column == 1, square[...], jnp.sum(part))
+    sums = jnp.where(column == 0, jnp.sum(value * value), sums)
+    coarse = sums.astype(message.dtype).astype(f32)
+    scalars = jnp.where(line == 0, coarse, jnp.where(line == 1, sums - coarse, 0.0)).astype(message.dtype)
+    for p in range(peers):
+        message[p, share] = scalars
+
+
+def close(head, arrived, small, small_arrived, square, peers, share):
     width = head.shape[0]
     rows = 8 * (small.shape[0] - share) * LANES // width
     return simple_call(
         close_body,
-        (head, small, square, *arrived),
+        (head, *arrived, small, *small_arrived, square),
         [
-            jax.ShapeDtypeStruct((LANES, width), jnp.float32),
+            jax.ShapeDtypeStruct((width, LANES), jnp.float32),
             jax.ShapeDtypeStruct((rows, width), jnp.float32),
-            jax.ShapeDtypeStruct((peers, share, 8, LANES), jnp.bfloat16),
-            jax.ShapeDtypeStruct((peers, 1, LANES), jnp.float32),
+            jax.ShapeDtypeStruct((peers, share + 1, 8, LANES), jnp.bfloat16),
         ],
     )
 
 
+def turn_body(value, out):
+    out[...] = value[...].T
+
+
+def turn(value):
+    return simple_call(turn_body, (value,), [jax.ShapeDtypeStruct(value.shape[::-1], value.dtype)])[0]
+
+
 def subtotal_body(arrived, out):
-    out[...] = jnp.sum(arrived[...], axis=0)
+    last = arrived.shape[1] - 1
+    total = None
+    for p in range(arrived.shape[0]):
+        some = arrived[p, last].astype(jnp.float32)
+        total = some if total is None else total + some
+    out[...] = jnp.sum(total, axis=0, keepdims=True)
 
 
 def subtotal(arrived):
-    return simple_call(subtotal_body, (arrived,), [jax.ShapeDtypeStruct(arrived.shape[1:], jnp.float32)])[0]
+    shape = jax.ShapeDtypeStruct((1, arrived.shape[3]), jnp.float32)
+    return simple_call(subtotal_body, (arrived,), [shape])[0]
 
 
 def scale_body(counts, mine, two, one, three, head, embed, shares, head_grad, bias_grad, embed_grad, span_grad):
@@ -399,7 +371,7 @@
     embed_grad[...] = factor(1) * embed[...]
     rest = factor(2)
     across = span_grad.shape[1] // LANES
-    share = shares.shape[1]
+    share = shares.shape[1] - 1
     for t in range(SPANS // 8 * across):
         r, c = divmod(t, across)
         tile = shares[t // share, t % share].astype(f32)
@@ -489,18 +461,18 @@
     send_a, send_b, keep = kept_call(pre, turned, arrived_kept, near, far)
     got_a = along_u(send_a, 3)
     got_b = along_u(send_b, 1)
-    small_send, small_keep, embed_square = small_sends(
-        kept, got, got_two, client_ids[None, :], bias_part, share
-    )
+    small_send, small_keep, embed_square = small_sends(kept, got, got_two, client_ids[None, :], bias_part, share)
     small_got = to_core(small_send)
     own, one, two, three = core_sum(small_keep, small_got)
-    arrived = along_u(two, 2), along_u(one, 1), along_u(three, 3)
-    final, small, one, two, three = join(keep, got_a, got_b, own, arrived)
-    arrived = along_v(two, 2), along_v(one, 1), along_v(three, 3)
-    head_raw, embed_raw, shares, scalars = close(final, small, embed_square, arrived, peers, share)
-    scalars = exchange(scalars, CLIENT)
-    shares = exchange(shares, CLIENT)
-    squares = subtotal(scalars)
+    small_arrived = along_v(one, 1), along_v(two, 2), along_v(three, 3)
+    final, one, two, three = join(keep, got_a, got_b)
+    arrived = along_v(one, 1), along_v(two, 2), along_v(three, 3)
+    small, one, two, three = line_sum(own, small_arrived)
+    small_arrived = along_u(one, 1), along_u(two, 2), along_u(three, 3)
+    total, embed_raw, message = close(final, arrived, small, small_arrived, embed_square, peers, share)
+    shares = exchange(message, CLIENT)
+    head_raw = turn(total)
+    squares = subtotal(shares)
     squares = (squares, *(to_head(squares, k) for k in (2, 1, 3)))
     emit_total = emit_here * head_devices
     counts = (

time: 107 us -> 107 us (level); the launches traced: 105 us -> 107 us
  waiting for transfers between devices: 23.7 us -> 30.3 us
  Pallas kernels: 36.8 us -> 31.4 us
  starting transfers between devices: 28.2 us -> 29.3 us
    pallas_call x4 -> x0, Pallas kernels: 14.3 us -> none  [head_call(): pl.pallas_call(body, grid=(len(FIRST) // STEP,), in_specs=[whole()] * len...]
    pallas_call x5 -> x11, Pallas kernels: 2.41 us -> 14.4 us  [simple_call(): pl.pallas_call(body, in_specs=[whole()] * len(operands), out_specs=[whole...]
    ppermute x7, waiting for transfers between devices: 7.63 us -> 13.9 us  [along_u(): return lax.ppermute(x, CLIENT, flipped((0, k), (k, 0)))]
    ppermute x3 -> x6, starting transfers between devices: 4.25 us -> 8.94 us  [along_v(): return lax.ppermute(x, CLIENT, flipped((k, 0), (0, k)))]
    all_to_all x1 -> x0, starting transfers between devices: 3.87 us -> none  [exchange(): return lax.all_to_all(x, axes, 0, 0, tiled=True)]
    pallas_call x2, Pallas kernels: 16.5 us -> 13.4 us  [slope_call(): pl.pallas_call(lambda *refs: slope_body(kept, *refs), grid=(2 * width //...]
    ppermute x3 -> x6, waiting for transfers between devices: 8.03 us -> 9.23 us  [along_v(): return lax.ppermute(x, CLIENT, flipped((k, 0), (0, k)))]
  transfers between devices with their start and end apart: 19 -> 21, of which waited for: 9 -> 10; matrix products, arithmetic and copies ran while one was open for 0% -> 0% of each run, Pallas kernels for 27% -> 22%
where the time goes in v3:
time: 107 us
  Pallas kernels  31.4 us (29%)
  waiting for transfers between devices  30.3 us (28%)
  starting transfers between devices  29.3 us (27%)
  blocking collectives  12.1 us (11%)
  local copies, waits for them, and re-layouts  2.65 us (2%)
    pallas_call x11, Pallas kernels, simple_call(): pl.pallas_call(body, in_specs=[whole()] * len(operands), out_specs=[whole...  14.4 us
    ppermute x7, waiting for transfers between devices, along_u(): return lax.ppermute(x, CLIENT, flipped((0, k), (k, 0)))  13.9 us
    pallas_call x2, Pallas kernels, slope_call(): pl.pallas_call(lambda *refs: slope_body(kept, *refs), grid=(2 * width //...  13.4 us
    all_to_all x1, blocking collectives, exchange(): return lax.all_to_all(x, axes, 0, 0, tiled=True)  12.1 us
    ppermute x7, starting transfers between devices, along_u(): return lax.ppermute(x, CLIENT, flipped((0, k), (k, 0)))  10.7 us
    ppermute x6, waiting for transfers between devices, along_v(): return lax.ppermute(x, CLIENT, flipped((k, 0), (0, k)))  9.23 us
    ppermute x6, starting transfers between devices, along_v(): return lax.ppermute(x, CLIENT, flipped((k, 0), (0, k)))  8.94 us
    ppermute x3, starting transfers between devices, to_head(): return lax.ppermute(x, 'head', [(h, h ^ k) for h in range(4)])  4.77 us
  transfers between devices with their start and end apart: 21, of which 10 were waited for; matrix products, arithmetic and copies ran while one was open for 0% of the time, Pallas kernels for 22%

profile of v3, /device:TPU:0, one launch (start us, length us, event | category | flops | bytes accessed | tf_op | source)
XLA Modules:
  0.0 106.7 jit_solution(14346521867381188032)
XLA Ops:
  0.6 0.0 copy-start
  0.6 2.9 %prepare.1 = (bf16[1280,1024]{1,0:T(8,128)(2,1)S(1)}, bf16[1024,1280]{1,0:T(8,128)(2,1)S(1)}, f32[8,1024]{1,0:T(8,128)S(1)}) custom-call(f32[1280,1024]{1,0:T(8,128)} %delta.1), custom_call_target="tpu_custom_call" | custom-call | flops 8000000000 | bytes 20000000 | tf_op jit(solution)/shard_map/prepare/pallas_call | solution.py:83
  3.5 2.6 %copy-done = bf16[1280,4096]{1,0:T(8,128)(2,1)S(1)} copy-done((bf16[1280,4096]{1,0:T(8,128)(2,1)S(1)}, bf16[1280,4096]{1,0:T(8,128)(2,1)}, u32[]{:S(2)}) %copy-start) | copy-done | bytes 10485784
  6.2 0.0 slice-start
  6.2 3.0 %shard_map.76 = bf16[8,1024,128]{2,1,0:T(8,128)(2,1)S(1)} custom-call(bf16[1280,4096]{1,0:T(8,128)(2,1)S(1)} %copy-done, bf16[1024,1280]{1,0:T(8,128)(2,1)S(1)} %get-tuple-element.34.refs_1_.turned), custom_call_target="tpu_custom_call" | custom-call | tf_op jit(solution)/shard_map/pallas_call | solution.py:103
  9.2 0.0 slice-start.1
  9.2 0.1 collective-permute-start.1
  9.3 3.0 %shard_map.75 = bf16[8,1024,128]{2,1,0:T(8,128)(2,1)S(1)} custom-call(bf16[1280,4096]{1,0:T(8,128)(2,1)S(1)} %copy-done, bf16[1024,1280]{1,0:T(8,128)(2,1)S(1)} %get-tuple-element.34.refs_1_.turned), custom_call_target="tpu_custom_call" | custom-call | tf_op jit(solution)/shard_map/pallas_call | solution.py:103
  12.3 0.5 collective-permute-start
  12.9 0.0 slice-done
  12.9 0.0 slice-done.1
  12.9 6.7 %slope_sent.1 = bf16[2,96,1024]{2,1,0:T(8,128)(2,1)S(1)} custom-call(bf16[1280,4096]{1,0:T(8,128)(2,1)S(1)} %copy-done, bf16[1280,1024]{1,0:T(8,128)(2,1)S(1)} %get-tuple-element.44.refs_1_, bf16[4096,1024]{1,0:T(8,128)(2,1)S(1)} %bitcast.5), custom_call_target="tpu_custom_call" | custom-call | tf_op jit(solution)/shard_map/slope_sent/pallas_call | solution.py:187
  19.6 2.0 %collective-permute-start.9 = (bf16[2,96,1024]{2,1,0:T(8,128)(2,1)S(1)}, bf16[2,96,1024]{2,1,0:T(8,128)(2,1)S(1)}, u32[]{:S(2)}, u32[]{:S(2)}) collective-permute-start(bf16[2,96,1024]{2,1,0:T(8,128)(2,1)S(1)} %slope_sent.1), channel_id=1, source_target_pairs={{0,1},{1,0},{2,3},{3,2},{4,7},{5,6},{6,5},{7,4},{8,9},{9,8},{10,11... | collective-permute-start | bytes 1179656 | tf_op jit(solution)/shard_map/ppermute | solution.py:421
  21.5 0.0 collective-permute-done.1.arrived
  21.5 3.0 %shard_map.77 = (bf16[4,1024,128]{2,1,0:T(8,128)(2,1)S(1)}, bf16[4,1024,128]{2,1,0:T(8,128)(2,1)S(1)}) custom-call(bf16[1280,4096]{1,0:T(8,128)(2,1)S(1)} %copy-done, bf16[1024,1280]{1,0:T(8,128)(2,1)S(1)} %get-tuple-element.34.refs_1_.turned, bf16[8,1024,128]{2,1,0:T(8,128)(2,1)S(1)} %collective-permute-done.1.arrived), custom_call_target="tpu_custom_call" | custom-call | tf_op jit(solution)/shard_map/pallas_call | solution.py:103
  24.6 1.6 %collective-permute-start.2 = (bf16[4,1024,128]{2,1,0:T(8,128)(2,1)S(1)}, bf16[4,1024,128]{2,1,0:T(8,128)(2,1)S(1)}, u32[]{:S(2)}, u32[]{:S(2)}) collective-permute-start(bf16[4,1024,128]{2,1,0:T(8,128)(2,1)S(1)} %get-tuple-element.35), channel_id=1, source_target_pairs={{0,8},{4,36},{8,0},{12,44},{16,24},{20,52},{24,16},{28,60},{32,40}... | collective-permute-start | bytes 3145736 | tf_op jit(solution)/shard_map/ppermute | solution.py:407
  26.2 2.1 %collective-permute-start.3 = (bf16[4,1024,128]{2,1,0:T(8,128)(2,1)S(1)}, bf16[4,1024,128]{2,1,0:T(8,128)(2,1)S(1)}, u32[]{:S(2)}, u32[]{:S(2)}) collective-permute-start(bf16[4,1024,128]{2,1,0:T(8,128)(2,1)S(1)} %get-tuple-element.36), channel_id=1, source_target_pairs={{0,24},{4,100},{8,16},{12,108},{16,8},{20,116},{24,0},{28,124},{32... | collective-permute-start | bytes 3145736 | tf_op jit(solution)/shard_map/ppermute | solution.py:407
  28.3 6.7 %slope_kept.1.kept = f32[2,96,1024]{2,1,0:T(8,128)S(1)} custom-call(bf16[1280,4096]{1,0:T(8,128)(2,1)S(1)} %copy-done, bf16[1280,1024]{1,0:T(8,128)(2,1)S(1)} %get-tuple-element.44.refs_1_, bf16[4096,1024]{1,0:T(8,128)(2,1)S(1)} %bitcast.5), custom_call_target="tpu_custom_call" | custom-call | tf_op jit(solution)/shard_map/slope_kept/pallas_call | solution.py:187
  35.0 0.0 collective-permute-done.9.got
  35.1 2.3 %collective-permute-start.10 = (bf16[96,1024]{1,0:T(8,128)(2,1)S(1)}, bf16[96,1024]{1,0:T(8,128)(2,1)S(1)}, u32[]{:S(2)}, u32[]{:S(2)}) collective-permute-start(bf16[96,1024]{1,0:T(8,128)(2,1)S(1)} %fusion.1), channel_id=1, source_target_pairs={{0,3},{1,2},{2,1},{3,0},{4,5},{5,4},{6,7},{7,6},{8,11},{9,10},{10,... | collective-permute-start | bytes 589832 | tf_op jit(solution)/shard_map/ppermute | solution.py:421
  37.3 4.7 %collective-permute-done.10.got_two = bf16[96,1024]{1,0:T(8,128)(2,1)S(1)} collective-permute-done((bf16[96,1024]{1,0:T(8,128)(2,1)S(1)}, bf16[96,1024]{1,0:T(8,128)(2,1)S(1)}, u32[]{:S(2)}, u32[]{:S(2)}) %collective-permute-start.10) | collective-permute-done | bytes 196640 | tf_op jit(solution)/shard_map/ppermute | solution.py:421
  42.0 0.0 copy-done.1
  42.0 0.6 small_sends.1
  42.7 0.1 collective-permute-start.11
  42.8 0.0 collective-permute-done.arrived
  42.8 0.0 collective-permute-done.2.near
  42.8 0.0 collective-permute-done.3.far
  42.8 3.2 %shard_map.78 = (bf16[2,1024,128]{2,1,0:T(8,128)(2,1)S(1)}, bf16[2,1024,128]{2,1,0:T(8,128)(2,1)S(1)}, f32[4,1024,128]{2,1,0:T(8,128)S(1)}) custom-call(bf16[1280,4096]{1,0:T(8,128)(2,1)S(1)} %copy-done, bf16[1024,1280]{1,0:T(8,128)(2,1)S(1)} %get-tuple-element.34.refs_1_.turned, bf16[8,1024,128]{2,1,0:T(8,128)(2,1)S(1)} %collective-permute-done.arrived, ...), custom_call_target="tpu_custom_call" | custom-call | tf_op jit(solution)/shard_map/pallas_call | solution.py:103
  46.0 2.3 %collective-permute-start.4 = (bf16[2,1024,128]{2,1,0:T(8,128)(2,1)S(1)}, bf16[2,1024,128]{2,1,0:T(8,128)(2,1)S(1)}, u32[]{:S(2)}, u32[]{:S(2)}) collective-permute-start(bf16[2,1024,128]{2,1,0:T(8,128)(2,1)S(1)} %get-tuple-element.38), channel_id=1, source_target_pairs={{0,24},{4,100},{8,16},{12,108},{16,8},{20,116},{24,0},{28,124},{32... | collective-permute-start | bytes 1572872 | tf_op jit(solution)/shard_map/ppermute | solution.py:407
  48.3 0.0 collective-permute-start.5
  48.3 0.0 collective-permute-done.11.arrived
  48.3 0.1 shard_map.80
  48.4 1.3 %collective-permute-start.12 = (bf16[4,19,8,128]{3,2,1,0:T(8,128)(2,1)S(1)}, bf16[4,19,8,128]{3,2,1,0:T(8,128)(2,1)S(1)}, u32[]{:S(2)}, u32[]{:S(2)}) collective-permute-start(bf16[4,19,8,128]{3,2,1,0:T(8,128)(2,1)S(1)} %get-tuple-element.49), channel_id=1, source_target_pairs={{0,32},{4,12},{8,40},{12,4},{16,48},{20,28},{24,56},{28,20},{32,0}... | collective-permute-start | bytes 466952 | tf_op jit(solution)/shard_map/ppermute | solution.py:411
  49.7 6.7 %collective-permute-done.4.got_a = bf16[2,1024,128]{2,1,0:T(8,128)(2,1)S(1)} collective-permute-done((bf16[2,1024,128]{2,1,0:T(8,128)(2,1)S(1)}, bf16[2,1024,128]{2,1,0:T(8,128)(2,1)S(1)}, u32[]{:S(2)}, u32[]{:S(2)}) %collective-permute-start.4) | collective-permute-done | bytes 524320 | tf_op jit(solution)/shard_map/ppermute | solution.py:407
  56.5 2.7 %collective-permute-done.5.got_b = bf16[2,1024,128]{2,1,0:T(8,128)(2,1)S(1)} collective-permute-done((bf16[2,1024,128]{2,1,0:T(8,128)(2,1)S(1)}, bf16[2,1024,128]{2,1,0:T(8,128)(2,1)S(1)}, u32[]{:S(2)}, u32[]{:S(2)}) %collective-permute-start.5) | collective-permute-done | bytes 524320 | tf_op jit(solution)/shard_map/ppermute | solution.py:407
  59.1 0.2 shard_map.79
  59.4 1.5 %collective-permute-start.6 = (bf16[1024,128]{1,0:T(8,128)(2,1)S(1)}, bf16[1024,128]{1,0:T(8,128)(2,1)S(1)}, u32[]{:S(2)}, u32[]{:S(2)}) collective-permute-start(bf16[1024,128]{1,0:T(8,128)(2,1)S(1)} %get-tuple-element.41), channel_id=1, source_target_pairs={{0,32},{4,12},{8,40},{12,4},{16,48},{20,28},{24,56},{28,20},{32,0}... | collective-permute-start | bytes 786440 | tf_op jit(solution)/shard_map/ppermute | solution.py:411
  60.8 2.1 %collective-permute-start.7 = (bf16[1024,128]{1,0:T(8,128)(2,1)S(1)}, bf16[1024,128]{1,0:T(8,128)(2,1)S(1)}, u32[]{:S(2)}, u32[]{:S(2)}) collective-permute-start(bf16[1024,128]{1,0:T(8,128)(2,1)S(1)} %get-tuple-element.42), channel_id=1, source_target_pairs={{0,64},{4,20},{8,72},{12,28},{16,80},{20,4},{24,88},{28,12},{32,96... | collective-permute-start | bytes 786440 | tf_op jit(solution)/shard_map/ppermute | solution.py:411
  62.9 1.4 %collective-permute-start.8 = (bf16[1024,128]{1,0:T(8,128)(2,1)S(1)}, bf16[1024,128]{1,0:T(8,128)(2,1)S(1)}, u32[]{:S(2)}, u32[]{:S(2)}) collective-permute-start(bf16[1024,128]{1,0:T(8,128)(2,1)S(1)} %get-tuple-element.43), channel_id=1, source_target_pairs={{0,96},{4,28},{8,104},{12,20},{16,112},{20,12},{24,120},{28,4},{32... | collective-permute-start | bytes 786440 | tf_op jit(solution)/shard_map/ppermute | solution.py:411
  64.4 1.7 %collective-permute-start.13 = (bf16[4,19,8,128]{3,2,1,0:T(8,128)(2,1)S(1)}, bf16[4,19,8,128]{3,2,1,0:T(8,128)(2,1)S(1)}, u32[]{:S(2)}, u32[]{:S(2)}) collective-permute-start(bf16[4,19,8,128]{3,2,1,0:T(8,128)(2,1)S(1)} %get-tuple-element.50), channel_id=1, source_target_pairs={{0,64},{4,20},{8,72},{12,28},{16,80},{20,4},{24,88},{28,12},{32,96... | collective-permute-start | bytes 466952 | tf_op jit(solution)/shard_map/ppermute | solution.py:411
  66.0 0.0 collective-permute-done.12.side_one
  66.0 1.0 collective-permute-start.14
  67.0 4.8 %collective-permute-done.13.side_two = bf16[4,19,8,128]{3,2,1,0:T(8,128)(2,1)S(1)} collective-permute-done((bf16[4,19,8,128]{3,2,1,0:T(8,128)(2,1)S(1)}, bf16[4,19,8,128]{3,2,1,0:T(8,128)(2,1)S(1)}, u32[]{:S(2)}, u32[]{:S(2)}) %collective-permute-start.13) | collective-permute-done | bytes 155680 | tf_op jit(solution)/shard_map/ppermute | solution.py:411
  71.9 4.4 %collective-permute-done.14.side_three = bf16[4,19,8,128]{3,2,1,0:T(8,128)(2,1)S(1)} collective-permute-done((bf16[4,19,8,128]{3,2,1,0:T(8,128)(2,1)S(1)}, bf16[4,19,8,128]{3,2,1,0:T(8,128)(2,1)S(1)}, u32[]{:S(2)}, u32[]{:S(2)}) %collective-permute-start.14) | collective-permute-done | bytes 155680 | tf_op jit(solution)/shard_map/ppermute | solution.py:411
  76.2 0.1 shard_map.81
  76.3 0.7 collective-permute-start.15
  77.0 2.5 %collective-permute-start.16 = (bf16[19,8,128]{2,1,0:T(8,128)(2,1)S(1)}, bf16[19,8,128]{2,1,0:T(8,128)(2,1)S(1)}, u32[]{:S(2)}, u32[]{:S(2)}) collective-permute-start(bf16[19,8,128]{2,1,0:T(8,128)(2,1)S(1)} %get-tuple-element.54), channel_id=1, source_target_pairs={{0,16},{4,68},{8,24},{12,76},{16,0},{20,84},{24,8},{28,92},{32,48}... | collective-permute-start | bytes 116744 | tf_op jit(solution)/shard_map/ppermute | solution.py:407
  79.4 0.9 collective-permute-done.15.s_one
  80.4 1.6 %collective-permute-start.17 = (bf16[19,8,128]{2,1,0:T(8,128)(2,1)S(1)}, bf16[19,8,128]{2,1,0:T(8,128)(2,1)S(1)}, u32[]{:S(2)}, u32[]{:S(2)}) collective-permute-start(bf16[19,8,128]{2,1,0:T(8,128)(2,1)S(1)} %get-tuple-element.55), channel_id=1, source_target_pairs={{0,24},{4,100},{8,16},{12,108},{16,8},{20,116},{24,0},{28,124},{32... | collective-permute-start | bytes 116744 | tf_op jit(solution)/shard_map/ppermute | solution.py:407
  82.0 0.5 collective-permute-done.16.s_two
  82.5 3.1 %collective-permute-done.17.s_three = bf16[19,8,128]{2,1,0:T(8,128)(2,1)S(1)} collective-permute-done((bf16[19,8,128]{2,1,0:T(8,128)(2,1)S(1)}, bf16[19,8,128]{2,1,0:T(8,128)(2,1)S(1)}, u32[]{:S(2)}, u32[]{:S(2)}) %collective-permute-start.17) | collective-permute-done | bytes 38944 | tf_op jit(solution)/shard_map/ppermute | solution.py:407
  85.6 0.0 collective-permute-done.6.one
  85.6 0.0 collective-permute-done.7.two
  85.6 0.0 collective-permute-done.8.three
  85.6 0.4 shard_map.82
  86.0 12.1 %all_to_all.5.arrived.refs_6_ = bf16[32,4,8,128]{3,2,1,0:T(8,128)(2,1)S(1)} all-to-all(bf16[32,4,8,128]{3,2,1,0:T(8,128)(2,1)S(1)} %get-tuple-element.57), channel_id=1, replica_groups=mesh['client_0'=4,'client_1'=4,'client_2'=2,'head'=4] {'client_0','clien..., dimensions={0} | all-to-all | bytes 524288 | tf_op jit(solution)/shard_map/all_to_all | solution.py:437
  98.2 2.2 %collective-permute-start.20 = (f32[1,128]{1,0:T(1,128)S(1)}, f32[1,128]{1,0:T(1,128)S(1)}, u32[]{:S(2)}, u32[]{:S(2)}) collective-permute-start(f32[1,128]{1,0:T(1,128)S(1)} %shard_map.83.refs_0_), channel_id=1, source_target_pairs={{0,3},{1,2},{2,1},{3,0},{4,7},{5,6},{6,5},{7,4},{8,11},{9,10},{10,... | collective-permute-start | bytes 1544 | tf_op jit(solution)/shard_map/ppermute | solution.py:433
  100.4 0.2 collective-permute-start.19
  100.6 2.4 %collective-permute-start.18 = (f32[1,128]{1,0:T(1,128)S(1)}, f32[1,128]{1,0:T(1,128)S(1)}, u32[]{:S(2)}, u32[]{:S(2)}) collective-permute-start(f32[1,128]{1,0:T(1,128)S(1)} %shard_map.83.refs_0_), channel_id=1, source_target_pairs={{0,2},{1,3},{2,0},{3,1},{4,6},{5,7},{6,4},{7,5},{8,10},{9,11},{10,... | collective-permute-start | bytes 1544 | tf_op jit(solution)/shard_map/ppermute | solution.py:433
  102.9 0.2 shard_map.84.refs_4_
  103.2 0.0 collective-permute-done.20.refs_3_
  103.2 0.8 collective-permute-done.19.refs_2_
  104.0 1.7 %collective-permute-done.18.refs_1_ = f32[1,128]{1,0:T(1,128)S(1)} collective-permute-done((f32[1,128]{1,0:T(1,128)S(1)}, f32[1,128]{1,0:T(1,128)S(1)}, u32[]{:S(2)}, u32[]{:S(2)}) %collective-permute-start.18) | collective-permute-done | bytes 544 | tf_op jit(solution)/shard_map/ppermute | solution.py:433
  105.6 1.0 shard_map.85
  (4 shorter events, 0.1 us)
Async XLA Ops:
  0.6 5.6 %copy-start = (bf16[1280,4096]{1,0:T(8,128)(2,1)S(1)}, bf16[1280,4096]{1,0:T(8,128)(2,1)}, u32[]{:S(2)}) copy-start(bf16[1280,4096]{1,0:T(8,128)(2,1)} %refs_0_.7) | copy-start | bytes 31457284
  6.2 6.7 %slice-start = ((s8[8388608]{0:T(1024)(128)(4,1)}), s8[4194304]{0:T(1024)(128)(4,1)S(1)}, s32[]{:S(2)}) async-start(s8[8388608]{0:T(1024)(128)(4,1)} %bitcast.4), calls=%async_computation.1 | async-start | bytes 8388608
  9.2 3.7 %slice-start.1 = ((s8[8388608]{0:T(1024)(128)(4,1)}), s8[4194304]{0:T(1024)(128)(4,1)S(1)}, s32[]{:S(2)}) async-start(s8[8388608]{0:T(1024)(128)(4,1)} %bitcast.4), calls=%async_computation.2 | async-start | bytes 8388608
  9.2 12.3 %collective-permute-start.1 = (bf16[8,1024,128]{2,1,0:T(8,128)(2,1)S(1)}, bf16[8,1024,128]{2,1,0:T(8,128)(2,1)S(1)}, u32[]{:S(2)}, u32[]{:S(2)}) collective-permute-start(bf16[8,1024,128]{2,1,0:T(8,128)(2,1)S(1)} %shard_map.76), channel_id=1, source_target_pairs={{0,4},{4,0},{1,5},{5,1},{2,6},{6,2},{3,7},{7,3},{8,12},{12,8},{9,1... | collective-permute-start | bytes 6291464 | tf_op jit(solution)/shard_map/ppermute | solution.py:415
  12.3 30.4 %collective-permute-start = (bf16[8,1024,128]{2,1,0:T(8,128)(2,1)S(1)}, bf16[8,1024,128]{2,1,0:T(8,128)(2,1)S(1)}, u32[]{:S(2)}, u32[]{:S(2)}) collective-permute-start(bf16[8,1024,128]{2,1,0:T(8,128)(2,1)S(1)} %shard_map.75), channel_id=1, source_target_pairs={{0,4},{4,0},{1,5},{5,1},{2,6},{6,2},{3,7},{7,3},{8,12},{12,8},{9,1... | collective-permute-start | bytes 6291464 | tf_op jit(solution)/shard_map/ppermute | solution.py:415
  19.6 15.4 %collective-permute-start.9 = (bf16[2,96,1024]{2,1,0:T(8,128)(2,1)S(1)}, bf16[2,96,1024]{2,1,0:T(8,128)(2,1)S(1)}, u32[]{:S(2)}, u32[]{:S(2)}) collective-permute-start(bf16[2,96,1024]{2,1,0:T(8,128)(2,1)S(1)} %slope_sent.1), channel_id=1, source_target_pairs={{0,1},{1,0},{2,3},{3,2},{4,7},{5,6},{6,5},{7,4},{8,9},{9,8},{10,11... | collective-permute-start | bytes 1179656 | tf_op jit(solution)/shard_map/ppermute | solution.py:421
  24.6 18.2 %collective-permute-start.2 = (bf16[4,1024,128]{2,1,0:T(8,128)(2,1)S(1)}, bf16[4,1024,128]{2,1,0:T(8,128)(2,1)S(1)}, u32[]{:S(2)}, u32[]{:S(2)}) collective-permute-start(bf16[4,1024,128]{2,1,0:T(8,128)(2,1)S(1)} %get-tuple-element.35), channel_id=1, source_target_pairs={{0,8},{4,36},{8,0},{12,44},{16,24},{20,52},{24,16},{28,60},{32,40}... | collective-permute-start | bytes 3145736 | tf_op jit(solution)/shard_map/ppermute | solution.py:407
  26.2 15.9 %copy-start.1 = (s32[16]{0:T(128)S(1)}, s32[16]{0:T(128)}, u32[]{:S(2)}) copy-start(s32[16]{0:T(128)} %param.7) | copy-start | bytes 196
  26.2 16.6 %collective-permute-start.3 = (bf16[4,1024,128]{2,1,0:T(8,128)(2,1)S(1)}, bf16[4,1024,128]{2,1,0:T(8,128)(2,1)S(1)}, u32[]{:S(2)}, u32[]{:S(2)}) collective-permute-start(bf16[4,1024,128]{2,1,0:T(8,128)(2,1)S(1)} %get-tuple-element.36), channel_id=1, source_target_pairs={{0,24},{4,100},{8,16},{12,108},{16,8},{20,116},{24,0},{28,124},{32... | collective-permute-start | bytes 3145736 | tf_op jit(solution)/shard_map/ppermute | solution.py:407
  35.1 7.0 %collective-permute-start.10 = (bf16[96,1024]{1,0:T(8,128)(2,1)S(1)}, bf16[96,1024]{1,0:T(8,128)(2,1)S(1)}, u32[]{:S(2)}, u32[]{:S(2)}) collective-permute-start(bf16[96,1024]{1,0:T(8,128)(2,1)S(1)} %fusion.1), channel_id=1, source_target_pairs={{0,3},{1,2},{2,1},{3,0},{4,5},{5,4},{6,7},{7,6},{8,11},{9,10},{10,... | collective-permute-start | bytes 589832 | tf_op jit(solution)/shard_map/ppermute | solution.py:421
  42.7 5.6 %collective-permute-start.11 = (bf16[16,19,8,128]{3,2,1,0:T(8,128)(2,1)S(1)}, bf16[16,19,8,128]{3,2,1,0:T(8,128)(2,1)S(1)}, u32[]{:S(2)}, u32[]{:S(2)}) collective-permute-start(bf16[16,19,8,128]{3,2,1,0:T(8,128)(2,1)S(1)} %get-tuple-element.47), channel_id=1, source_target_pairs={{0,4},{4,0},{1,5},{5,1},{2,6},{6,2},{3,7},{7,3},{8,12},{12,8},{9,1... | collective-permute-start | bytes 1867784 | tf_op jit(solution)/shard_map/ppermute | solution.py:415
  46.0 10.5 %collective-permute-start.4 = (bf16[2,1024,128]{2,1,0:T(8,128)(2,1)S(1)}, bf16[2,1024,128]{2,1,0:T(8,128)(2,1)S(1)}, u32[]{:S(2)}, u32[]{:S(2)}) collective-permute-start(bf16[2,1024,128]{2,1,0:T(8,128)(2,1)S(1)} %get-tuple-element.38), channel_id=1, source_target_pairs={{0,24},{4,100},{8,16},{12,108},{16,8},{20,116},{24,0},{28,124},{32... | collective-permute-start | bytes 1572872 | tf_op jit(solution)/shard_map/ppermute | solution.py:407
  48.3 10.8 %collective-permute-start.5 = (bf16[2,1024,128]{2,1,0:T(8,128)(2,1)S(1)}, bf16[2,1024,128]{2,1,0:T(8,128)(2,1)S(1)}, u32[]{:S(2)}, u32[]{:S(2)}) collective-permute-start(bf16[2,1024,128]{2,1,0:T(8,128)(2,1)S(1)} %get-tuple-element.39), channel_id=1, source_target_pairs={{0,8},{4,36},{8,0},{12,44},{16,24},{20,52},{24,16},{28,60},{32,40}... | collective-permute-start | bytes 1572872 | tf_op jit(solution)/shard_map/ppermute | solution.py:407
  48.4 17.6 %collective-permute-start.12 = (bf16[4,19,8,128]{3,2,1,0:T(8,128)(2,1)S(1)}, bf16[4,19,8,128]{3,2,1,0:T(8,128)(2,1)S(1)}, u32[]{:S(2)}, u32[]{:S(2)}) collective-permute-start(bf16[4,19,8,128]{3,2,1,0:T(8,128)(2,1)S(1)} %get-tuple-element.49), channel_id=1, source_target_pairs={{0,32},{4,12},{8,40},{12,4},{16,48},{20,28},{24,56},{28,20},{32,0}... | collective-permute-start | bytes 466952 | tf_op jit(solution)/shard_map/ppermute | solution.py:411
  59.4 26.2 %collective-permute-start.6 = (bf16[1024,128]{1,0:T(8,128)(2,1)S(1)}, bf16[1024,128]{1,0:T(8,128)(2,1)S(1)}, u32[]{:S(2)}, u32[]{:S(2)}) collective-permute-start(bf16[1024,128]{1,0:T(8,128)(2,1)S(1)} %get-tuple-element.41), channel_id=1, source_target_pairs={{0,32},{4,12},{8,40},{12,4},{16,48},{20,28},{24,56},{28,20},{32,0}... | collective-permute-start | bytes 786440 | tf_op jit(solution)/shard_map/ppermute | solution.py:411
  60.8 24.7 %collective-permute-start.7 = (bf16[1024,128]{1,0:T(8,128)(2,1)S(1)}, bf16[1024,128]{1,0:T(8,128)(2,1)S(1)}, u32[]{:S(2)}, u32[]{:S(2)}) collective-permute-start(bf16[1024,128]{1,0:T(8,128)(2,1)S(1)} %get-tuple-element.42), channel_id=1, source_target_pairs={{0,64},{4,20},{8,72},{12,28},{16,80},{20,4},{24,88},{28,12},{32,96... | collective-permute-start | bytes 786440 | tf_op jit(solution)/shard_map/ppermute | solution.py:411
  62.9 22.6 %collective-permute-start.8 = (bf16[1024,128]{1,0:T(8,128)(2,1)S(1)}, bf16[1024,128]{1,0:T(8,128)(2,1)S(1)}, u32[]{:S(2)}, u32[]{:S(2)}) collective-permute-start(bf16[1024,128]{1,0:T(8,128)(2,1)S(1)} %get-tuple-element.43), channel_id=1, source_target_pairs={{0,96},{4,28},{8,104},{12,20},{16,112},{20,12},{24,120},{28,4},{32... | collective-permute-start | bytes 786440 | tf_op jit(solution)/shard_map/ppermute | solution.py:411
  64.4 7.5 %collective-permute-start.13 = (bf16[4,19,8,128]{3,2,1,0:T(8,128)(2,1)S(1)}, bf16[4,19,8,128]{3,2,1,0:T(8,128)(2,1)S(1)}, u32[]{:S(2)}, u32[]{:S(2)}) collective-permute-start(bf16[4,19,8,128]{3,2,1,0:T(8,128)(2,1)S(1)} %get-tuple-element.50), channel_id=1, source_target_pairs={{0,64},{4,20},{8,72},{12,28},{16,80},{20,4},{24,88},{28,12},{32,96... | collective-permute-start | bytes 466952 | tf_op jit(solution)/shard_map/ppermute | solution.py:411
  66.0 10.2 %collective-permute-start.14 = (bf16[4,19,8,128]{3,2,1,0:T(8,128)(2,1)S(1)}, bf16[4,19,8,128]{3,2,1,0:T(8,128)(2,1)S(1)}, u32[]{:S(2)}, u32[]{:S(2)}) collective-permute-start(bf16[4,19,8,128]{3,2,1,0:T(8,128)(2,1)S(1)} %get-tuple-element.51), channel_id=1, source_target_pairs={{0,96},{4,28},{8,104},{12,20},{16,112},{20,12},{24,120},{28,4},{32... | collective-permute-start | bytes 466952 | tf_op jit(solution)/shard_map/ppermute | solution.py:411
  76.3 4.1 %collective-permute-start.15 = (bf16[19,8,128]{2,1,0:T(8,128)(2,1)S(1)}, bf16[19,8,128]{2,1,0:T(8,128)(2,1)S(1)}, u32[]{:S(2)}, u32[]{:S(2)}) collective-permute-start(bf16[19,8,128]{2,1,0:T(8,128)(2,1)S(1)} %get-tuple-element.53), channel_id=1, source_target_pairs={{0,8},{4,36},{8,0},{12,44},{16,24},{20,52},{24,16},{28,60},{32,40}... | collective-permute-start | bytes 116744 | tf_op jit(solution)/shard_map/ppermute | solution.py:407
  77.0 5.5 %collective-permute-start.16 = (bf16[19,8,128]{2,1,0:T(8,128)(2,1)S(1)}, bf16[19,8,128]{2,1,0:T(8,128)(2,1)S(1)}, u32[]{:S(2)}, u32[]{:S(2)}) collective-permute-start(bf16[19,8,128]{2,1,0:T(8,128)(2,1)S(1)} %get-tuple-element.54), channel_id=1, source_target_pairs={{0,16},{4,68},{8,24},{12,76},{16,0},{20,84},{24,8},{28,92},{32,48}... | collective-permute-start | bytes 116744 | tf_op jit(solution)/shard_map/ppermute | solution.py:407
  80.4 5.2 %collective-permute-start.17 = (bf16[19,8,128]{2,1,0:T(8,128)(2,1)S(1)}, bf16[19,8,128]{2,1,0:T(8,128)(2,1)S(1)}, u32[]{:S(2)}, u32[]{:S(2)}) collective-permute-start(bf16[19,8,128]{2,1,0:T(8,128)(2,1)S(1)} %get-tuple-element.55), channel_id=1, source_target_pairs={{0,24},{4,100},{8,16},{12,108},{16,8},{20,116},{24,0},{28,124},{32... | collective-permute-start | bytes 116744 | tf_op jit(solution)/shard_map/ppermute | solution.py:407
  98.2 5.0 %collective-permute-start.20 = (f32[1,128]{1,0:T(1,128)S(1)}, f32[1,128]{1,0:T(1,128)S(1)}, u32[]{:S(2)}, u32[]{:S(2)}) collective-permute-start(f32[1,128]{1,0:T(1,128)S(1)} %shard_map.83.refs_0_), channel_id=1, source_target_pairs={{0,3},{1,2},{2,1},{3,0},{4,7},{5,6},{6,5},{7,4},{8,11},{9,10},{10,... | collective-permute-start | bytes 1544 | tf_op jit(solution)/shard_map/ppermute | solution.py:433
  100.4 3.6 %collective-permute-start.19 = (f32[1,128]{1,0:T(1,128)S(1)}, f32[1,128]{1,0:T(1,128)S(1)}, u32[]{:S(2)}, u32[]{:S(2)}) collective-permute-start(f32[1,128]{1,0:T(1,128)S(1)} %shard_map.83.refs_0_), channel_id=1, source_target_pairs={{0,1},{1,0},{2,3},{3,2},{4,5},{5,4},{6,7},{7,6},{8,9},{9,8},{10,11... | collective-permute-start | bytes 1544 | tf_op jit(solution)/shard_map/ppermute | solution.py:433
  100.6 5.1 %collective-permute-start.18 = (f32[1,128]{1,0:T(1,128)S(1)}, f32[1,128]{1,0:T(1,128)S(1)}, u32[]{:S(2)}, u32[]{:S(2)}) collective-permute-start(f32[1,128]{1,0:T(1,128)S(1)} %shard_map.83.refs_0_), channel_id=1, source_target_pairs={{0,2},{1,3},{2,0},{3,1},{4,6},{5,7},{6,4},{7,5},{8,10},{9,11},{10,... | collective-permute-start | bytes 1544 | tf_op jit(solution)/shard_map/ppermute | solution.py:433

commit v4 on v3

--- a/solution.py
+++ b/solution.py
@@ -9,7 +9,7 @@
 CLIENT = ("client_0", "client_1", "client_2")
 EPSILON = 1e-06
 LIMIT = 16 * 2**20
-PREPARE_LIMIT = 44 * 2**20
+PREPARE_LIMIT = 46 * 2**20
 LANES = 128
 
 FIRST = ((2, 0), (2, 1), (1, 0), (1, 1), (2, 2), (2, 3), (3, 2), (3, 3))
@@ -50,7 +50,8 @@
 def product(owners, pre, turned):
     units = []
     for owner in owners:
-        v = pre[:, pl.ds(pl.multiple_of(owner * LANES, LANES), LANES)].astype(jnp.float32)
+        at = owner * LANES if isinstance(owner, int) else pl.multiple_of(owner * LANES, LANES)
+        v = pre[:, pl.ds(at, LANES)].astype(jnp.float32)
         units.append((v * sigmoid(v)).astype(jnp.bfloat16))
     return jnp.dot(turned[...], jnp.concatenate(units, axis=1), preferred_element_type=jnp.float32)
 
@@ -59,13 +60,20 @@
     return [acc[:, j * LANES : (j + 1) * LANES] for j in range(acc.shape[1] // LANES)]
 
 
-def prepare_body(delta, low, turned, sums, buffer, arrived):
+def prepare_body(delta, source, low, turned, sums, early, buffer, arrived, loaded):
     rows = delta.shape[0] // PARTS
     copies = [
         pltpu.make_async_copy(delta.at[pl.ds(k * rows, rows)], buffer.at[k], arrived.at[k]) for k in range(PARTS)
     ]
     for copy in copies:
         copy.start()
+    other = 1 - lax.axis_index("client_2")
+    loads = []
+    for k, place in enumerate(FIRST):
+        at = pl.ds(pl.multiple_of(owner_at(other, *place) * LANES, LANES), LANES)
+        to = slice(k * LANES, (k + 1) * LANES)
+        loads.append(pltpu.make_async_copy(source.at[:, at], early.at[:, to], loaded.at[k]))
+        loads[-1].start()
     total = None
     for k in range(PARTS):
         copies[k].wait()
@@ -76,27 +84,31 @@
         part = jnp.sum(value.reshape(rows // 8, 8, value.shape[1]), axis=0)
         total = part if total is None else total + part
     sums[...] = total
-
-
-def prepare(delta):
+    for load in loads:
+        load.wait()
+
+
+def prepare(delta, pre):
     rows, width = delta.shape
     return pl.pallas_call(
         prepare_body,
-        in_specs=[pl.BlockSpec(memory_space=pltpu.HBM)],
-        out_specs=[whole()] * 3,
+        in_specs=[pl.BlockSpec(memory_space=pltpu.HBM)] * 2,
+        out_specs=[whole()] * 4,
         out_shape=[
             jax.ShapeDtypeStruct((rows, width), jnp.bfloat16),
             jax.ShapeDtypeStruct((width, rows), jnp.bfloat16),
             jax.ShapeDtypeStruct((8, width), jnp.float32),
+            jax.ShapeDtypeStruct((rows, len(FIRST) * LANES), pre.dtype),
         ],
         scratch_shapes=[
             pltpu.VMEM((PARTS, rows // PARTS, width), jnp.float32),
             pltpu.SemaphoreType.DMA((PARTS,)),
+            pltpu.SemaphoreType.DMA((len(FIRST),)),
         ],
         compiler_params=pltpu.CompilerParams(vmem_limit_bytes=PREPARE_LIMIT),
         cost_estimate=pl.CostEstimate(flops=8 * 10**9, bytes_accessed=2 * 10**7, transcendentals=0),
         name="prepare",
-    )(delta)
+    )(delta, pre)
 
 
 def simple_call(body, operands, shapes):
@@ -109,16 +121,19 @@
     )(*operands)
 
 
-def partner_body(places, pre, turned, out):
-    other = 1 - lax.axis_index("client_2")
-    acc = product([owner_at(other, *place) for place in places], pre, turned)
+def partner_body(owners, pre, turned, out):
+    acc = product(owners(), pre, turned)
     for j, piece in enumerate(pieces(acc)):
         out[j] = piece.astype(out.dtype)
 
 
-def partner_call(places, pre, turned):
-    shape = jax.ShapeDtypeStruct((len(places), turned.shape[0], LANES), jnp.bfloat16)
-    return simple_call(lambda *refs: partner_body(places, *refs), (pre, turned), [shape])[0]
+def partner_call(owners, pre, turned):
+    shape = jax.ShapeDtypeStruct((len(FIRST), turned.shape[0], LANES), jnp.bfloat16)
+    return simple_call(lambda *refs: partner_body(owners, *refs), (pre, turned), [shape])[0]
+
+
+def partner_kept():
+    return [owner_at(1 - lax.axis_index("client_2"), *place) for place in KEPT]
 
 
 def first_body(pre, turned, arrived, near, far):
@@ -445,10 +460,10 @@
     peers = lax.axis_size(CLIENT)
     share = -(-(SPANS // 8 * (emit_here // LANES) + 1) // peers)
 
-    low, turned, bias_part = prepare(delta)
-    part = partner_call(FIRST, pre, turned)
+    low, turned, bias_part, early = prepare(delta, pre)
+    part = partner_call(lambda: range(len(FIRST)), early, turned)
     arrived_first = to_core(part)
-    part = partner_call(KEPT, pre, turned)
+    part = partner_call(partner_kept, pre, turned)
     arrived_kept = to_core(part)
     near, far = first_call(pre, turned, arrived_first)
     near = along_u(near, 1)

time: 107 us -> 105 us (0.981)
  local copies, waits for them, and re-layouts: 2.65 us -> 0.02 us
    unnamed x8, local copies, waits for them, and re-layouts: 2.65 us -> 0.02 us
  transfers between devices with their start and end apart: 21 -> 21, of which waited for: 10 -> 10; matrix products, arithmetic and copies ran while one was open for 0% -> 0% of each run, Pallas kernels for 22% -> 23%
where the time goes in v4:
time: 105 us
  Pallas kernels  32 us (30%)
  waiting for transfers between devices  30.4 us (29%)
  starting transfers between devices  29.3 us (28%)
  blocking collectives  12.1 us (12%)
    pallas_call x11, Pallas kernels, simple_call(): pl.pallas_call(body, in_specs=[whole()] * len(operands), out_specs=[whole...  14.2 us
    ppermute x7, waiting for transfers between devices, along_u(): return lax.ppermute(x, CLIENT, flipped((0, k), (k, 0)))  14 us
    pallas_call x2, Pallas kernels, slope_call(): pl.pallas_call(lambda *refs: slope_body(kept, *refs), grid=(2 * width //...  13.5 us
    all_to_all x1, blocking collectives, exchange(): return lax.all_to_all(x, axes, 0, 0, tiled=True)  12.1 us
    ppermute x7, starting transfers between devices, along_u(): return lax.ppermute(x, CLIENT, flipped((0, k), (k, 0)))  10.7 us
    ppermute x6, waiting for transfers between devices, along_v(): return lax.ppermute(x, CLIENT, flipped((k, 0), (0, k)))  9.22 us
    ppermute x6, starting transfers between devices, along_v(): return lax.ppermute(x, CLIENT, flipped((k, 0), (0, k)))  8.96 us
    ppermute x3, starting transfers between devices, to_head(): return lax.ppermute(x, 'head', [(h, h ^ k) for h in range(4)])  4.77 us
  transfers between devices with their start and end apart: 21, of which 10 were waited for; matrix products, arithmetic and copies ran while one was open for 0% of the time, Pallas kernels for 23%

profile of v4, /device:TPU:0, one launch (start us, length us, event | category | flops | bytes accessed | tf_op | source)
XLA Modules:
  0.0 104.8 jit_solution(9406889455678506788)
XLA Ops:
  0.6 0.0 copy-start
  0.6 3.8 %prepare.1 = (bf16[1280,1024]{1,0:T(8,128)(2,1)S(1)}, bf16[1024,1280]{1,0:T(8,128)(2,1)S(1)}, f32[8,1024]{1,0:T(8,128)S(1)}, bf16[1280,1024]{1,0:T(8,128)(2,1)S(1)}) custom-call(f32[1280,1024]{1,0:T(8,128)} %delta.1, bf16[1280,4096]{1,0:T(8,128)(2,1)} %refs_0_.5), custom_call_target="tpu_custom_call" | custom-call | flops 8000000000 | bytes 20000000 | tf_op jit(solution)/shard_map/prepare/pallas_call | solution.py:93
  4.4 0.0 slice-start
  4.4 3.0 %shard_map.76 = bf16[8,1024,128]{2,1,0:T(8,128)(2,1)S(1)} custom-call(bf16[1280,1024]{1,0:T(8,128)(2,1)S(1)} %get-tuple-element.36.refs_0_, bf16[1024,1280]{1,0:T(8,128)(2,1)S(1)} %get-tuple-element.35.refs_1_.turned), custom_call_target="tpu_custom_call" | custom-call | tf_op jit(solution)/shard_map/pallas_call | solution.py:115
  7.4 0.0 slice-start.1
  7.4 0.1 collective-permute-start.1
  7.5 0.0 copy-done
  7.5 3.0 %shard_map.75 = bf16[8,1024,128]{2,1,0:T(8,128)(2,1)S(1)} custom-call(bf16[1280,4096]{1,0:T(8,128)(2,1)S(1)} %copy-done, bf16[1024,1280]{1,0:T(8,128)(2,1)S(1)} %get-tuple-element.35.refs_1_.turned), custom_call_target="tpu_custom_call" | custom-call | tf_op jit(solution)/shard_map/pallas_call | solution.py:115
  10.5 0.5 collective-permute-start
  11.1 0.0 slice-done
  11.1 0.0 slice-done.1
  11.1 6.7 %slope_sent.1 = bf16[2,96,1024]{2,1,0:T(8,128)(2,1)S(1)} custom-call(bf16[1280,4096]{1,0:T(8,128)(2,1)S(1)} %copy-done, bf16[1280,1024]{1,0:T(8,128)(2,1)S(1)} %get-tuple-element.46.refs_1_, bf16[4096,1024]{1,0:T(8,128)(2,1)S(1)} %bitcast.5), custom_call_target="tpu_custom_call" | custom-call | tf_op jit(solution)/shard_map/slope_sent/pallas_call | solution.py:202
  17.8 1.9 %collective-permute-start.9 = (bf16[2,96,1024]{2,1,0:T(8,128)(2,1)S(1)}, bf16[2,96,1024]{2,1,0:T(8,128)(2,1)S(1)}, u32[]{:S(2)}, u32[]{:S(2)}) collective-permute-start(bf16[2,96,1024]{2,1,0:T(8,128)(2,1)S(1)} %slope_sent.1), channel_id=1, source_target_pairs={{0,1},{1,0},{2,3},{3,2},{4,7},{5,6},{6,5},{7,4},{8,9},{9,8},{10,11... | collective-permute-start | bytes 1179656 | tf_op jit(solution)/shard_map/ppermute | solution.py:436
  19.7 0.0 collective-permute-done.1.arrived
  19.7 3.0 %shard_map.77 = (bf16[4,1024,128]{2,1,0:T(8,128)(2,1)S(1)}, bf16[4,1024,128]{2,1,0:T(8,128)(2,1)S(1)}) custom-call(bf16[1280,4096]{1,0:T(8,128)(2,1)S(1)} %copy-done, bf16[1024,1280]{1,0:T(8,128)(2,1)S(1)} %get-tuple-element.35.refs_1_.turned, bf16[8,1024,128]{2,1,0:T(8,128)(2,1)S(1)} %collective-permute-done.1.arrived), custom_call_target="tpu_custom_call" | custom-call | tf_op jit(solution)/shard_map/pallas_call | solution.py:115
  22.8 1.6 %collective-permute-start.2 = (bf16[4,1024,128]{2,1,0:T(8,128)(2,1)S(1)}, bf16[4,1024,128]{2,1,0:T(8,128)(2,1)S(1)}, u32[]{:S(2)}, u32[]{:S(2)}) collective-permute-start(bf16[4,1024,128]{2,1,0:T(8,128)(2,1)S(1)} %get-tuple-element.37), channel_id=1, source_target_pairs={{0,8},{4,36},{8,0},{12,44},{16,24},{20,52},{24,16},{28,60},{32,40}... | collective-permute-start | bytes 3145736 | tf_op jit(solution)/shard_map/ppermute | solution.py:422
  24.4 2.1 %collective-permute-start.3 = (bf16[4,1024,128]{2,1,0:T(8,128)(2,1)S(1)}, bf16[4,1024,128]{2,1,0:T(8,128)(2,1)S(1)}, u32[]{:S(2)}, u32[]{:S(2)}) collective-permute-start(bf16[4,1024,128]{2,1,0:T(8,128)(2,1)S(1)} %get-tuple-element.38), channel_id=1, source_target_pairs={{0,24},{4,100},{8,16},{12,108},{16,8},{20,116},{24,0},{28,124},{32... | collective-permute-start | bytes 3145736 | tf_op jit(solution)/shard_map/ppermute | solution.py:422
  26.4 6.7 %slope_kept.1.kept = f32[2,96,1024]{2,1,0:T(8,128)S(1)} custom-call(bf16[1280,4096]{1,0:T(8,128)(2,1)S(1)} %copy-done, bf16[1280,1024]{1,0:T(8,128)(2,1)S(1)} %get-tuple-element.46.refs_1_, bf16[4096,1024]{1,0:T(8,128)(2,1)S(1)} %bitcast.5), custom_call_target="tpu_custom_call" | custom-call | tf_op jit(solution)/shard_map/slope_kept/pallas_call | solution.py:202
  33.2 0.0 collective-permute-done.9.got
  33.3 2.3 %collective-permute-start.10 = (bf16[96,1024]{1,0:T(8,128)(2,1)S(1)}, bf16[96,1024]{1,0:T(8,128)(2,1)S(1)}, u32[]{:S(2)}, u32[]{:S(2)}) collective-permute-start(bf16[96,1024]{1,0:T(8,128)(2,1)S(1)} %fusion.1), channel_id=1, source_target_pairs={{0,3},{1,2},{2,1},{3,0},{4,5},{5,4},{6,7},{7,6},{8,11},{9,10},{10,... | collective-permute-start | bytes 589832 | tf_op jit(solution)/shard_map/ppermute | solution.py:436
  35.5 4.7 %collective-permute-done.10.got_two = bf16[96,1024]{1,0:T(8,128)(2,1)S(1)} collective-permute-done((bf16[96,1024]{1,0:T(8,128)(2,1)S(1)}, bf16[96,1024]{1,0:T(8,128)(2,1)S(1)}, u32[]{:S(2)}, u32[]{:S(2)}) %collective-permute-start.10) | collective-permute-done | bytes 196640 | tf_op jit(solution)/shard_map/ppermute | solution.py:436
  40.2 0.0 copy-done.1
  40.2 0.6 small_sends.1
  40.8 0.1 collective-permute-start.11
  40.9 0.0 collective-permute-done.arrived
  40.9 0.0 collective-permute-done.2.near
  40.9 0.0 collective-permute-done.3.far
  41.0 3.2 %shard_map.78 = (bf16[2,1024,128]{2,1,0:T(8,128)(2,1)S(1)}, bf16[2,1024,128]{2,1,0:T(8,128)(2,1)S(1)}, f32[4,1024,128]{2,1,0:T(8,128)S(1)}) custom-call(bf16[1280,4096]{1,0:T(8,128)(2,1)S(1)} %copy-done, bf16[1024,1280]{1,0:T(8,128)(2,1)S(1)} %get-tuple-element.35.refs_1_.turned, bf16[8,1024,128]{2,1,0:T(8,128)(2,1)S(1)} %collective-permute-done.arrived, ...), custom_call_target="tpu_custom_call" | custom-call | tf_op jit(solution)/shard_map/pallas_call | solution.py:115
  44.1 2.3 %collective-permute-start.4 = (bf16[2,1024,128]{2,1,0:T(8,128)(2,1)S(1)}, bf16[2,1024,128]{2,1,0:T(8,128)(2,1)S(1)}, u32[]{:S(2)}, u32[]{:S(2)}) collective-permute-start(bf16[2,1024,128]{2,1,0:T(8,128)(2,1)S(1)} %get-tuple-element.40), channel_id=1, source_target_pairs={{0,24},{4,100},{8,16},{12,108},{16,8},{20,116},{24,0},{28,124},{32... | collective-permute-start | bytes 1572872 | tf_op jit(solution)/shard_map/ppermute | solution.py:422
  46.4 0.0 collective-permute-start.5
  46.4 0.0 collective-permute-done.11.arrived
  46.5 0.1 shard_map.80
  46.6 1.3 %collective-permute-start.12 = (bf16[4,19,8,128]{3,2,1,0:T(8,128)(2,1)S(1)}, bf16[4,19,8,128]{3,2,1,0:T(8,128)(2,1)S(1)}, u32[]{:S(2)}, u32[]{:S(2)}) collective-permute-start(bf16[4,19,8,128]{3,2,1,0:T(8,128)(2,1)S(1)} %get-tuple-element.51), channel_id=1, source_target_pairs={{0,32},{4,12},{8,40},{12,4},{16,48},{20,28},{24,56},{28,20},{32,0}... | collective-permute-start | bytes 466952 | tf_op jit(solution)/shard_map/ppermute | solution.py:426
  47.9 6.7 %collective-permute-done.4.got_a = bf16[2,1024,128]{2,1,0:T(8,128)(2,1)S(1)} collective-permute-done((bf16[2,1024,128]{2,1,0:T(8,128)(2,1)S(1)}, bf16[2,1024,128]{2,1,0:T(8,128)(2,1)S(1)}, u32[]{:S(2)}, u32[]{:S(2)}) %collective-permute-start.4) | collective-permute-done | bytes 524320 | tf_op jit(solution)/shard_map/ppermute | solution.py:422
  54.6 2.7 %collective-permute-done.5.got_b = bf16[2,1024,128]{2,1,0:T(8,128)(2,1)S(1)} collective-permute-done((bf16[2,1024,128]{2,1,0:T(8,128)(2,1)S(1)}, bf16[2,1024,128]{2,1,0:T(8,128)(2,1)S(1)}, u32[]{:S(2)}, u32[]{:S(2)}) %collective-permute-start.5) | collective-permute-done | bytes 524320 | tf_op jit(solution)/shard_map/ppermute | solution.py:422
  57.3 0.2 shard_map.79
  57.5 1.5 %collective-permute-start.6 = (bf16[1024,128]{1,0:T(8,128)(2,1)S(1)}, bf16[1024,128]{1,0:T(8,128)(2,1)S(1)}, u32[]{:S(2)}, u32[]{:S(2)}) collective-permute-start(bf16[1024,128]{1,0:T(8,128)(2,1)S(1)} %get-tuple-element.43), channel_id=1, source_target_pairs={{0,32},{4,12},{8,40},{12,4},{16,48},{20,28},{24,56},{28,20},{32,0}... | collective-permute-start | bytes 786440 | tf_op jit(solution)/shard_map/ppermute | solution.py:426
  59.0 2.1 %collective-permute-start.7 = (bf16[1024,128]{1,0:T(8,128)(2,1)S(1)}, bf16[1024,128]{1,0:T(8,128)(2,1)S(1)}, u32[]{:S(2)}, u32[]{:S(2)}) collective-permute-start(bf16[1024,128]{1,0:T(8,128)(2,1)S(1)} %get-tuple-element.44), channel_id=1, source_target_pairs={{0,64},{4,20},{8,72},{12,28},{16,80},{20,4},{24,88},{28,12},{32,96... | collective-permute-start | bytes 786440 | tf_op jit(solution)/shard_map/ppermute | solution.py:426
  61.0 1.4 %collective-permute-start.8 = (bf16[1024,128]{1,0:T(8,128)(2,1)S(1)}, bf16[1024,128]{1,0:T(8,128)(2,1)S(1)}, u32[]{:S(2)}, u32[]{:S(2)}) collective-permute-start(bf16[1024,128]{1,0:T(8,128)(2,1)S(1)} %get-tuple-element.45), channel_id=1, source_target_pairs={{0,96},{4,28},{8,104},{12,20},{16,112},{20,12},{24,120},{28,4},{32... | collective-permute-start | bytes 786440 | tf_op jit(solution)/shard_map/ppermute | solution.py:426
  62.5 1.6 %collective-permute-start.13 = (bf16[4,19,8,128]{3,2,1,0:T(8,128)(2,1)S(1)}, bf16[4,19,8,128]{3,2,1,0:T(8,128)(2,1)S(1)}, u32[]{:S(2)}, u32[]{:S(2)}) collective-permute-start(bf16[4,19,8,128]{3,2,1,0:T(8,128)(2,1)S(1)} %get-tuple-element.52), channel_id=1, source_target_pairs={{0,64},{4,20},{8,72},{12,28},{16,80},{20,4},{24,88},{28,12},{32,96... | collective-permute-start | bytes 466952 | tf_op jit(solution)/shard_map/ppermute | solution.py:426
  64.1 0.0 collective-permute-done.12.side_one
  64.1 1.0 collective-permute-start.14
  65.1 4.8 %collective-permute-done.13.side_two = bf16[4,19,8,128]{3,2,1,0:T(8,128)(2,1)S(1)} collective-permute-done((bf16[4,19,8,128]{3,2,1,0:T(8,128)(2,1)S(1)}, bf16[4,19,8,128]{3,2,1,0:T(8,128)(2,1)S(1)}, u32[]{:S(2)}, u32[]{:S(2)}) %collective-permute-start.13) | collective-permute-done | bytes 155680 | tf_op jit(solution)/shard_map/ppermute | solution.py:426
  70.0 4.4 %collective-permute-done.14.side_three = bf16[4,19,8,128]{3,2,1,0:T(8,128)(2,1)S(1)} collective-permute-done((bf16[4,19,8,128]{3,2,1,0:T(8,128)(2,1)S(1)}, bf16[4,19,8,128]{3,2,1,0:T(8,128)(2,1)S(1)}, u32[]{:S(2)}, u32[]{:S(2)}) %collective-permute-start.14) | collective-permute-done | bytes 155680 | tf_op jit(solution)/shard_map/ppermute | solution.py:426
  74.3 0.1 shard_map.81
  74.4 0.6 collective-permute-start.15
  75.0 2.5 %collective-permute-start.16 = (bf16[19,8,128]{2,1,0:T(8,128)(2,1)S(1)}, bf16[19,8,128]{2,1,0:T(8,128)(2,1)S(1)}, u32[]{:S(2)}, u32[]{:S(2)}) collective-permute-start(bf16[19,8,128]{2,1,0:T(8,128)(2,1)S(1)} %get-tuple-element.56), channel_id=1, source_target_pairs={{0,16},{4,68},{8,24},{12,76},{16,0},{20,84},{24,8},{28,92},{32,48}... | collective-permute-start | bytes 116744 | tf_op jit(solution)/shard_map/ppermute | solution.py:422
  77.5 0.9 collective-permute-done.15.s_one
  78.5 1.6 %collective-permute-start.17 = (bf16[19,8,128]{2,1,0:T(8,128)(2,1)S(1)}, bf16[19,8,128]{2,1,0:T(8,128)(2,1)S(1)}, u32[]{:S(2)}, u32[]{:S(2)}) collective-permute-start(bf16[19,8,128]{2,1,0:T(8,128)(2,1)S(1)} %get-tuple-element.57), channel_id=1, source_target_pairs={{0,24},{4,100},{8,16},{12,108},{16,8},{20,116},{24,0},{28,124},{32... | collective-permute-start | bytes 116744 | tf_op jit(solution)/shard_map/ppermute | solution.py:422
  80.1 0.5 collective-permute-done.16.s_two
  80.5 3.1 %collective-permute-done.17.s_three = bf16[19,8,128]{2,1,0:T(8,128)(2,1)S(1)} collective-permute-done((bf16[19,8,128]{2,1,0:T(8,128)(2,1)S(1)}, bf16[19,8,128]{2,1,0:T(8,128)(2,1)S(1)}, u32[]{:S(2)}, u32[]{:S(2)}) %collective-permute-start.17) | collective-permute-done | bytes 38944 | tf_op jit(solution)/shard_map/ppermute | solution.py:422
  83.7 0.0 collective-permute-done.6.one
  83.7 0.0 collective-permute-done.7.two
  83.7 0.0 collective-permute-done.8.three
  83.7 0.4 shard_map.82
  84.1 12.1 %all_to_all.5.arrived.refs_6_ = bf16[32,4,8,128]{3,2,1,0:T(8,128)(2,1)S(1)} all-to-all(bf16[32,4,8,128]{3,2,1,0:T(8,128)(2,1)S(1)} %get-tuple-element.59), channel_id=1, replica_groups=mesh['client_0'=4,'client_1'=4,'client_2'=2,'head'=4] {'client_0','clien..., dimensions={0} | all-to-all | bytes 524288 | tf_op jit(solution)/shard_map/all_to_all | solution.py:452
  96.3 2.3 %collective-permute-start.20 = (f32[1,128]{1,0:T(1,128)S(1)}, f32[1,128]{1,0:T(1,128)S(1)}, u32[]{:S(2)}, u32[]{:S(2)}) collective-permute-start(f32[1,128]{1,0:T(1,128)S(1)} %shard_map.83.refs_0_), channel_id=1, source_target_pairs={{0,3},{1,2},{2,1},{3,0},{4,7},{5,6},{6,5},{7,4},{8,11},{9,10},{10,... | collective-permute-start | bytes 1544 | tf_op jit(solution)/shard_map/ppermute | solution.py:448
  98.5 0.1 collective-permute-start.19
  98.7 2.4 %collective-permute-start.18 = (f32[1,128]{1,0:T(1,128)S(1)}, f32[1,128]{1,0:T(1,128)S(1)}, u32[]{:S(2)}, u32[]{:S(2)}) collective-permute-start(f32[1,128]{1,0:T(1,128)S(1)} %shard_map.83.refs_0_), channel_id=1, source_target_pairs={{0,2},{1,3},{2,0},{3,1},{4,6},{5,7},{6,4},{7,5},{8,10},{9,11},{10,... | collective-permute-start | bytes 1544 | tf_op jit(solution)/shard_map/ppermute | solution.py:448
  101.0 0.2 shard_map.84.refs_4_
  101.2 0.0 collective-permute-done.20.refs_3_
  101.2 0.8 collective-permute-done.19.refs_2_
  102.1 1.6 %collective-permute-done.18.refs_1_ = f32[1,128]{1,0:T(1,128)S(1)} collective-permute-done((f32[1,128]{1,0:T(1,128)S(1)}, f32[1,128]{1,0:T(1,128)S(1)}, u32[]{:S(2)}, u32[]{:S(2)}) %collective-permute-start.18) | collective-permute-done | bytes 544 | tf_op jit(solution)/shard_map/ppermute | solution.py:448
  103.7 1.0 shard_map.85
  (4 shorter events, 0.1 us)
Async XLA Ops:
  0.6 6.9 %copy-start = (bf16[1280,4096]{1,0:T(8,128)(2,1)S(1)}, bf16[1280,4096]{1,0:T(8,128)(2,1)}, u32[]{:S(2)}) copy-start(bf16[1280,4096]{1,0:T(8,128)(2,1)} %refs_0_.5) | copy-start | bytes 31457284
  4.4 6.7 %slice-start = ((s8[8388608]{0:T(1024)(128)(4,1)}), s8[4194304]{0:T(1024)(128)(4,1)S(1)}, s32[]{:S(2)}) async-start(s8[8388608]{0:T(1024)(128)(4,1)} %bitcast.4), calls=%async_computation.1 | async-start | bytes 8388608
  7.4 3.7 %slice-start.1 = ((s8[8388608]{0:T(1024)(128)(4,1)}), s8[4194304]{0:T(1024)(128)(4,1)S(1)}, s32[]{:S(2)}) async-start(s8[8388608]{0:T(1024)(128)(4,1)} %bitcast.4), calls=%async_computation.2 | async-start | bytes 8388608
  7.4 12.3 %collective-permute-start.1 = (bf16[8,1024,128]{2,1,0:T(8,128)(2,1)S(1)}, bf16[8,1024,128]{2,1,0:T(8,128)(2,1)S(1)}, u32[]{:S(2)}, u32[]{:S(2)}) collective-permute-start(bf16[8,1024,128]{2,1,0:T(8,128)(2,1)S(1)} %shard_map.76), channel_id=1, source_target_pairs={{0,4},{4,0},{1,5},{5,1},{2,6},{6,2},{3,7},{7,3},{8,12},{12,8},{9,1... | collective-permute-start | bytes 6291464 | tf_op jit(solution)/shard_map/ppermute | solution.py:430
  10.5 30.4 %collective-permute-start = (bf16[8,1024,128]{2,1,0:T(8,128)(2,1)S(1)}, bf16[8,1024,128]{2,1,0:T(8,128)(2,1)S(1)}, u32[]{:S(2)}, u32[]{:S(2)}) collective-permute-start(bf16[8,1024,128]{2,1,0:T(8,128)(2,1)S(1)} %shard_map.75), channel_id=1, source_target_pairs={{0,4},{4,0},{1,5},{5,1},{2,6},{6,2},{3,7},{7,3},{8,12},{12,8},{9,1... | collective-permute-start | bytes 6291464 | tf_op jit(solution)/shard_map/ppermute | solution.py:430
  17.8 15.4 %collective-permute-start.9 = (bf16[2,96,1024]{2,1,0:T(8,128)(2,1)S(1)}, bf16[2,96,1024]{2,1,0:T(8,128)(2,1)S(1)}, u32[]{:S(2)}, u32[]{:S(2)}) collective-permute-start(bf16[2,96,1024]{2,1,0:T(8,128)(2,1)S(1)} %slope_sent.1), channel_id=1, source_target_pairs={{0,1},{1,0},{2,3},{3,2},{4,7},{5,6},{6,5},{7,4},{8,9},{9,8},{10,11... | collective-permute-start | bytes 1179656 | tf_op jit(solution)/shard_map/ppermute | solution.py:436
  22.8 18.2 %collective-permute-start.2 = (bf16[4,1024,128]{2,1,0:T(8,128)(2,1)S(1)}, bf16[4,1024,128]{2,1,0:T(8,128)(2,1)S(1)}, u32[]{:S(2)}, u32[]{:S(2)}) collective-permute-start(bf16[4,1024,128]{2,1,0:T(8,128)(2,1)S(1)} %get-tuple-element.37), channel_id=1, source_target_pairs={{0,8},{4,36},{8,0},{12,44},{16,24},{20,52},{24,16},{28,60},{32,40}... | collective-permute-start | bytes 3145736 | tf_op jit(solution)/shard_map/ppermute | solution.py:422
  24.3 15.9 %copy-start.1 = (s32[16]{0:T(128)S(1)}, s32[16]{0:T(128)}, u32[]{:S(2)}) copy-start(s32[16]{0:T(128)} %param.7) | copy-start | bytes 196
  24.4 16.6 %collective-permute-start.3 = (bf16[4,1024,128]{2,1,0:T(8,128)(2,1)S(1)}, bf16[4,1024,128]{2,1,0:T(8,128)(2,1)S(1)}, u32[]{:S(2)}, u32[]{:S(2)}) collective-permute-start(bf16[4,1024,128]{2,1,0:T(8,128)(2,1)S(1)} %get-tuple-element.38), channel_id=1, source_target_pairs={{0,24},{4,100},{8,16},{12,108},{16,8},{20,116},{24,0},{28,124},{32... | collective-permute-start | bytes 3145736 | tf_op jit(solution)/shard_map/ppermute | solution.py:422
  33.3 7.0 %collective-permute-start.10 = (bf16[96,1024]{1,0:T(8,128)(2,1)S(1)}, bf16[96,1024]{1,0:T(8,128)(2,1)S(1)}, u32[]{:S(2)}, u32[]{:S(2)}) collective-permute-start(bf16[96,1024]{1,0:T(8,128)(2,1)S(1)} %fusion.1), channel_id=1, source_target_pairs={{0,3},{1,2},{2,1},{3,0},{4,5},{5,4},{6,7},{7,6},{8,11},{9,10},{10,... | collective-permute-start | bytes 589832 | tf_op jit(solution)/shard_map/ppermute | solution.py:436
  40.8 5.6 %collective-permute-start.11 = (bf16[16,19,8,128]{3,2,1,0:T(8,128)(2,1)S(1)}, bf16[16,19,8,128]{3,2,1,0:T(8,128)(2,1)S(1)}, u32[]{:S(2)}, u32[]{:S(2)}) collective-permute-start(bf16[16,19,8,128]{3,2,1,0:T(8,128)(2,1)S(1)} %get-tuple-element.49), channel_id=1, source_target_pairs={{0,4},{4,0},{1,5},{5,1},{2,6},{6,2},{3,7},{7,3},{8,12},{12,8},{9,1... | collective-permute-start | bytes 1867784 | tf_op jit(solution)/shard_map/ppermute | solution.py:430
  44.1 10.5 %collective-permute-start.4 = (bf16[2,1024,128]{2,1,0:T(8,128)(2,1)S(1)}, bf16[2,1024,128]{2,1,0:T(8,128)(2,1)S(1)}, u32[]{:S(2)}, u32[]{:S(2)}) collective-permute-start(bf16[2,1024,128]{2,1,0:T(8,128)(2,1)S(1)} %get-tuple-element.40), channel_id=1, source_target_pairs={{0,24},{4,100},{8,16},{12,108},{16,8},{20,116},{24,0},{28,124},{32... | collective-permute-start | bytes 1572872 | tf_op jit(solution)/shard_map/ppermute | solution.py:422
  46.4 10.8 %collective-permute-start.5 = (bf16[2,1024,128]{2,1,0:T(8,128)(2,1)S(1)}, bf16[2,1024,128]{2,1,0:T(8,128)(2,1)S(1)}, u32[]{:S(2)}, u32[]{:S(2)}) collective-permute-start(bf16[2,1024,128]{2,1,0:T(8,128)(2,1)S(1)} %get-tuple-element.41), channel_id=1, source_target_pairs={{0,8},{4,36},{8,0},{12,44},{16,24},{20,52},{24,16},{28,60},{32,40}... | collective-permute-start | bytes 1572872 | tf_op jit(solution)/shard_map/ppermute | solution.py:422
  46.6 17.5 %collective-permute-start.12 = (bf16[4,19,8,128]{3,2,1,0:T(8,128)(2,1)S(1)}, bf16[4,19,8,128]{3,2,1,0:T(8,128)(2,1)S(1)}, u32[]{:S(2)}, u32[]{:S(2)}) collective-permute-start(bf16[4,19,8,128]{3,2,1,0:T(8,128)(2,1)S(1)} %get-tuple-element.51), channel_id=1, source_target_pairs={{0,32},{4,12},{8,40},{12,4},{16,48},{20,28},{24,56},{28,20},{32,0}... | collective-permute-start | bytes 466952 | tf_op jit(solution)/shard_map/ppermute | solution.py:426
  57.5 26.2 %collective-permute-start.6 = (bf16[1024,128]{1,0:T(8,128)(2,1)S(1)}, bf16[1024,128]{1,0:T(8,128)(2,1)S(1)}, u32[]{:S(2)}, u32[]{:S(2)}) collective-permute-start(bf16[1024,128]{1,0:T(8,128)(2,1)S(1)} %get-tuple-element.43), channel_id=1, source_target_pairs={{0,32},{4,12},{8,40},{12,4},{16,48},{20,28},{24,56},{28,20},{32,0}... | collective-permute-start | bytes 786440 | tf_op jit(solution)/shard_map/ppermute | solution.py:426
  59.0 24.7 %collective-permute-start.7 = (bf16[1024,128]{1,0:T(8,128)(2,1)S(1)}, bf16[1024,128]{1,0:T(8,128)(2,1)S(1)}, u32[]{:S(2)}, u32[]{:S(2)}) collective-permute-start(bf16[1024,128]{1,0:T(8,128)(2,1)S(1)} %get-tuple-element.44), channel_id=1, source_target_pairs={{0,64},{4,20},{8,72},{12,28},{16,80},{20,4},{24,88},{28,12},{32,96... | collective-permute-start | bytes 786440 | tf_op jit(solution)/shard_map/ppermute | solution.py:426
  61.0 22.6 %collective-permute-start.8 = (bf16[1024,128]{1,0:T(8,128)(2,1)S(1)}, bf16[1024,128]{1,0:T(8,128)(2,1)S(1)}, u32[]{:S(2)}, u32[]{:S(2)}) collective-permute-start(bf16[1024,128]{1,0:T(8,128)(2,1)S(1)} %get-tuple-element.45), channel_id=1, source_target_pairs={{0,96},{4,28},{8,104},{12,20},{16,112},{20,12},{24,120},{28,4},{32... | collective-permute-start | bytes 786440 | tf_op jit(solution)/shard_map/ppermute | solution.py:426
  62.5 7.5 %collective-permute-start.13 = (bf16[4,19,8,128]{3,2,1,0:T(8,128)(2,1)S(1)}, bf16[4,19,8,128]{3,2,1,0:T(8,128)(2,1)S(1)}, u32[]{:S(2)}, u32[]{:S(2)}) collective-permute-start(bf16[4,19,8,128]{3,2,1,0:T(8,128)(2,1)S(1)} %get-tuple-element.52), channel_id=1, source_target_pairs={{0,64},{4,20},{8,72},{12,28},{16,80},{20,4},{24,88},{28,12},{32,96... | collective-permute-start | bytes 466952 | tf_op jit(solution)/shard_map/ppermute | solution.py:426
  64.1 10.3 %collective-permute-start.14 = (bf16[4,19,8,128]{3,2,1,0:T(8,128)(2,1)S(1)}, bf16[4,19,8,128]{3,2,1,0:T(8,128)(2,1)S(1)}, u32[]{:S(2)}, u32[]{:S(2)}) collective-permute-start(bf16[4,19,8,128]{3,2,1,0:T(8,128)(2,1)S(1)} %get-tuple-element.53), channel_id=1, source_target_pairs={{0,96},{4,28},{8,104},{12,20},{16,112},{20,12},{24,120},{28,4},{32... | collective-permute-start | bytes 466952 | tf_op jit(solution)/shard_map/ppermute | solution.py:426
  74.4 4.1 %collective-permute-start.15 = (bf16[19,8,128]{2,1,0:T(8,128)(2,1)S(1)}, bf16[19,8,128]{2,1,0:T(8,128)(2,1)S(1)}, u32[]{:S(2)}, u32[]{:S(2)}) collective-permute-start(bf16[19,8,128]{2,1,0:T(8,128)(2,1)S(1)} %get-tuple-element.55), channel_id=1, source_target_pairs={{0,8},{4,36},{8,0},{12,44},{16,24},{20,52},{24,16},{28,60},{32,40}... | collective-permute-start | bytes 116744 | tf_op jit(solution)/shard_map/ppermute | solution.py:422
  75.0 5.5 %collective-permute-start.16 = (bf16[19,8,128]{2,1,0:T(8,128)(2,1)S(1)}, bf16[19,8,128]{2,1,0:T(8,128)(2,1)S(1)}, u32[]{:S(2)}, u32[]{:S(2)}) collective-permute-start(bf16[19,8,128]{2,1,0:T(8,128)(2,1)S(1)} %get-tuple-element.56), channel_id=1, source_target_pairs={{0,16},{4,68},{8,24},{12,76},{16,0},{20,84},{24,8},{28,92},{32,48}... | collective-permute-start | bytes 116744 | tf_op jit(solution)/shard_map/ppermute | solution.py:422
  78.5 5.2 %collective-permute-start.17 = (bf16[19,8,128]{2,1,0:T(8,128)(2,1)S(1)}, bf16[19,8,128]{2,1,0:T(8,128)(2,1)S(1)}, u32[]{:S(2)}, u32[]{:S(2)}) collective-permute-start(bf16[19,8,128]{2,1,0:T(8,128)(2,1)S(1)} %get-tuple-element.57), channel_id=1, source_target_pairs={{0,24},{4,100},{8,16},{12,108},{16,8},{20,116},{24,0},{28,124},{32... | collective-permute-start | bytes 116744 | tf_op jit(solution)/shard_map/ppermute | solution.py:422
  96.3 5.0 %collective-permute-start.20 = (f32[1,128]{1,0:T(1,128)S(1)}, f32[1,128]{1,0:T(1,128)S(1)}, u32[]{:S(2)}, u32[]{:S(2)}) collective-permute-start(f32[1,128]{1,0:T(1,128)S(1)} %shard_map.83.refs_0_), channel_id=1, source_target_pairs={{0,3},{1,2},{2,1},{3,0},{4,7},{5,6},{6,5},{7,4},{8,11},{9,10},{10,... | collective-permute-start | bytes 1544 | tf_op jit(solution)/shard_map/ppermute | solution.py:448
  98.5 3.6 %collective-permute-start.19 = (f32[1,128]{1,0:T(1,128)S(1)}, f32[1,128]{1,0:T(1,128)S(1)}, u32[]{:S(2)}, u32[]{:S(2)}) collective-permute-start(f32[1,128]{1,0:T(1,128)S(1)} %shard_map.83.refs_0_), channel_id=1, source_target_pairs={{0,1},{1,0},{2,3},{3,2},{4,5},{5,4},{6,7},{7,6},{8,9},{9,8},{10,11... | collective-permute-start | bytes 1544 | tf_op jit(solution)/shard_map/ppermute | solution.py:448
  98.7 5.1 %collective-permute-start.18 = (f32[1,128]{1,0:T(1,128)S(1)}, f32[1,128]{1,0:T(1,128)S(1)}, u32[]{:S(2)}, u32[]{:S(2)}) collective-permute-start(f32[1,128]{1,0:T(1,128)S(1)} %shard_map.83.refs_0_), channel_id=1, source_target_pairs={{0,2},{1,3},{2,0},{3,1},{4,6},{5,7},{6,4},{7,5},{8,10},{9,11},{10,... | collective-permute-start | bytes 1544 | tf_op jit(solution)/shard_map/ppermute | solution.py:448

commit v5 on v4

--- a/solution.py
+++ b/solution.py
@@ -29,7 +29,7 @@
     return pl.BlockSpec(memory_space=pltpu.VMEM)
 
 
-PARTS = 5
+PARTS = 10
 STEP = 4
 TILE = 1024
 CHUNK = 320
@@ -374,7 +374,7 @@
     return simple_call(subtotal_body, (arrived,), [shape])[0]
 
 
-def scale_body(counts, mine, two, one, three, head, embed, shares, head_grad, bias_grad, embed_grad, span_grad):
+def scale_body(counts, mine, one, two, three, head, embed, shares, head_grad, bias_grad, embed_grad, span_grad):
     f32 = jnp.float32
     totals = (mine[...] + two[...]) + (one[...] + three[...])
 
@@ -446,6 +446,13 @@
 
 def to_head(x, k):
     return lax.ppermute(x, "head", [(h, h ^ k) for h in range(4)])
+
+
+def around(move, one, two, three):
+    two = move(two, 2)
+    one = move(one, 1)
+    three = move(three, 3)
+    return one, two, three
 
 
 def exchange(x, axes):
@@ -479,16 +486,16 @@
     small_send, small_keep, embed_square = small_sends(kept, got, got_two, client_ids[None, :], bias_part, share)
     small_got = to_core(small_send)
     own, one, two, three = core_sum(small_keep, small_got)
-    small_arrived = along_v(one, 1), along_v(two, 2), along_v(three, 3)
+    small_arrived = around(along_v, one, two, three)
     final, one, two, three = join(keep, got_a, got_b)
-    arrived = along_v(one, 1), along_v(two, 2), along_v(three, 3)
+    arrived = around(along_v, one, two, three)
     small, one, two, three = line_sum(own, small_arrived)
-    small_arrived = along_u(one, 1), along_u(two, 2), along_u(three, 3)
+    small_arrived = around(along_u, one, two, three)
     total, embed_raw, message = close(final, arrived, small, small_arrived, embed_square, peers, share)
     shares = exchange(message, CLIENT)
     head_raw = turn(total)
     squares = subtotal(shares)
-    squares = (squares, *(to_head(squares, k) for k in (2, 1, 3)))
+    squares = (squares, *around(to_head, squares, squares, squares))
     emit_total = emit_here * head_devices
     counts = (
         float(hidden_width * emit_total),

time: 105 us -> 105 us (level)
  no operation moved by 1% of the time
where the time goes in v5:
time: 105 us
  Pallas kernels  31.9 us (30%)
  waiting for transfers between devices  30.9 us (29%)
  starting transfers between devices  28.7 us (27%)
  blocking collectives  12.1 us (12%)
    pallas_call x11, Pallas kernels, simple_call(): pl.pallas_call(body, in_specs=[whole()] * len(operands), out_specs=[whole...  14.2 us
    ppermute x7, waiting for transfers between devices, along_u(): return lax.ppermute(x, CLIENT, flipped((0, k), (k, 0)))  13.9 us
    pallas_call x2, Pallas kernels, slope_call(): pl.pallas_call(lambda *refs: slope_body(kept, *refs), grid=(2 * width //...  13.4 us
    all_to_all x1, blocking collectives, exchange(): return lax.all_to_all(x, axes, 0, 0, tiled=True)  12.1 us
    ppermute x7, starting transfers between devices, along_u(): return lax.ppermute(x, CLIENT, flipped((0, k), (k, 0)))  10.7 us
    ppermute x6, waiting for transfers between devices, along_v(): return lax.ppermute(x, CLIENT, flipped((k, 0), (0, k)))  9.24 us
    ppermute x6, starting transfers between devices, along_v(): return lax.ppermute(x, CLIENT, flipped((k, 0), (0, k)))  8.98 us
    ppermute x2, waiting for transfers between devices, along_head(): return lax.ppermute(x, axes, pairs)  4.7 us
  transfers between devices with their start and end apart: 21, of which 10 were waited for; matrix products, arithmetic and copies ran while one was open for 0% of the time, Pallas kernels for 23%

profile of v5, /device:TPU:0, one launch (start us, length us, event | category | flops | bytes accessed | tf_op | source)
XLA Modules:
  0.0 104.5 jit_solution(11861581084679803017)
XLA Ops:
  0.6 0.0 copy-start
  0.6 3.7 %prepare.1 = (bf16[1280,1024]{1,0:T(8,128)(2,1)S(1)}, bf16[1024,1280]{1,0:T(8,128)(2,1)S(1)}, f32[8,1024]{1,0:T(8,128)S(1)}, bf16[1280,1024]{1,0:T(8,128)(2,1)S(1)}) custom-call(f32[1280,1024]{1,0:T(8,128)} %delta.1, bf16[1280,4096]{1,0:T(8,128)(2,1)} %refs_0_.5), custom_call_target="tpu_custom_call" | custom-call | flops 8000000000 | bytes 20000000 | tf_op jit(solution)/shard_map/prepare/pallas_call | solution.py:93
  4.3 0.0 slice-start
  4.3 3.0 %shard_map.76 = bf16[8,1024,128]{2,1,0:T(8,128)(2,1)S(1)} custom-call(bf16[1280,1024]{1,0:T(8,128)(2,1)S(1)} %get-tuple-element.36.refs_0_, bf16[1024,1280]{1,0:T(8,128)(2,1)S(1)} %get-tuple-element.35.refs_1_.turned), custom_call_target="tpu_custom_call" | custom-call | tf_op jit(solution)/shard_map/pallas_call | solution.py:115
  7.3 0.0 slice-start.1
  7.3 0.1 collective-permute-start.1
  7.4 0.0 copy-done
  7.4 3.0 %shard_map.75 = bf16[8,1024,128]{2,1,0:T(8,128)(2,1)S(1)} custom-call(bf16[1280,4096]{1,0:T(8,128)(2,1)S(1)} %copy-done, bf16[1024,1280]{1,0:T(8,128)(2,1)S(1)} %get-tuple-element.35.refs_1_.turned), custom_call_target="tpu_custom_call" | custom-call | tf_op jit(solution)/shard_map/pallas_call | solution.py:115
  10.4 0.5 collective-permute-start
  10.9 0.0 slice-done
  11.0 0.0 slice-done.1
  11.0 6.7 %slope_sent.1 = bf16[2,96,1024]{2,1,0:T(8,128)(2,1)S(1)} custom-call(bf16[1280,4096]{1,0:T(8,128)(2,1)S(1)} %copy-done, bf16[1280,1024]{1,0:T(8,128)(2,1)S(1)} %get-tuple-element.46.refs_1_, bf16[4096,1024]{1,0:T(8,128)(2,1)S(1)} %bitcast.5), custom_call_target="tpu_custom_call" | custom-call | tf_op jit(solution)/shard_map/slope_sent/pallas_call | solution.py:202
  17.7 2.0 %collective-permute-start.9 = (bf16[2,96,1024]{2,1,0:T(8,128)(2,1)S(1)}, bf16[2,96,1024]{2,1,0:T(8,128)(2,1)S(1)}, u32[]{:S(2)}, u32[]{:S(2)}) collective-permute-start(bf16[2,96,1024]{2,1,0:T(8,128)(2,1)S(1)} %slope_sent.1), channel_id=1, source_target_pairs={{0,1},{1,0},{2,3},{3,2},{4,7},{5,6},{6,5},{7,4},{8,9},{9,8},{10,11... | collective-permute-start | bytes 1179656 | tf_op jit(solution)/shard_map/ppermute | solution.py:436
  19.6 0.0 collective-permute-done.1.arrived
  19.6 3.0 %shard_map.77 = (bf16[4,1024,128]{2,1,0:T(8,128)(2,1)S(1)}, bf16[4,1024,128]{2,1,0:T(8,128)(2,1)S(1)}) custom-call(bf16[1280,4096]{1,0:T(8,128)(2,1)S(1)} %copy-done, bf16[1024,1280]{1,0:T(8,128)(2,1)S(1)} %get-tuple-element.35.refs_1_.turned, bf16[8,1024,128]{2,1,0:T(8,128)(2,1)S(1)} %collective-permute-done.1.arrived), custom_call_target="tpu_custom_call" | custom-call | tf_op jit(solution)/shard_map/pallas_call | solution.py:115
  22.7 1.6 %collective-permute-start.2 = (bf16[4,1024,128]{2,1,0:T(8,128)(2,1)S(1)}, bf16[4,1024,128]{2,1,0:T(8,128)(2,1)S(1)}, u32[]{:S(2)}, u32[]{:S(2)}) collective-permute-start(bf16[4,1024,128]{2,1,0:T(8,128)(2,1)S(1)} %get-tuple-element.37), channel_id=1, source_target_pairs={{0,8},{4,36},{8,0},{12,44},{16,24},{20,52},{24,16},{28,60},{32,40}... | collective-permute-start | bytes 3145736 | tf_op jit(solution)/shard_map/ppermute | solution.py:422
  24.2 2.1 %collective-permute-start.3 = (bf16[4,1024,128]{2,1,0:T(8,128)(2,1)S(1)}, bf16[4,1024,128]{2,1,0:T(8,128)(2,1)S(1)}, u32[]{:S(2)}, u32[]{:S(2)}) collective-permute-start(bf16[4,1024,128]{2,1,0:T(8,128)(2,1)S(1)} %get-tuple-element.38), channel_id=1, source_target_pairs={{0,24},{4,100},{8,16},{12,108},{16,8},{20,116},{24,0},{28,124},{32... | collective-permute-start | bytes 3145736 | tf_op jit(solution)/shard_map/ppermute | solution.py:422
  26.3 6.7 %slope_kept.1.kept = f32[2,96,1024]{2,1,0:T(8,128)S(1)} custom-call(bf16[1280,4096]{1,0:T(8,128)(2,1)S(1)} %copy-done, bf16[1280,1024]{1,0:T(8,128)(2,1)S(1)} %get-tuple-element.46.refs_1_, bf16[4096,1024]{1,0:T(8,128)(2,1)S(1)} %bitcast.5), custom_call_target="tpu_custom_call" | custom-call | tf_op jit(solution)/shard_map/slope_kept/pallas_call | solution.py:202
  33.1 0.0 collective-permute-done.9.got
  33.2 2.3 %collective-permute-start.10 = (bf16[96,1024]{1,0:T(8,128)(2,1)S(1)}, bf16[96,1024]{1,0:T(8,128)(2,1)S(1)}, u32[]{:S(2)}, u32[]{:S(2)}) collective-permute-start(bf16[96,1024]{1,0:T(8,128)(2,1)S(1)} %fusion.1), channel_id=1, source_target_pairs={{0,3},{1,2},{2,1},{3,0},{4,5},{5,4},{6,7},{7,6},{8,11},{9,10},{10,... | collective-permute-start | bytes 589832 | tf_op jit(solution)/shard_map/ppermute | solution.py:436
  35.4 4.7 %collective-permute-done.10.got_two = bf16[96,1024]{1,0:T(8,128)(2,1)S(1)} collective-permute-done((bf16[96,1024]{1,0:T(8,128)(2,1)S(1)}, bf16[96,1024]{1,0:T(8,128)(2,1)S(1)}, u32[]{:S(2)}, u32[]{:S(2)}) %collective-permute-start.10) | collective-permute-done | bytes 196640 | tf_op jit(solution)/shard_map/ppermute | solution.py:436
  40.1 0.0 copy-done.1
  40.1 0.6 small_sends.1
  40.7 0.1 collective-permute-start.11
  40.8 0.0 collective-permute-done.arrived
  40.8 0.0 collective-permute-done.2.near
  40.8 0.0 collective-permute-done.3.far
  40.8 3.2 %shard_map.78 = (bf16[2,1024,128]{2,1,0:T(8,128)(2,1)S(1)}, bf16[2,1024,128]{2,1,0:T(8,128)(2,1)S(1)}, f32[4,1024,128]{2,1,0:T(8,128)S(1)}) custom-call(bf16[1280,4096]{1,0:T(8,128)(2,1)S(1)} %copy-done, bf16[1024,1280]{1,0:T(8,128)(2,1)S(1)} %get-tuple-element.35.refs_1_.turned, bf16[8,1024,128]{2,1,0:T(8,128)(2,1)S(1)} %collective-permute-done.arrived, ...), custom_call_target="tpu_custom_call" | custom-call | tf_op jit(solution)/shard_map/pallas_call | solution.py:115
  44.0 2.3 %collective-permute-start.4 = (bf16[2,1024,128]{2,1,0:T(8,128)(2,1)S(1)}, bf16[2,1024,128]{2,1,0:T(8,128)(2,1)S(1)}, u32[]{:S(2)}, u32[]{:S(2)}) collective-permute-start(bf16[2,1024,128]{2,1,0:T(8,128)(2,1)S(1)} %get-tuple-element.40), channel_id=1, source_target_pairs={{0,24},{4,100},{8,16},{12,108},{16,8},{20,116},{24,0},{28,124},{32... | collective-permute-start | bytes 1572872 | tf_op jit(solution)/shard_map/ppermute | solution.py:422
  46.3 0.0 collective-permute-start.5
  46.3 0.0 collective-permute-done.11.arrived
  46.3 0.1 shard_map.80
  46.4 1.3 %collective-permute-start.12 = (bf16[4,19,8,128]{3,2,1,0:T(8,128)(2,1)S(1)}, bf16[4,19,8,128]{3,2,1,0:T(8,128)(2,1)S(1)}, u32[]{:S(2)}, u32[]{:S(2)}) collective-permute-start(bf16[4,19,8,128]{3,2,1,0:T(8,128)(2,1)S(1)} %get-tuple-element.51), channel_id=1, source_target_pairs={{0,32},{4,12},{8,40},{12,4},{16,48},{20,28},{24,56},{28,20},{32,0}... | collective-permute-start | bytes 466952 | tf_op jit(solution)/shard_map/ppermute | solution.py:426
  47.8 6.7 %collective-permute-done.4.got_a = bf16[2,1024,128]{2,1,0:T(8,128)(2,1)S(1)} collective-permute-done((bf16[2,1024,128]{2,1,0:T(8,128)(2,1)S(1)}, bf16[2,1024,128]{2,1,0:T(8,128)(2,1)S(1)}, u32[]{:S(2)}, u32[]{:S(2)}) %collective-permute-start.4) | collective-permute-done | bytes 524320 | tf_op jit(solution)/shard_map/ppermute | solution.py:422
  54.5 2.7 %collective-permute-done.5.got_b = bf16[2,1024,128]{2,1,0:T(8,128)(2,1)S(1)} collective-permute-done((bf16[2,1024,128]{2,1,0:T(8,128)(2,1)S(1)}, bf16[2,1024,128]{2,1,0:T(8,128)(2,1)S(1)}, u32[]{:S(2)}, u32[]{:S(2)}) %collective-permute-start.5) | collective-permute-done | bytes 524320 | tf_op jit(solution)/shard_map/ppermute | solution.py:422
  57.2 0.2 shard_map.79
  57.4 1.5 %collective-permute-start.6 = (bf16[1024,128]{1,0:T(8,128)(2,1)S(1)}, bf16[1024,128]{1,0:T(8,128)(2,1)S(1)}, u32[]{:S(2)}, u32[]{:S(2)}) collective-permute-start(bf16[1024,128]{1,0:T(8,128)(2,1)S(1)} %get-tuple-element.43), channel_id=1, source_target_pairs={{0,32},{4,12},{8,40},{12,4},{16,48},{20,28},{24,56},{28,20},{32,0}... | collective-permute-start | bytes 786440 | tf_op jit(solution)/shard_map/ppermute | solution.py:426
  58.8 2.1 %collective-permute-start.7 = (bf16[1024,128]{1,0:T(8,128)(2,1)S(1)}, bf16[1024,128]{1,0:T(8,128)(2,1)S(1)}, u32[]{:S(2)}, u32[]{:S(2)}) collective-permute-start(bf16[1024,128]{1,0:T(8,128)(2,1)S(1)} %get-tuple-element.44), channel_id=1, source_target_pairs={{0,64},{4,20},{8,72},{12,28},{16,80},{20,4},{24,88},{28,12},{32,96... | collective-permute-start | bytes 786440 | tf_op jit(solution)/shard_map/ppermute | solution.py:426
  60.9 1.4 %collective-permute-start.8 = (bf16[1024,128]{1,0:T(8,128)(2,1)S(1)}, bf16[1024,128]{1,0:T(8,128)(2,1)S(1)}, u32[]{:S(2)}, u32[]{:S(2)}) collective-permute-start(bf16[1024,128]{1,0:T(8,128)(2,1)S(1)} %get-tuple-element.45), channel_id=1, source_target_pairs={{0,96},{4,28},{8,104},{12,20},{16,112},{20,12},{24,120},{28,4},{32... | collective-permute-start | bytes 786440 | tf_op jit(solution)/shard_map/ppermute | solution.py:426
  62.4 1.6 %collective-permute-start.13 = (bf16[4,19,8,128]{3,2,1,0:T(8,128)(2,1)S(1)}, bf16[4,19,8,128]{3,2,1,0:T(8,128)(2,1)S(1)}, u32[]{:S(2)}, u32[]{:S(2)}) collective-permute-start(bf16[4,19,8,128]{3,2,1,0:T(8,128)(2,1)S(1)} %get-tuple-element.52), channel_id=1, source_target_pairs={{0,64},{4,20},{8,72},{12,28},{16,80},{20,4},{24,88},{28,12},{32,96... | collective-permute-start | bytes 466952 | tf_op jit(solution)/shard_map/ppermute | solution.py:426
  64.0 0.0 collective-permute-done.12.side_one
  64.0 1.0 collective-permute-start.14
  65.0 4.8 %collective-permute-done.13.side_two = bf16[4,19,8,128]{3,2,1,0:T(8,128)(2,1)S(1)} collective-permute-done((bf16[4,19,8,128]{3,2,1,0:T(8,128)(2,1)S(1)}, bf16[4,19,8,128]{3,2,1,0:T(8,128)(2,1)S(1)}, u32[]{:S(2)}, u32[]{:S(2)}) %collective-permute-start.13) | collective-permute-done | bytes 155680 | tf_op jit(solution)/shard_map/ppermute | solution.py:426
  69.9 4.4 %collective-permute-done.14.side_three = bf16[4,19,8,128]{3,2,1,0:T(8,128)(2,1)S(1)} collective-permute-done((bf16[4,19,8,128]{3,2,1,0:T(8,128)(2,1)S(1)}, bf16[4,19,8,128]{3,2,1,0:T(8,128)(2,1)S(1)}, u32[]{:S(2)}, u32[]{:S(2)}) %collective-permute-start.14) | collective-permute-done | bytes 155680 | tf_op jit(solution)/shard_map/ppermute | solution.py:426
  74.2 0.1 shard_map.81
  74.3 0.6 collective-permute-start.15
  74.9 2.5 %collective-permute-start.16 = (bf16[19,8,128]{2,1,0:T(8,128)(2,1)S(1)}, bf16[19,8,128]{2,1,0:T(8,128)(2,1)S(1)}, u32[]{:S(2)}, u32[]{:S(2)}) collective-permute-start(bf16[19,8,128]{2,1,0:T(8,128)(2,1)S(1)} %get-tuple-element.56), channel_id=1, source_target_pairs={{0,16},{4,68},{8,24},{12,76},{16,0},{20,84},{24,8},{28,92},{32,48}... | collective-permute-start | bytes 116744 | tf_op jit(solution)/shard_map/ppermute | solution.py:422
  77.4 0.9 collective-permute-done.15.s_one
  78.4 1.6 %collective-permute-start.17 = (bf16[19,8,128]{2,1,0:T(8,128)(2,1)S(1)}, bf16[19,8,128]{2,1,0:T(8,128)(2,1)S(1)}, u32[]{:S(2)}, u32[]{:S(2)}) collective-permute-start(bf16[19,8,128]{2,1,0:T(8,128)(2,1)S(1)} %get-tuple-element.57), channel_id=1, source_target_pairs={{0,24},{4,100},{8,16},{12,108},{16,8},{20,116},{24,0},{28,124},{32... | collective-permute-start | bytes 116744 | tf_op jit(solution)/shard_map/ppermute | solution.py:422
  80.0 0.5 collective-permute-done.16.s_two
  80.4 3.1 %collective-permute-done.17.s_three = bf16[19,8,128]{2,1,0:T(8,128)(2,1)S(1)} collective-permute-done((bf16[19,8,128]{2,1,0:T(8,128)(2,1)S(1)}, bf16[19,8,128]{2,1,0:T(8,128)(2,1)S(1)}, u32[]{:S(2)}, u32[]{:S(2)}) %collective-permute-start.17) | collective-permute-done | bytes 38944 | tf_op jit(solution)/shard_map/ppermute | solution.py:422
  83.6 0.0 collective-permute-done.6.one
  83.6 0.0 collective-permute-done.7.two
  83.6 0.0 collective-permute-done.8.three
  83.6 0.4 shard_map.82
  84.0 12.1 %all_to_all.5.arrived.refs_6_ = bf16[32,4,8,128]{3,2,1,0:T(8,128)(2,1)S(1)} all-to-all(bf16[32,4,8,128]{3,2,1,0:T(8,128)(2,1)S(1)} %get-tuple-element.59), channel_id=1, replica_groups=mesh['client_0'=4,'client_1'=4,'client_2'=2,'head'=4] {'client_0','clien..., dimensions={0} | all-to-all | bytes 524288 | tf_op jit(solution)/shard_map/all_to_all | solution.py:459
  96.2 2.3 %collective-permute-start.20 = (f32[1,128]{1,0:T(1,128)S(1)}, f32[1,128]{1,0:T(1,128)S(1)}, u32[]{:S(2)}, u32[]{:S(2)}) collective-permute-start(f32[1,128]{1,0:T(1,128)S(1)} %shard_map.83.refs_0_), channel_id=1, source_target_pairs={{0,3},{1,2},{2,1},{3,0},{4,7},{5,6},{6,5},{7,4},{8,11},{9,10},{10,... | collective-permute-start | bytes 1544 | tf_op jit(solution)/shard_map/ppermute | solution.py:448
  98.4 0.3 collective-permute-start.19
  98.7 1.6 %collective-permute-start.18 = (f32[1,128]{1,0:T(1,128)S(1)}, f32[1,128]{1,0:T(1,128)S(1)}, u32[]{:S(2)}, u32[]{:S(2)}) collective-permute-start(f32[1,128]{1,0:T(1,128)S(1)} %shard_map.83.refs_0_), channel_id=1, source_target_pairs={{0,1},{1,0},{2,3},{3,2},{4,5},{5,4},{6,7},{7,6},{8,9},{9,8},{10,11... | collective-permute-start | bytes 1544 | tf_op jit(solution)/shard_map/ppermute | solution.py:448
  100.3 0.2 shard_map.84.refs_4_
  100.5 0.5 collective-permute-done.20.refs_3_
  101.0 2.5 %collective-permute-done.19.refs_2_ = f32[1,128]{1,0:T(1,128)S(1)} collective-permute-done((f32[1,128]{1,0:T(1,128)S(1)}, f32[1,128]{1,0:T(1,128)S(1)}, u32[]{:S(2)}, u32[]{:S(2)}) %collective-permute-start.19) | collective-permute-done | bytes 544 | tf_op jit(solution)/shard_map/ppermute | solution.py:448
  103.5 0.0 collective-permute-done.18.refs_1_
  103.5 1.0 shard_map.85
  (4 shorter events, 0.1 us)
Async XLA Ops:
  0.6 6.8 %copy-start = (bf16[1280,4096]{1,0:T(8,128)(2,1)S(1)}, bf16[1280,4096]{1,0:T(8,128)(2,1)}, u32[]{:S(2)}) copy-start(bf16[1280,4096]{1,0:T(8,128)(2,1)} %refs_0_.5) | copy-start | bytes 31457284
  4.3 6.7 %slice-start = ((s8[8388608]{0:T(1024)(128)(4,1)}), s8[4194304]{0:T(1024)(128)(4,1)S(1)}, s32[]{:S(2)}) async-start(s8[8388608]{0:T(1024)(128)(4,1)} %bitcast.4), calls=%async_computation.1 | async-start | bytes 8388608
  7.3 3.7 %slice-start.1 = ((s8[8388608]{0:T(1024)(128)(4,1)}), s8[4194304]{0:T(1024)(128)(4,1)S(1)}, s32[]{:S(2)}) async-start(s8[8388608]{0:T(1024)(128)(4,1)} %bitcast.4), calls=%async_computation.2 | async-start | bytes 8388608
  7.3 12.3 %collective-permute-start.1 = (bf16[8,1024,128]{2,1,0:T(8,128)(2,1)S(1)}, bf16[8,1024,128]{2,1,0:T(8,128)(2,1)S(1)}, u32[]{:S(2)}, u32[]{:S(2)}) collective-permute-start(bf16[8,1024,128]{2,1,0:T(8,128)(2,1)S(1)} %shard_map.76), channel_id=1, source_target_pairs={{0,4},{4,0},{1,5},{5,1},{2,6},{6,2},{3,7},{7,3},{8,12},{12,8},{9,1... | collective-permute-start | bytes 6291464 | tf_op jit(solution)/shard_map/ppermute | solution.py:430
  10.4 30.4 %collective-permute-start = (bf16[8,1024,128]{2,1,0:T(8,128)(2,1)S(1)}, bf16[8,1024,128]{2,1,0:T(8,128)(2,1)S(1)}, u32[]{:S(2)}, u32[]{:S(2)}) collective-permute-start(bf16[8,1024,128]{2,1,0:T(8,128)(2,1)S(1)} %shard_map.75), channel_id=1, source_target_pairs={{0,4},{4,0},{1,5},{5,1},{2,6},{6,2},{3,7},{7,3},{8,12},{12,8},{9,1... | collective-permute-start | bytes 6291464 | tf_op jit(solution)/shard_map/ppermute | solution.py:430
  17.7 15.4 %collective-permute-start.9 = (bf16[2,96,1024]{2,1,0:T(8,128)(2,1)S(1)}, bf16[2,96,1024]{2,1,0:T(8,128)(2,1)S(1)}, u32[]{:S(2)}, u32[]{:S(2)}) collective-permute-start(bf16[2,96,1024]{2,1,0:T(8,128)(2,1)S(1)} %slope_sent.1), channel_id=1, source_target_pairs={{0,1},{1,0},{2,3},{3,2},{4,7},{5,6},{6,5},{7,4},{8,9},{9,8},{10,11... | collective-permute-start | bytes 1179656 | tf_op jit(solution)/shard_map/ppermute | solution.py:436
  22.7 18.2 %collective-permute-start.2 = (bf16[4,1024,128]{2,1,0:T(8,128)(2,1)S(1)}, bf16[4,1024,128]{2,1,0:T(8,128)(2,1)S(1)}, u32[]{:S(2)}, u32[]{:S(2)}) collective-permute-start(bf16[4,1024,128]{2,1,0:T(8,128)(2,1)S(1)} %get-tuple-element.37), channel_id=1, source_target_pairs={{0,8},{4,36},{8,0},{12,44},{16,24},{20,52},{24,16},{28,60},{32,40}... | collective-permute-start | bytes 3145736 | tf_op jit(solution)/shard_map/ppermute | solution.py:422
  24.2 15.9 %copy-start.1 = (s32[16]{0:T(128)S(1)}, s32[16]{0:T(128)}, u32[]{:S(2)}) copy-start(s32[16]{0:T(128)} %param.7) | copy-start | bytes 196
  24.2 16.6 %collective-permute-start.3 = (bf16[4,1024,128]{2,1,0:T(8,128)(2,1)S(1)}, bf16[4,1024,128]{2,1,0:T(8,128)(2,1)S(1)}, u32[]{:S(2)}, u32[]{:S(2)}) collective-permute-start(bf16[4,1024,128]{2,1,0:T(8,128)(2,1)S(1)} %get-tuple-element.38), channel_id=1, source_target_pairs={{0,24},{4,100},{8,16},{12,108},{16,8},{20,116},{24,0},{28,124},{32... | collective-permute-start | bytes 3145736 | tf_op jit(solution)/shard_map/ppermute | solution.py:422
  33.2 7.0 %collective-permute-start.10 = (bf16[96,1024]{1,0:T(8,128)(2,1)S(1)}, bf16[96,1024]{1,0:T(8,128)(2,1)S(1)}, u32[]{:S(2)}, u32[]{:S(2)}) collective-permute-start(bf16[96,1024]{1,0:T(8,128)(2,1)S(1)} %fusion.1), channel_id=1, source_target_pairs={{0,3},{1,2},{2,1},{3,0},{4,5},{5,4},{6,7},{7,6},{8,11},{9,10},{10,... | collective-permute-start | bytes 589832 | tf_op jit(solution)/shard_map/ppermute | solution.py:436
  40.7 5.6 %collective-permute-start.11 = (bf16[16,19,8,128]{3,2,1,0:T(8,128)(2,1)S(1)}, bf16[16,19,8,128]{3,2,1,0:T(8,128)(2,1)S(1)}, u32[]{:S(2)}, u32[]{:S(2)}) collective-permute-start(bf16[16,19,8,128]{3,2,1,0:T(8,128)(2,1)S(1)} %get-tuple-element.49), channel_id=1, source_target_pairs={{0,4},{4,0},{1,5},{5,1},{2,6},{6,2},{3,7},{7,3},{8,12},{12,8},{9,1... | collective-permute-start | bytes 1867784 | tf_op jit(solution)/shard_map/ppermute | solution.py:430
  44.0 10.5 %collective-permute-start.4 = (bf16[2,1024,128]{2,1,0:T(8,128)(2,1)S(1)}, bf16[2,1024,128]{2,1,0:T(8,128)(2,1)S(1)}, u32[]{:S(2)}, u32[]{:S(2)}) collective-permute-start(bf16[2,1024,128]{2,1,0:T(8,128)(2,1)S(1)} %get-tuple-element.40), channel_id=1, source_target_pairs={{0,24},{4,100},{8,16},{12,108},{16,8},{20,116},{24,0},{28,124},{32... | collective-permute-start | bytes 1572872 | tf_op jit(solution)/shard_map/ppermute | solution.py:422
  46.3 10.8 %collective-permute-start.5 = (bf16[2,1024,128]{2,1,0:T(8,128)(2,1)S(1)}, bf16[2,1024,128]{2,1,0:T(8,128)(2,1)S(1)}, u32[]{:S(2)}, u32[]{:S(2)}) collective-permute-start(bf16[2,1024,128]{2,1,0:T(8,128)(2,1)S(1)} %get-tuple-element.41), channel_id=1, source_target_pairs={{0,8},{4,36},{8,0},{12,44},{16,24},{20,52},{24,16},{28,60},{32,40}... | collective-permute-start | bytes 1572872 | tf_op jit(solution)/shard_map/ppermute | solution.py:422
  46.4 17.5 %collective-permute-start.12 = (bf16[4,19,8,128]{3,2,1,0:T(8,128)(2,1)S(1)}, bf16[4,19,8,128]{3,2,1,0:T(8,128)(2,1)S(1)}, u32[]{:S(2)}, u32[]{:S(2)}) collective-permute-start(bf16[4,19,8,128]{3,2,1,0:T(8,128)(2,1)S(1)} %get-tuple-element.51), channel_id=1, source_target_pairs={{0,32},{4,12},{8,40},{12,4},{16,48},{20,28},{24,56},{28,20},{32,0}... | collective-permute-start | bytes 466952 | tf_op jit(solution)/shard_map/ppermute | solution.py:426
  57.4 26.2 %collective-permute-start.6 = (bf16[1024,128]{1,0:T(8,128)(2,1)S(1)}, bf16[1024,128]{1,0:T(8,128)(2,1)S(1)}, u32[]{:S(2)}, u32[]{:S(2)}) collective-permute-start(bf16[1024,128]{1,0:T(8,128)(2,1)S(1)} %get-tuple-element.43), channel_id=1, source_target_pairs={{0,32},{4,12},{8,40},{12,4},{16,48},{20,28},{24,56},{28,20},{32,0}... | collective-permute-start | bytes 786440 | tf_op jit(solution)/shard_map/ppermute | solution.py:426
  58.8 24.7 %collective-permute-start.7 = (bf16[1024,128]{1,0:T(8,128)(2,1)S(1)}, bf16[1024,128]{1,0:T(8,128)(2,1)S(1)}, u32[]{:S(2)}, u32[]{:S(2)}) collective-permute-start(bf16[1024,128]{1,0:T(8,128)(2,1)S(1)} %get-tuple-element.44), channel_id=1, source_target_pairs={{0,64},{4,20},{8,72},{12,28},{16,80},{20,4},{24,88},{28,12},{32,96... | collective-permute-start | bytes 786440 | tf_op jit(solution)/shard_map/ppermute | solution.py:426
  60.9 22.6 %collective-permute-start.8 = (bf16[1024,128]{1,0:T(8,128)(2,1)S(1)}, bf16[1024,128]{1,0:T(8,128)(2,1)S(1)}, u32[]{:S(2)}, u32[]{:S(2)}) collective-permute-start(bf16[1024,128]{1,0:T(8,128)(2,1)S(1)} %get-tuple-element.45), channel_id=1, source_target_pairs={{0,96},{4,28},{8,104},{12,20},{16,112},{20,12},{24,120},{28,4},{32... | collective-permute-start | bytes 786440 | tf_op jit(solution)/shard_map/ppermute | solution.py:426
  62.4 7.5 %collective-permute-start.13 = (bf16[4,19,8,128]{3,2,1,0:T(8,128)(2,1)S(1)}, bf16[4,19,8,128]{3,2,1,0:T(8,128)(2,1)S(1)}, u32[]{:S(2)}, u32[]{:S(2)}) collective-permute-start(bf16[4,19,8,128]{3,2,1,0:T(8,128)(2,1)S(1)} %get-tuple-element.52), channel_id=1, source_target_pairs={{0,64},{4,20},{8,72},{12,28},{16,80},{20,4},{24,88},{28,12},{32,96... | collective-permute-start | bytes 466952 | tf_op jit(solution)/shard_map/ppermute | solution.py:426
  64.0 10.3 %collective-permute-start.14 = (bf16[4,19,8,128]{3,2,1,0:T(8,128)(2,1)S(1)}, bf16[4,19,8,128]{3,2,1,0:T(8,128)(2,1)S(1)}, u32[]{:S(2)}, u32[]{:S(2)}) collective-permute-start(bf16[4,19,8,128]{3,2,1,0:T(8,128)(2,1)S(1)} %get-tuple-element.53), channel_id=1, source_target_pairs={{0,96},{4,28},{8,104},{12,20},{16,112},{20,12},{24,120},{28,4},{32... | collective-permute-start | bytes 466952 | tf_op jit(solution)/shard_map/ppermute | solution.py:426
  74.3 4.1 %collective-permute-start.15 = (bf16[19,8,128]{2,1,0:T(8,128)(2,1)S(1)}, bf16[19,8,128]{2,1,0:T(8,128)(2,1)S(1)}, u32[]{:S(2)}, u32[]{:S(2)}) collective-permute-start(bf16[19,8,128]{2,1,0:T(8,128)(2,1)S(1)} %get-tuple-element.55), channel_id=1, source_target_pairs={{0,8},{4,36},{8,0},{12,44},{16,24},{20,52},{24,16},{28,60},{32,40}... | collective-permute-start | bytes 116744 | tf_op jit(solution)/shard_map/ppermute | solution.py:422
  74.9 5.5 %collective-permute-start.16 = (bf16[19,8,128]{2,1,0:T(8,128)(2,1)S(1)}, bf16[19,8,128]{2,1,0:T(8,128)(2,1)S(1)}, u32[]{:S(2)}, u32[]{:S(2)}) collective-permute-start(bf16[19,8,128]{2,1,0:T(8,128)(2,1)S(1)} %get-tuple-element.56), channel_id=1, source_target_pairs={{0,16},{4,68},{8,24},{12,76},{16,0},{20,84},{24,8},{28,92},{32,48}... | collective-permute-start | bytes 116744 | tf_op jit(solution)/shard_map/ppermute | solution.py:422
  78.4 5.2 %collective-permute-start.17 = (bf16[19,8,128]{2,1,0:T(8,128)(2,1)S(1)}, bf16[19,8,128]{2,1,0:T(8,128)(2,1)S(1)}, u32[]{:S(2)}, u32[]{:S(2)}) collective-permute-start(bf16[19,8,128]{2,1,0:T(8,128)(2,1)S(1)} %get-tuple-element.57), channel_id=1, source_target_pairs={{0,24},{4,100},{8,16},{12,108},{16,8},{20,116},{24,0},{28,124},{32... | collective-permute-start | bytes 116744 | tf_op jit(solution)/shard_map/ppermute | solution.py:422
  96.2 4.9 %collective-permute-start.20 = (f32[1,128]{1,0:T(1,128)S(1)}, f32[1,128]{1,0:T(1,128)S(1)}, u32[]{:S(2)}, u32[]{:S(2)}) collective-permute-start(f32[1,128]{1,0:T(1,128)S(1)} %shard_map.83.refs_0_), channel_id=1, source_target_pairs={{0,3},{1,2},{2,1},{3,0},{4,7},{5,6},{6,5},{7,4},{8,11},{9,10},{10,... | collective-permute-start | bytes 1544 | tf_op jit(solution)/shard_map/ppermute | solution.py:448
  98.4 5.1 %collective-permute-start.19 = (f32[1,128]{1,0:T(1,128)S(1)}, f32[1,128]{1,0:T(1,128)S(1)}, u32[]{:S(2)}, u32[]{:S(2)}) collective-permute-start(f32[1,128]{1,0:T(1,128)S(1)} %shard_map.83.refs_0_), channel_id=1, source_target_pairs={{0,2},{1,3},{2,0},{3,1},{4,6},{5,7},{6,4},{7,5},{8,10},{9,11},{10,... | collective-permute-start | bytes 1544 | tf_op jit(solution)/shard_map/ppermute | solution.py:448
  98.7 4.8 %collective-permute-start.18 = (f32[1,128]{1,0:T(1,128)S(1)}, f32[1,128]{1,0:T(1,128)S(1)}, u32[]{:S(2)}, u32[]{:S(2)}) collective-permute-start(f32[1,128]{1,0:T(1,128)S(1)} %shard_map.83.refs_0_), channel_id=1, source_target_pairs={{0,1},{1,0},{2,3},{3,2},{4,5},{5,4},{6,7},{7,6},{8,9},{9,8},{10,11... | collective-permute-start | bytes 1544 | tf_op jit(solution)/shard_map/ppermute | solution.py:448
